TPU v7x, 32 devices: a whole 2x2x4 slice. The times are simulated.
32 devices in a mesh: row: 8 (over y, x, core), col: 4 (over z).
Axes of the slice: x: 2, y: 2, z: 4, core: 2. Of those that a mesh axis runs over, the one named last changes fastest.
Arguments:
- alignment_state: bfloat16 [128, 128, 256], P('col', 'row'), may hold values from -6 to 6
- layer_norm_gain: float32 [256], replicated, may hold values from 0.1 to 1.9
- left_weight_matrix: bfloat16 [256, 32], replicated, may hold values from -0.375 to 0.375
- right_weight_matrix: bfloat16 [256, 32], replicated, may hold values from -0.375 to 0.375
- output_weight_matrix: bfloat16 [1024, 128], replicated, may hold values from -0.1875 to 0.1875
- output_bias_vector: float32 [128], replicated, may hold values from -3 to 3
- pair_update_cotangent: bfloat16 [128, 128, 128], P('row', 'col'), may hold values from -40 to 40
Outputs:
- pair_update_output: bfloat16 [128, 128, 128], P('row', 'col')
- alignment_gradient: bfloat16 [128, 128, 256], P('col', 'row')
- left_weight_gradient: float32 [256, 32], replicated
- right_weight_gradient: float32 [256, 32], replicated
- out_w_grad: float32 [1024, 128], P(('row', 'col'))
- norm_gain_gradient: float32 [256], replicated
- output_bias_gradient: float32 [128], replicated
All inputs are finite; a program needn't handle non-finite values.
Results may differ from a plain program's by a relative error of at most 0.024.
Values may be sent and summed in bfloat16 or wider, within the bound.
No kernel may reach another device: no remote copies, remote signals or barrier semaphores. Data moves between devices by JAX's collectives and lax.ppermute only.
A program may use at most 64 MiB of HBM per device.

v0:
```python
import jax
import jax.numpy as jnp
from jax import lax
from jax.sharding import PartitionSpec as P


def from_root(block, axis, holder):
    block = jnp.where(lax.axis_index(axis) == holder, block, jnp.zeros_like(block))
    return lax.psum(block, axis)


def apply_layer_norm(alignment_state):
    value_entries = alignment_state.astype(jnp.float32)
    center = value_entries - jnp.mean(value_entries, axis=-1, keepdims=True)
    inverse_deviation = lax.rsqrt(jnp.mean(center * center, axis=-1, keepdims=True) + 1e-05)
    return (center * inverse_deviation, inverse_deviation)


def on_device(
    alignment_state,
    layer_norm_gain,
    left_weight_matrix,
    right_weight_matrix,
    output_weight_matrix,
    output_bias_vector,
    pair_update_cotangent,
):
    sequence_block_local, residue_block_local, alignment_weight = alignment_state.shape
    proj_w = left_weight_matrix.shape[1]
    pair_w = output_weight_matrix.shape[1]
    row_count = lax.axis_size("row")
    col_count = lax.axis_size("col")
    row_ratio = row_count // col_count
    total_res = residue_block_local * row_count
    col_res = residue_block_local * row_ratio
    col_index = lax.axis_index("col")
    row_index = lax.axis_index("row")
    normed_alignment, inverse_deviation = apply_layer_norm(alignment_state)
    layer_norm_output = (normed_alignment * layer_norm_gain).astype(jnp.bfloat16)
    normed_flat_rows = layer_norm_output.reshape(-1, alignment_weight)
    left_local = (
        jnp.dot(normed_flat_rows, left_weight_matrix, preferred_element_type=jnp.float32)
        .astype(jnp.bfloat16)
        .reshape(sequence_block_local, residue_block_local, proj_w)
    )
    right_local = (
        jnp.dot(normed_flat_rows, right_weight_matrix, preferred_element_type=jnp.float32)
        .astype(jnp.bfloat16)
        .reshape(sequence_block_local, residue_block_local, proj_w)
    )
    left_all, right_rows = (
        lax.all_gather(left_local, "col", axis=0, tiled=True),
        lax.all_gather(right_local, "col", axis=0, tiled=True),
    )
    seq_total = left_all.shape[0]
    right_every = lax.all_gather(right_rows, "row", axis=1, tiled=True)
    right_block = lax.dynamic_slice_in_dim(right_every, col_index * col_res, col_res, 1)
    block_res = min(8, residue_block_local)

    def visit(totals, row_start):
        right_acc, projection_running_sum = totals
        left_part = lax.dynamic_slice_in_dim(left_all, row_start, block_res, 1)
        cot_part = lax.dynamic_slice_in_dim(pair_update_cotangent, row_start, block_res, 0)
        outer_prod = jnp.einsum(
            "sic,sjd->ijcd", left_part, right_block, preferred_element_type=jnp.float32
        )
        outer_flat = (
            (outer_prod / seq_total)
            .astype(jnp.bfloat16)
            .reshape(block_res * col_res, proj_w * proj_w)
        )
        cot_flat = cot_part.reshape(block_res * col_res, pair_w)
        pair_part = (
            jnp.dot(outer_flat, output_weight_matrix, preferred_element_type=jnp.float32)
            + output_bias_vector
        ).astype(jnp.bfloat16)
        projection_running_sum = projection_running_sum + lax.dot_general(
            outer_flat, cot_flat, (((0,), (0,)), ((), ())), preferred_element_type=jnp.float32
        )
        outer_grad = lax.dot_general(
            cot_flat,
            output_weight_matrix,
            (((1,), (1,)), ((), ())),
            preferred_element_type=jnp.float32,
        ).astype(jnp.bfloat16)
        outer_grad = outer_grad.reshape(block_res, col_res, proj_w, proj_w)
        left_part_grad = (
            jnp.einsum("ijcd,sjd->sic", outer_grad, right_block, preferred_element_type=jnp.float32)
            / seq_total
        )
        right_acc = (
            right_acc
            + jnp.einsum("ijcd,sic->sjd", outer_grad, left_part, preferred_element_type=jnp.float32)
            / seq_total
        )
        return (
            (right_acc, projection_running_sum),
            (pair_part.reshape(block_res, col_res, pair_w), left_part_grad),
        )

    starts = jnp.arange(residue_block_local // block_res, dtype=jnp.int32) * block_res
    initial = (
        jnp.zeros((seq_total, col_res, proj_w), jnp.float32),
        jnp.zeros((proj_w * proj_w, pair_w), jnp.float32),
    )
    (right_acc, projection_running_sum), (pair_parts, left_parts) = lax.scan(visit, initial, starts)
    pair_update_output = pair_parts.reshape(residue_block_local, col_res, pair_w)
    left_partial = jnp.transpose(left_parts, (1, 0, 2, 3)).reshape(
        seq_total, residue_block_local, proj_w
    )
    left_d = lax.psum_scatter(
        left_partial.astype(jnp.bfloat16), "col", scatter_dimension=0, tiled=True
    )
    right_full = lax.psum(right_acc.astype(jnp.bfloat16), "row").astype(jnp.float32)
    right_half = lax.dynamic_slice_in_dim(
        right_full, row_index % row_ratio * residue_block_local, residue_block_local, 1
    )
    right_home = from_root(right_half.astype(jnp.bfloat16), "col", row_index // row_ratio).astype(
        right_half.dtype
    )
    right_d = lax.dynamic_slice_in_dim(
        right_home, col_index * sequence_block_local, sequence_block_local, 0
    ).astype(jnp.bfloat16)
    left_flat = left_d.reshape(-1, proj_w)
    right_flat = right_d.reshape(-1, proj_w)
    normed_derivative = lax.dot_general(
        left_flat, left_weight_matrix, (((1,), (1,)), ((), ())), preferred_element_type=jnp.float32
    )
    normed_derivative = normed_derivative + lax.dot_general(
        right_flat,
        right_weight_matrix,
        (((1,), (1,)), ((), ())),
        preferred_element_type=jnp.float32,
    )
    normed_derivative = normed_derivative.reshape(
        sequence_block_local, residue_block_local, alignment_weight
    )
    scaled_product = normed_derivative * layer_norm_gain
    alignment_gradient = (
        (
            scaled_product
            - jnp.mean(scaled_product, axis=-1, keepdims=True)
            - normed_alignment * jnp.mean(scaled_product * normed_alignment, axis=-1, keepdims=True)
        )
        * inverse_deviation
    ).astype(jnp.bfloat16)
    weight_left = lax.dot_general(
        normed_flat_rows, left_flat, (((0,), (0,)), ((), ())), preferred_element_type=jnp.float32
    )
    weight_right = lax.dot_general(
        normed_flat_rows, right_flat, (((0,), (0,)), ((), ())), preferred_element_type=jnp.float32
    )
    gain_part = jnp.sum(normed_derivative * normed_alignment, axis=(0, 1))
    bias_part = jnp.sum(pair_update_cotangent, axis=(0, 1), dtype=jnp.float32)
    param_totals = lax.psum((weight_left, weight_right, gain_part, bias_part), ("row", "col"))
    proj_partial = lax.psum_scatter(
        projection_running_sum.astype(jnp.bfloat16), "row", scatter_dimension=0, tiled=True
    ).astype(jnp.float32)
    proj_total = lax.psum_scatter(proj_partial, "col", scatter_dimension=0, tiled=True)
    return (
        pair_update_output,
        alignment_gradient,
        param_totals[0] / total_res,
        param_totals[1] / total_res,
        proj_total / total_res,
        param_totals[2] / total_res,
        param_totals[3] / total_res,
    )


def solution(mesh):
    return jax.shard_map(
        on_device,
        mesh=mesh,
        in_specs=(P("col", "row", None), P(), P(), P(), P(), P(), P("row", "col", None)),
        out_specs=(
            P("row", "col", None),
            P("col", "row", None),
            P(),
            P(),
            P(("row", "col"), None),
            P(),
            P(),
        ),
        check_vma=False,
    )
```

profile of v0, /device:TPU:24, one launch (start us, length us, event | category | flops | bytes accessed | tf_op | source)
XLA Modules:
  0.0 411.6 jit_solution(7871246451103388164)
XLA Ops:
  7.2 1.1 convert_reduce_fusion
  8.4 1.2 fusion.27
  9.6 1.2 fusion.21
  10.8 0.2 convolution_convert_fusion.1
  11.0 0.1 copy.42
  11.1 17.2 %all_gather.10 = bf16[128,16,32]{2,1,0:T(8,128)(2,1)} all-gather(bf16[32,16,32]{2,1,0:T(8,128)(2,1)S(1)} %bitcast.126), channel_id=1, replica_groups=mesh['row'=8,'col'=4] {'col'}, dimensions={0}, use_global_device_ids=true | all-gather | bytes 163840 | tf_op jit(solution)/shard_map/all_gather | solution.py:53
  28.4 0.2 convolution_convert_fusion.2
  28.6 0.1 copy.41
  28.7 15.1 %all_gather.9 = bf16[128,16,32]{2,1,0:T(8,128)(2,1)S(1)} all-gather(bf16[32,16,32]{2,1,0:T(8,128)(2,1)S(1)} %bitcast.127), channel_id=1, replica_groups=mesh['row'=8,'col'=4] {'col'}, dimensions={0}, use_global_device_ids=true | all-gather | bytes 163840 | tf_op jit(solution)/shard_map/all_gather | solution.py:52
  43.9 0.4 copy.43
  44.3 0.5 iota_multiply_fusion
  44.8 22.0 %all-gather.2.cloned.1.call-done = bf16[128,128,32]{2,1,0:T(8,128)(2,1)} async-done(((bf16[128,16,32]{2,1,0:T(8,128)(2,1)}), bf16[128,128,32]{2,1,0:T(8,128)(2,1)}) %all-gather.2.cloned.1.call-update) | async-done | bytes 1048592 | tf_op jit(solution)/shard_map/all_gather | solution.py:56
  66.8 1.3 constant_dynamic-slice_fusion.1
  68.1 1.8 copy.44
  69.9 32.7 %while.17 = (s32[]{:T(128)}, f32[128,32,32]{0,2,1:T(8,128)}, f32[1024,128]{1,0:T(8,128)S(1)}, bf16[2,8,32,128]{3,2,1,0:T(8,128)(2,1)}, bf16[2,128,8,32]{1,3,2,0:...) while((s32[]{:T(128)}, f32[128,32,32]{0,2,1:T(8,128)}, ...), condition=%wide.region_3.4_spmd.clone, body=%wide.region_2.3_spmd.clone.sunk | while | flops 404193280 | bytes 15928666 | solution.py:106
  69.9 1.2 dynamic_slice.46
  73.0 1.7 fusion.79
  74.7 2.2 reshape.95
  77.0 0.9 constant_dynamic-slice_fusion.3
  77.8 0.5 convolution_add_fusion.4
  78.3 0.8 copy-done.2
  79.1 0.3 convolution_convert_fusion.4
  79.4 1.6 reshape.94
  81.0 1.5 fusion.78
  82.5 0.3 fusion.80
  82.9 0.6 copy-done.17
  83.5 2.1 fusion.81
  85.7 1.2 dynamic_slice.46
  88.8 1.7 fusion.79
  90.5 2.2 reshape.95
  92.7 0.9 constant_dynamic-slice_fusion.3
  93.6 0.5 convolution_add_fusion.4
  94.1 0.8 copy-done.2
  94.9 0.3 convolution_convert_fusion.4
  95.2 1.6 reshape.94
  96.8 2.6 fusion.78
  99.4 0.3 fusion.80
  99.7 0.6 copy-done.17
  100.4 2.1 fusion.81
  102.5 1.8 convert_element_type.67
  104.4 2.1 copy.45
  106.6 0.6 convert_reduce_fusion.1
  107.2 51.2 %all-reduce.5.cloned.1.call-done = bf16[128,32,32]{0,2,1:T(8,128)(2,1)} async-done(((bf16[128,32,32]{0,2,1:T(8,128)(2,1)}), bf16[128,32,32]{0,2,1:T(8,128)(2,1)}) %all-reduce.5.cloned.1.call-update) | async-done | bytes 262160 | tf_op jit(solution)/shard_map/psum | solution.py:114
  158.4 1.6 fusion.28
  160.1 18.8 %reduce-scatter.4.cloned.1.call-done = bf16[32,16,32]{2,1,0:T(8,128)(2,1)} async-done(((bf16[128,16,32]{2,1,0:T(8,128)(2,1)}), bf16[32,16,32]{2,1,0:T(8,128)(2,1)}) %reduce-scatter.4.cloned.1.call-update) | async-done | bytes 32784 | tf_op jit(solution)/shard_map/reduce_scatter | solution.py:111
  178.9 1.1 fusion.29
  180.0 1.7 convolution_bitcast_fusion.3
  181.7 34.7 %all-reduce.7.cloned.1.call-done = bf16[128,16,32]{0,2,1:T(8,128)(2,1)} async-done(((bf16[128,16,32]{0,2,1:T(8,128)(2,1)}), bf16[128,16,32]{0,2,1:T(8,128)(2,1)}) %all-reduce.7.cloned.1.call-update) | async-done | bytes 131088 | tf_op jit(solution)/shard_map/psum | solution.py:9
  216.4 1.0 convert_convert_fusion
  217.5 0.2 copy.46
  217.6 0.8 convolution_bitcast_fusion.2
  218.4 0.3 multiply_reduce_fusion
  218.8 0.8 fusion.26
  219.6 0.7 convert_element_type.73
  220.5 0.1 div.63
  220.5 1.0 fusion.25
  221.6 125.5 %all-reduce.9.cloned.1.call-done = (f32[256,32]{0,1:T(8,128)}, f32[256,32]{0,1:T(8,128)}, f32[256]{0:T(256)}, f32[128]{0:T(128)}) async-done(((f32[256,32]{0,1:T(8,128)}, f32[256,32]{0,1:T(8,128)}, f32[256]{0:T(256)}, f32[128]{0:T(128)}), (f32[256,32]{0,1:T(8,128)}, f32[256,32]{0,1:T(8,128)}, f32[256]{0:T(256)}, f32[128]{0:T(128)})) %all-reduce.9.cloned.1.call-update) | async-done | bytes 67088 | tf_op jit(solution)/shard_map/psum | solution.py:155
  347.1 1.2 broadcast_multiply_fusion.6
  348.4 1.4 broadcast_multiply_fusion
  349.8 34.9 %reduce-scatter.6.cloned.1.call-done = bf16[128,128]{1,0:T(8,128)(2,1)} async-done(((bf16[1024,128]{1,0:T(8,128)(2,1)}), bf16[128,128]{1,0:T(8,128)(2,1)}) %reduce-scatter.6.cloned.1.call-update) | async-done | bytes 32784 | tf_op jit(solution)/shard_map/reduce_scatter | solution.py:156
  384.7 1.4 convert_element_type.74
  386.1 1.1 broadcast_multiply_fusion.7
  387.2 16.2 %reduce-scatter.8.cloned.1.call-done = f32[32,128]{1,0:T(8,128)} async-done(((f32[128,128]{1,0:T(8,128)}), f32[32,128]{1,0:T(8,128)}) %reduce-scatter.8.cloned.1.call-update) | async-done | bytes 16400 | tf_op jit(solution)/shard_map/reduce_scatter | solution.py:159
  403.4 1.3 broadcast_multiply_fusion.2
  (66 shorter events, 0.6 us)
Async XLA Ops:
  7.2 3.6 copy-start
  7.2 21.2 %copy-start.12 = (bf16[256,32]{0,1:T(8,128)(2,1)S(1)}, bf16[256,32]{0,1:T(8,128)(2,1)}, u32[]{:S(2)}) copy-start(bf16[256,32]{0,1:T(8,128)(2,1)} %param.11) | copy-start | bytes 49156
  7.2 59.6 %all-gather.2.cloned.1.call-start = ((), (), s32[]{:S(2)}) async-start(), calls=%async_computation.3 | async-start | bytes 4718592 | tf_op jit(solution)/shard_map/all_gather | solution.py:56
  8.3 2.4 copy-start.8
  9.6 1.2 copy-start.10
  10.8 18.0 %copy-start.5 = (bf16[32,16,256]{2,1,0:T(8,128)(2,1)}, bf16[32,16,256]{2,1,0:T(8,128)(2,1)S(1)}, u32[]{:S(2)}) copy-start(bf16[32,16,256]{2,1,0:T(8,128)(2,1)S(1)} %fusion.21) | copy-start | bytes 786436
  28.3 130.1 %all-reduce.5.cloned.1.call-start = ((), (), s32[]{:S(2)}) async-start(), calls=%async_computation.5 | async-start | bytes 524288 | tf_op jit(solution)/shard_map/psum | solution.py:114
  43.9 26.0 %copy-start.1 = (bf16[1024,128]{1,0:T(8,128)(2,1)S(1)}, bf16[1024,128]{1,0:T(8,128)(2,1)}, u32[]{:S(2)}) copy-start(bf16[1024,128]{1,0:T(8,128)(2,1)} %param.13) | copy-start | bytes 786436
  78.3 0.8 copy-start.2
  81.0 1.6 copy-start.15
  81.0 1.9 copy-start.16
  82.5 3.1 copy-start.3
  82.9 0.7 copy-start.17
  94.1 0.8 copy-start.2
  96.8 2.7 copy-start.15
  96.8 2.9 copy-start.16
  99.4 3.1 copy-start.3
  99.7 0.7 copy-start.17
  102.5 4.1 %copy-start.7 = (bf16[16,32,128]{2,1,0:T(8,128)(2,1)S(1)}, bf16[16,32,128]{2,1,0:T(8,128)(2,1)}, u32[]{:S(2)}) copy-start(bf16[16,32,128]{2,1,0:T(8,128)(2,1)} %get-tuple-element.299) | copy-start | bytes 393220
  102.5 76.4 %copy-start.13 = (bf16[256,32]{0,1:T(8,128)(2,1)S(1)}, bf16[256,32]{0,1:T(8,128)(2,1)}, u32[]{:S(2)}) copy-start(bf16[256,32]{0,1:T(8,128)(2,1)} %param.11) | copy-start | bytes 49156
  102.5 77.5 %copy-start.6 = (bf16[32,16,256]{2,1,0:T(8,128)(2,1)S(1)}, bf16[32,16,256]{2,1,0:T(8,128)(2,1)}, u32[]{:S(2)}) copy-start(bf16[32,16,256]{2,1,0:T(8,128)(2,1)} %copy-done.5) | copy-start | bytes 786436
  104.4 114.1 %copy-start.14 = (f32[256]{0:T(256)S(1)}, f32[256]{0:T(256)}, u32[]{:S(2)}) copy-start(f32[256]{0:T(256)} %param.10) | copy-start | bytes 3076
  104.4 74.5 %reduce-scatter.4.cloned.1.call-start = ((), (), s32[]{:S(2)}) async-start(), calls=%async_computation.4 | async-start | bytes 655360 | tf_op jit(solution)/shard_map/reduce_scatter | solution.py:111
  106.5 112.2 %copy-start.4 = (bf16[32,16,256]{2,1,0:T(8,128)(2,1)S(1)}, bf16[32,16,256]{2,1,0:T(8,128)(2,1)}, u32[]{:S(2)}) copy-start(bf16[32,16,256]{2,1,0:T(8,128)(2,1)} %param.9) | copy-start | bytes 786436
  106.5 112.2 %copy-start.9 = (f32[32,16]{1,0:T(8,128)S(1)}, f32[32,16]{1,0:T(8,128)}, u32[]{:S(2)}) copy-start(f32[32,16]{1,0:T(8,128)} %copy-done.8) | copy-start | bytes 6148
  106.5 112.2 %copy-start.11 = (f32[32,16]{1,0:T(8,128)S(1)}, f32[32,16]{1,0:T(8,128)}, u32[]{:S(2)}) copy-start(f32[32,16]{1,0:T(8,128)} %copy-done.10) | copy-start | bytes 6148
  106.6 109.9 %all-reduce.7.cloned.1.call-start = ((), (), s32[]{:S(2)}) async-start(), calls=%async_computation.6 | async-start | bytes 262144 | tf_op jit(solution)/shard_map/psum | solution.py:9
  160.0 187.1 %all-reduce.9.cloned.1.call-start = ((), (), s32[]{:S(2)}) async-start(), calls=%async_computation.9 | async-start | bytes 134144 | tf_op jit(solution)/shard_map/psum | solution.py:155
  219.6 165.1 %reduce-scatter.6.cloned.1.call-start = ((), (), s32[]{:S(2)}) async-start(), calls=%async_computation.7 | async-start | bytes 294912 | tf_op jit(solution)/shard_map/reduce_scatter | solution.py:156
  220.4 183.0 %reduce-scatter.8.cloned.1.call-start = ((), (), s32[]{:S(2)}) async-start(), calls=%async_computation.8 | async-start | bytes 81920 | tf_op jit(solution)/shard_map/reduce_scatter | solution.py:159
Sparse Core Ops, SparseCore 0:
  28.4 38.3 all-gather.1
  104.5 53.8 all-reduce.4
  160.7 18.1 reduce-scatter.3
  181.6 34.7 all-reduce.6
  223.0 124.1 all-reduce.8
  350.0 34.6 reduce-scatter.5
  386.9 16.4 reduce-scatter.7
where the time goes:
time: 417 us; the launch traced here: 412 us
  waiting for transfers between devices  303 us (73%)
  blocking collectives  32.3 us (8%)
  local copies, waits for them, and re-layouts  21 us (5%)
  matrix products  18.1 us (4%)
  other arithmetic  18 us (4%)
  between operations  14.4 us (3%)
    psum x1, waiting for transfers between devices, on_device(): lax.psum((weight_left, weight_right, gain_part, bias_part), ('row', 'col'))  126 us
    psum x1, waiting for transfers between devices, on_device(): lax.psum(right_acc.astype(jnp.bfloat16), 'row').astype(jnp.float32)  51.2 us
    reduce_scatter x1, waiting for transfers between devices, on_device(): lax.psum_scatter(projection_running_sum.astype(jnp.bfloat16), 'row', scat...  34.9 us
    psum x1, waiting for transfers between devices, from_root(): return lax.psum(block, axis)  34.7 us
    all_gather x1, waiting for transfers between devices, on_device(): right_every = lax.all_gather(right_rows, 'row', axis=1, tiled=True)  22 us
    reduce_scatter x1, waiting for transfers between devices, on_device(): lax.psum_scatter(left_partial.astype(jnp.bfloat16), 'col', scatter_dimens...  18.8 us
    all_gather x1, blocking collectives, on_device(): lax.all_gather(right_local, 'col', axis=0, tiled=True)  17.2 us
    reduce_scatter x1, waiting for transfers between devices, on_device(): lax.psum_scatter(proj_partial, 'col', scatter_dimension=0, tiled=True)  16.2 us
  transfers between devices with their start and end apart: 7, of which 7 were waited for; matrix products, arithmetic and copies ran while one was open for 3% of the time, Pallas kernels for 0%

commit v1 on v0

v1 whole, which is shorter than its diff:
```python
import functools

import jax
import jax.numpy as jnp
from jax import lax
from jax.experimental import pallas as pl
from jax.experimental.pallas import tpu as pltpu
from jax.sharding import PartitionSpec as P

F32, BF16 = jnp.float32, jnp.bfloat16
LANES = 128


def product(a, b, over=((1,), (0,))):
    return lax.dot_general(a, b, (over, ((), ())), preferred_element_type=F32)


def tree(terms):
    while len(terms) > 1:
        terms = [a + b for a, b in zip(terms[::2], terms[1::2])]
    return terms[0]


def wide(ref):
    return ref[...].astype(F32)


def call(name, body, args, outs, scratch=(), flops=1, limit=24):
    spec = pl.BlockSpec(memory_space=pltpu.VMEM)
    moved = sum(a.size * a.dtype.itemsize for a in args)
    return pl.pallas_call(
        body,
        out_shape=[jax.ShapeDtypeStruct(s, t) for s, t in outs],
        in_specs=[spec] * len(args),
        out_specs=[spec] * len(outs),
        scratch_shapes=list(scratch),
        name=name,
        cost_estimate=pl.CostEstimate(flops=flops, bytes_accessed=moved, transcendentals=0),
        compiler_params=pltpu.CompilerParams(vmem_limit_bytes=limit << 20),
    )(*args)


def normalize(rows):
    center = rows - jnp.mean(rows, axis=-1, keepdims=True)
    inverse = lax.rsqrt(jnp.mean(center * center, axis=-1, keepdims=True) + 1e-05)
    return center * inverse, inverse


def by_residue(x_ref, flat):
    seqs, residues, width = x_ref.shape
    values = wide(x_ref).reshape(seqs * residues, width)
    halves = range(width // LANES)
    for k in halves:
        flat[k] = values[:, k * LANES : (k + 1) * LANES]
    return [
        jnp.concatenate([flat[k, pl.ds(i, seqs, stride=residues), :] for k in halves], axis=1)
        for i in range(residues)
    ]


def channel_first(residues, chans):
    size = residues * chans
    source = lax.broadcasted_iota(jnp.int32, (size, size), 0)
    target = lax.broadcasted_iota(jnp.int32, (size, size), 1)
    place = (source % chans) * residues + source // chans
    return jnp.where(place == target, 1.0, 0.0).astype(BF16)


def project_kernel(chans, swap, x_ref, gain_ref, tiled_ref, out_ref, flat):
    seqs, residues, width = x_ref.shape
    rows = by_residue(x_ref, flat)
    normed, _ = normalize(jnp.concatenate(rows, axis=0))
    ln_out = (normed * gain_ref[...]).astype(F32)
    pack = LANES // chans
    lane = lax.broadcasted_iota(jnp.int32, (width, LANES), 1) // chans
    tiled = tiled_ref[...]
    weights = jnp.concatenate(
        [jnp.where(lane == k, tiled, jnp.zeros_like(tiled)) for k in range(pack)], axis=0
    )
    parts = []
    for g in range(residues // pack):
        piece = jnp.concatenate(
            [ln_out[(g * pack + k) * seqs : (g * pack + k + 1) * seqs] for k in range(pack)], axis=1
        )
        parts.append(product(piece.astype(BF16), weights))
    out = jnp.concatenate(parts, axis=1).astype(BF16)
    if swap:
        out = product(out, channel_first(residues, chans)).astype(BF16)
    out_ref[...] = out


def project(name, x, gain, tiled, chans, swap):
    seqs, residues, width = x.shape
    return call(
        name,
        functools.partial(project_kernel, chans, swap),
        (x, gain, tiled),
        [((seqs, residues * chans), BF16)],
        [pltpu.VMEM((width // LANES, seqs * residues, LANES), F32)],
        flops=40_000_000,
    )[0]


def spread_weight(w_ref, spread, chans):
    pack = LANES // chans
    pair_w = w_ref.shape[1]
    spread[...] = jnp.zeros_like(spread)
    for c in range(chans):
        block = w_ref[c * chans : (c + 1) * chans, :]
        for k in range(pack):
            row = c * LANES + k * chans
            spread[row : row + chans, k * pair_w : (k + 1) * pair_w] = block


def grad_kernel(chans, cot_ref, w_ref, og_ref, cotk_ref, bias_ref, flat, spread):
    residues, seconds, pair_w = cot_ref.shape
    pack = LANES // chans
    groups = seconds // pack
    cot = wide(cot_ref).reshape(residues * seconds, pair_w)
    flat[...] = cot
    bias_ref[...] = jnp.broadcast_to(jnp.sum(cot, axis=0, keepdims=True), bias_ref.shape)
    spread_weight(w_ref, spread, chans)
    for k in range(pack):
        rows = [flat[pl.ds(g * pack + k, residues, stride=seconds), :] for g in range(groups)]
        cotk_ref[k] = jnp.concatenate(rows, axis=0).astype(BF16)
    cot_wide = jnp.concatenate([cotk_ref[k] for k in range(pack)], axis=1)
    chunk = 8
    for first in range(0, chans, chunk):
        part = spread[first * LANES : (first + chunk) * LANES, :]
        out = product(cot_wide, part, ((1,), (1,))).astype(BF16)
        for c in range(chunk):
            for g in range(groups):
                row = (first + c) * residues
                og_ref[row : row + residues, g * LANES : (g + 1) * LANES] = out[
                    g * residues : (g + 1) * residues, c * LANES : (c + 1) * LANES
                ]


def places(ratio):
    row, col = lax.axis_index("row"), lax.axis_index("col")
    return row // ratio, row % ratio, col


def partial_kernel(cols, ratio, *refs):
    left_in, refs = refs[:cols], refs[cols:]
    right_in, refs = refs[: cols * ratio], refs[cols * ratio :]
    og_ref, refs = refs[0], refs[1:]
    left_out, refs = refs[:cols], refs[cols:]
    right_out, refs = refs[:ratio], refs[ratio:]
    left_all, right_all, left_sum, right_sum = refs
    seqs, width = left_in[0].shape
    total = seqs * cols
    q, h, z = places(ratio)
    for k in range(cols):
        left_all[pl.ds(pl.multiple_of((z ^ k) * seqs, seqs), seqs), :] = wide(left_in[k])
        for e in range(ratio):
            place = pl.ds(pl.multiple_of((q ^ k) * seqs, seqs), seqs)
            right_all[h ^ e, place, :] = wide(right_in[k * ratio + e])
    left = left_all[...].astype(BF16)
    sums = []
    for e in range(ratio):
        og = og_ref[:, e * width : (e + 1) * width]
        right_sum[e] = product(left, og) * (1.0 / total)
        sums.append(product(right_all[e].astype(BF16), og, ((1,), (1,))))
    left_sum[...] = sum(sums) * (1.0 / total)
    for k in range(cols):
        place = pl.ds(pl.multiple_of((z ^ k) * seqs, seqs), seqs)
        left_out[k][...] = left_sum[place, :].astype(BF16)
    for e in range(ratio):
        right_out[e][...] = right_sum[h ^ e].astype(BF16)


def forward_kernel(chans, ratio, *refs):
    left_ref, right_ref, cotk_ref, w_ref, bias_ref, pair_ref = refs[:6]
    proj_out, (flat, spread, facing, turned, proj) = refs[6 : 6 + ratio], refs[6 + ratio :]
    residues, seconds, pair_w = pair_ref.shape
    pack = LANES // chans
    groups = seconds // pack
    total = left_ref.shape[0]
    width = right_ref.shape[2]
    _, h, _ = places(ratio)
    spread_weight(w_ref, spread, chans)
    left = left_ref[...].astype(BF16)
    part = groups // ratio
    for e in range(ratio):
        outer = product(left, right_ref[e].astype(BF16), ((0,), (0,)))
        outer = (outer * (1.0 / total)).astype(BF16)
        for c in range(chans):
            for g in range(part):
                row = (e * part + g) * residues
                facing[row : row + residues, c * LANES : (c + 1) * LANES] = outer[
                    c * residues : (c + 1) * residues, g * LANES : (g + 1) * LANES
                ]
    pair = product(facing[...], spread[...])
    for g in range(groups):
        for k in range(pack):
            block = pair[g * residues : (g + 1) * residues, k * pair_w : (k + 1) * pair_w]
            flat[pl.ds(g * pack + k, residues, stride=seconds), :] = block + bias_ref[...]
    pair_ref[...] = flat[...].astype(BF16).reshape(residues, seconds, pair_w)
    size = groups * residues
    for c in range(chans):
        block = facing[:, c * LANES : (c + 1) * LANES].T
        for k in range(pack):
            turned[c * chans : (c + 1) * chans, k * size : (k + 1) * size] = block[
                k * chans : (k + 1) * chans
            ]
    cot = jnp.concatenate([cotk_ref[k] for k in range(pack)], axis=0)
    out = product(turned[...], cot)
    count, height = proj_out[0].shape[:2]
    proj[...] = out.reshape(count, ratio, height, pair_w)
    for e in range(ratio):
        for q in range(count):
            proj_out[e][q] = proj[q, h ^ e].astype(BF16)


def stacked(value, residues, chans):
    return jnp.concatenate(
        [value[:, i * chans : (i + 1) * chans] for i in range(residues)], axis=0
    )


def moment_kernel(cols, chans, *refs):
    left_in, right_in = refs[:cols], refs[cols : 2 * cols]
    x_ref, across_ref, bias_ref, left_ref, right_ref, stat_ref, flat = refs[2 * cols :]
    residues = x_ref.shape[1]
    width = x_ref.shape[2]
    left = tree([wide(r) for r in left_in]).astype(BF16)
    left = product(left, channel_first(residues, chans), ((1,), (1,)))
    right = tree([wide(r) for r in right_in])
    left_ref[...] = left.astype(BF16)
    right_ref[...] = right.astype(BF16)
    moments = []
    for value, rows_ref in ((left, x_ref), (right, across_ref)):
        normed, _ = normalize(jnp.concatenate(by_residue(rows_ref, flat), axis=0))
        value = stacked(value, residues, chans).astype(BF16)
        moments.append(product(value, normed.astype(BF16), ((0,), (0,))))
    moment = jnp.concatenate(moments, axis=0)
    halves = [moment[:, k * LANES : (k + 1) * LANES] for k in range(width // LANES)]
    bias = jnp.concatenate([bias_ref[...]] * 2, axis=0)
    stat_ref[...] = jnp.concatenate(halves + [bias], axis=0).astype(BF16)


def input_grad_kernel(chans, x_ref, gain_ref, lw_ref, rw_ref, left_ref, right_ref, out_ref, flat):
    seqs, residues, width = x_ref.shape
    normed, inverse = normalize(jnp.concatenate(by_residue(x_ref, flat), axis=0))
    left = stacked(wide(left_ref), residues, chans).astype(BF16)
    right = stacked(wide(right_ref), residues, chans).astype(BF16)
    ln_d = product(left, lw_ref[...], ((1,), (1,))) + product(right, rw_ref[...], ((1,), (1,)))
    scaled = ln_d * gain_ref[...]
    mean = jnp.mean(scaled, axis=-1, keepdims=True)
    tilt = jnp.mean(scaled * normed, axis=-1, keepdims=True)
    grad = (scaled - mean - normed * tilt) * inverse
    halves = range(width // LANES)
    for i in range(residues):
        for k in halves:
            piece = grad[i * seqs : (i + 1) * seqs, k * LANES : (k + 1) * LANES]
            flat[k, pl.ds(i, seqs, stride=residues), :] = piece
    values = jnp.concatenate([flat[k] for k in halves], axis=1)
    out_ref[...] = values.astype(BF16).reshape(seqs, residues, width)


def core_sum_kernel(ratio, *refs):
    right_in, refs = refs[:ratio], refs[ratio:]
    outs, flat = refs[:-1], refs[-1]
    seqs = outs[0].shape[0]
    q, _, _ = places(ratio)
    flat[...] = tree([wide(r) for r in right_in])
    for k, out in enumerate(outs):
        place = pl.ds(pl.multiple_of((q ^ k) * seqs, seqs), seqs)
        out[...] = flat[place, :].astype(BF16)


def first_stat_kernel(ratio, *refs):
    proj_in, stat_in = refs[:ratio], refs[ratio : 2 * ratio]
    outs, scratch = refs[2 * ratio : -1], refs[-1]
    height = scratch.shape[1]
    q, _, _ = places(ratio)
    scratch[...] = tree([wide(r) for r in proj_in])
    stat = tree([wide(r) for r in stat_in]).astype(BF16)
    for k, out in enumerate(outs):
        out[:height] = scratch[q ^ k].astype(BF16)
        out[height:] = stat


def second_stat_kernel(ratio, height, *refs):
    count = (len(refs) - 1) // 2
    ins, outs, scratch = refs[:count], refs[count : 2 * count], refs[-1]
    _, _, z = places(ratio)
    total = tree([wide(r) for r in ins])
    size = height * count
    scratch[...] = total[:size].reshape(scratch.shape)
    stat = total[size:].astype(BF16)
    for k, out in enumerate(outs):
        out[:height] = scratch[z ^ k].astype(BF16)
        out[height:] = stat


def last_stat_kernel(chans, height, scale, *refs):
    ins, (gain_ref, lw_ref, rw_ref) = refs[:-8], refs[-8:-5]
    left_ref, right_ref, proj_ref, norm_ref, bias_ref = refs[-5:]
    total = tree([wide(r) for r in ins]) * scale
    proj_ref[...] = total[:height]
    stat = total[height:]
    width = lw_ref.shape[0]
    size = 2 * chans
    halves = width // LANES
    moment = jnp.concatenate([stat[k * size : (k + 1) * size] for k in range(halves)], axis=1)
    moment = moment.T
    left, right = moment[:, :chans], moment[:, chans:]
    norm = left * wide(lw_ref) + right * wide(rw_ref)
    left_ref[...] = left * gain_ref[...]
    right_ref[...] = right * gain_ref[...]
    norm_ref[...] = jnp.sum(norm, axis=1, keepdims=True)
    bias_ref[...] = stat[halves * size : halves * size + 1]


def on_device(x, gain, left_w, right_w, out_w, bias, cot):
    seqs, residues, width = x.shape
    chans = left_w.shape[1]
    pair_w = out_w.shape[1]
    rows, cols = lax.axis_size("row"), lax.axis_size("col")
    ratio = rows // cols
    seconds = residues * ratio
    total_seqs, total_res = seqs * cols, residues * rows
    wide_proj, wide_pair = residues * chans, seconds * chans
    pack = LANES // chans
    groups = seconds // pack
    gain_row = gain.reshape(1, width)

    def col_swap(value, k):
        return lax.ppermute(value, "col", [(i, i ^ k) for i in range(cols)])

    def chip_swap(value, k):
        return lax.ppermute(value, "row", [(i, i ^ (k * ratio)) for i in range(rows)])

    def core_swap(value, e):
        return lax.ppermute(value, "row", [(i, i ^ e) for i in range(rows)])

    def across(value):
        pairs = [
            ((q * ratio + h) * cols + z, (z * ratio + h) * cols + q)
            for q in range(cols)
            for h in range(ratio)
            for z in range(cols)
        ]
        return lax.ppermute(value, ("row", "col"), pairs)

    x_across = across(x)
    left_own = project("left", x, gain_row, jnp.tile(left_w, (1, pack)), chans, True)
    left_in = [left_own] + [col_swap(left_own, k) for k in range(1, cols)]
    og, cotk, bias_part = call(
        "outer_grad",
        functools.partial(grad_kernel, chans),
        (cot, out_w),
        [
            ((chans * residues, wide_pair), BF16),
            ((pack, groups * residues, pair_w), BF16),
            ((8, pair_w), F32),
        ],
        [
            pltpu.VMEM((residues * seconds, pair_w), F32),
            pltpu.VMEM((chans * LANES, pack * pair_w), BF16),
        ],
        flops=540_000_000,
    )
    right_own = project("right", x_across, gain_row, jnp.tile(right_w, (1, pack)), chans, False)
    right_in = []
    for k in range(cols):
        chip = right_own if k == 0 else chip_swap(right_own, k)
        right_in += [chip] + [core_swap(chip, e) for e in range(1, ratio)]

    outs = call(
        "partials",
        functools.partial(partial_kernel, cols, ratio),
        (*left_in, *right_in, og),
        [((seqs, wide_proj), BF16)] * cols
        + [((total_seqs, wide_proj), BF16)] * ratio
        + [((total_seqs, wide_proj), F32), ((ratio, total_seqs, wide_proj), F32)],
        [
            pltpu.VMEM((total_seqs, wide_proj), F32),
            pltpu.VMEM((ratio, total_seqs, wide_proj), F32),
        ],
        flops=270_000_000,
    )
    left_parts, right_parts = outs[:cols], outs[cols : cols + ratio]
    left_all, right_all = outs[cols + ratio :]

    right_core = [right_parts[0]] + [core_swap(right_parts[e], e) for e in range(1, ratio)]
    left_parts = [left_parts[0]] + [col_swap(left_parts[k], k) for k in range(1, cols)]
    right_parts = call(
        "core_sum",
        functools.partial(core_sum_kernel, ratio),
        right_core,
        [((seqs, wide_proj), BF16)] * cols,
        [pltpu.VMEM((total_seqs, wide_proj), F32)],
    )
    right_parts = [right_parts[0]] + [chip_swap(right_parts[k], k) for k in range(1, cols)]

    block = chans * chans // rows
    outs = call(
        "forward",
        functools.partial(forward_kernel, chans, ratio),
        (left_all, right_all, cotk, out_w, bias.reshape(1, pair_w)),
        [((residues, seconds, pair_w), BF16)] + [((cols, block, pair_w), BF16)] * ratio,
        [
            pltpu.VMEM((residues * seconds, pair_w), F32),
            pltpu.VMEM((chans * LANES, pack * pair_w), BF16),
            pltpu.VMEM((groups * residues, chans * LANES), BF16),
            pltpu.VMEM((chans * chans, pack * groups * residues), BF16),
            pltpu.VMEM((cols, ratio, block, pair_w), F32),
        ],
        flops=800_000_000,
        limit=32,
    )
    pair_update, proj_parts = outs[0], outs[1:]
    proj_core = [proj_parts[0]] + [core_swap(proj_parts[e], e) for e in range(1, ratio)]

    stat_rows = 2 * chans * (width // LANES) + 16
    left_d, right_d, stat = call(
        "moments",
        functools.partial(moment_kernel, cols, chans),
        (*left_parts, *right_parts, x, x_across, bias_part),
        [((seqs, wide_proj), BF16), ((seqs, wide_proj), BF16), ((stat_rows, LANES), BF16)],
        [pltpu.VMEM((width // LANES, seqs * residues, LANES), F32)],
    )
    stat_core = [stat] + [core_swap(stat, e) for e in range(1, ratio)]
    right_home = across(right_d)
    firsts = call(
        "first_stat",
        functools.partial(first_stat_kernel, ratio),
        (*proj_core, *stat_core),
        [((block + stat_rows, pair_w), BF16)] * cols,
        [pltpu.VMEM((cols, block, pair_w), F32)],
    )
    firsts = [firsts[0]] + [chip_swap(firsts[k], k) for k in range(1, cols)]
    height = block // cols
    seconds_out = call(
        "second_stat",
        functools.partial(second_stat_kernel, ratio, height),
        firsts,
        [((height + stat_rows, pair_w), BF16)] * cols,
        [pltpu.VMEM((cols, height, pair_w), F32)],
    )
    seconds_out = [seconds_out[0]] + [col_swap(seconds_out[k], k) for k in range(1, cols)]
    grad = call(
        "input_grad",
        functools.partial(input_grad_kernel, chans),
        (x, gain_row, left_w, right_w, left_d, right_home),
        [((seqs, residues, width), BF16)],
        [pltpu.VMEM((width // LANES, seqs * residues, LANES), F32)],
    )[0]
    left_g, right_g, proj_g, norm_g, bias_g = call(
        "last_stat",
        functools.partial(last_stat_kernel, chans, height, 1.0 / total_res),
        (*seconds_out, gain.reshape(width, 1), left_w, right_w),
        [
            ((width, chans), F32),
            ((width, chans), F32),
            ((height, pair_w), F32),
            ((width, 1), F32),
            ((1, pair_w), F32),
        ],
    )
    return (
        pair_update,
        grad,
        left_g,
        right_g,
        proj_g,
        norm_g.reshape(width),
        bias_g.reshape(pair_w),
    )


def solution(mesh):
    return jax.shard_map(
        on_device,
        mesh=mesh,
        in_specs=(P("col", "row", None), P(), P(), P(), P(), P(), P("row", "col", None)),
        out_specs=(
            P("row", "col", None),
            P("col", "row", None),
            P(),
            P(),
            P(("row", "col"), None),
            P(),
            P(),
        ),
        check_vma=False,
    )
```

time: 417 us -> 77.7 us (0.19); the launches traced: 412 us -> 77.4 us
  waiting for transfers between devices: 303 us -> 24.7 us
  starting transfers between devices: 0.29 us -> 36.7 us
  blocking collectives: 32.3 us -> 0 us
  matrix products: 18.1 us -> 0 us
  other arithmetic: 18 us -> 0.68 us
  local copies, waits for them, and re-layouts: 21 us -> 5.01 us
  between operations: 14.4 us -> 0.85 us
  Pallas kernels: 0 us -> 9.55 us
    psum x3 -> x0, waiting for transfers between devices: 211 us -> none  [the longest x1 126 us: on_device(): lax.psum((weight_left, weight_right, gain_part, bias_part), ('row', 'col'))]
    reduce_scatter x3 -> x0, waiting for transfers between devices: 69.9 us -> none  [the longest x1 34.9 us: on_device(): lax.psum_scatter(projection_running_sum.astype(jnp.bfloat16), 'row', scat...]
    ppermute x0 -> x27, starting transfers between devices: none -> 36.7 us  [the longest x9 19 us: chip_swap(): return lax.ppermute(value, 'row', [(i, i ^ k * ratio) for i in range(rows)])]
    all_gather x2 -> x0, blocking collectives: 32.3 us -> none  [the longest x1 17.2 us: on_device(): lax.all_gather(right_local, 'col', axis=0, tiled=True)]
    ppermute x0 -> x27, waiting for transfers between devices: none -> 24.7 us  [the longest x2 12.8 us: across(): return lax.ppermute(value, ('row', 'col'), pairs)]
    all_gather x1 -> x0, waiting for transfers between devices: 22 us -> none  [on_device(): right_every = lax.all_gather(right_rows, 'row', axis=1, tiled=True)]
    dot_general x18 -> x0, matrix products: 18.1 us -> none  [the longest x2 4.25 us: visit(): jnp.einsum('ijcd,sjd->sic', outer_grad, right_block, preferred_element_ty...]
    pallas_call x0 -> x11, Pallas kernels: none -> 9.55 us  [call(): pl.pallas_call(body, out_shape=[jax.ShapeDtypeStruct(s, t) for s, t in ou...]
  transfers between devices with their start and end apart: 7 -> 27, of which waited for: 7 -> 11; matrix products, arithmetic and copies ran while one was open for 3% -> 2% of each run, Pallas kernels for 0% -> 10%
where the time goes in v1:
time: 77.7 us; the launch traced here: 77.4 us
  starting transfers between devices  36.7 us (47%)
  waiting for transfers between devices  24.7 us (32%)
  Pallas kernels  9.55 us (12%)
  local copies, waits for them, and re-layouts  5.01 us (6%)
  between operations  0.85 us (1%)
    ppermute x9, starting transfers between devices, chip_swap(): return lax.ppermute(value, 'row', [(i, i ^ k * ratio) for i in range(rows)])  19 us
    ppermute x2, waiting for transfers between devices, across(): return lax.ppermute(value, ('row', 'col'), pairs)  12.8 us
    ppermute x9, waiting for transfers between devices, chip_swap(): return lax.ppermute(value, 'row', [(i, i ^ k * ratio) for i in range(rows)])  10.6 us
    pallas_call x11, Pallas kernels, call(): pl.pallas_call(body, out_shape=[jax.ShapeDtypeStruct(s, t) for s, t in ou...  9.55 us
    ppermute x9, starting transfers between devices, col_swap(): return lax.ppermute(value, 'col', [(i, i ^ k) for i in range(cols)])  9.14 us
    ppermute x2, starting transfers between devices, across(): return lax.ppermute(value, ('row', 'col'), pairs)  7.35 us
    unnamed x20, local copies, waits for them, and re-layouts  3.92 us
  transfers between devices with their start and end apart: 27, of which 11 were waited for; matrix products, arithmetic and copies ran while one was open for 2% of the time, Pallas kernels for 10%

profile of v1, /device:TPU:24, one launch (start us, length us, event | category | flops | bytes accessed | tf_op | source)
XLA Modules:
  0.0 77.4 jit_solution(2127484071530523992)
XLA Ops:
  0.6 4.0 %collective-permute-start.3 = (bf16[32,16,256]{2,1,0:T(8,128)(2,1)}, bf16[32,16,256]{2,1,0:T(8,128)(2,1)S(1)}, u32[]{:S(2)}, u32[]{:S(2)}) collective-permute-start(bf16[32,16,256]{2,1,0:T(8,128)(2,1)} %x_ref.3), channel_id=1, source_target_pairs={{0,0},{1,8},{2,16},{3,24},{4,4},{5,12},{6,20},{7,28},{8,1},{9,9},{... | collective-permute-start | bytes 786440 | tf_op jit(solution)/shard_map/ppermute | solution.py:346
  4.7 0.7 tile.8
  5.4 0.1 copy.22.tiled_ref
  5.5 0.0 copy-start.2
  5.5 0.7 copy-done.2
  6.2 0.9 %copy-done = bf16[32,16,256]{2,1,0:T(8,128)(2,1)S(1)} copy-done((bf16[32,16,256]{2,1,0:T(8,128)(2,1)S(1)}, bf16[32,16,256]{2,1,0:T(8,128)(2,1)}, u32[]{:S(2)}) %copy-start) | copy-done | bytes 262168
  7.1 0.7 left.1.refs_0_
  7.8 0.1 collective-permute-start.1
  7.9 0.0 copy-start.3
  7.9 0.1 copy.23.tiled_ref
  8.0 0.0 copy-start.4
  8.1 7.1 %collective-permute-done.3.x_ref.refs_9_ = bf16[32,16,256]{2,1,0:T(8,128)(2,1)S(1)} collective-permute-done((bf16[32,16,256]{2,1,0:T(8,128)(2,1)}, bf16[32,16,256]{2,1,0:T(8,128)(2,1)S(1)}, u32[]{:S(2)}, u32[]{:S(2)}) %collective-permute-start.3) | collective-permute-done | bytes 262176 | tf_op jit(solution)/shard_map/ppermute | solution.py:346
  15.2 0.5 right.1.refs_4_
  15.7 0.1 collective-permute-start.9
  15.8 11.8 %collective-permute-start.5 = (bf16[32,512]{1,0:T(8,128)(2,1)S(1)}, bf16[32,512]{1,0:T(8,128)(2,1)S(1)}, u32[]{:S(2)}, u32[]{:S(2)}) collective-permute-start(bf16[32,512]{1,0:T(8,128)(2,1)S(1)} %right.1.refs_4_), channel_id=1, source_target_pairs={{0,8},{4,12},{8,0},{12,4},{16,24},{20,28},{24,16},{28,20},{1,9},{5... | collective-permute-start | bytes 98312 | tf_op jit(solution)/shard_map/ppermute | solution.py:334
  27.6 0.0 collective-permute-start.7
  27.6 0.0 collective-permute-done.refs_1_
  27.6 0.2 collective-permute-start.2
  27.8 0.0 collective-permute-done.1.refs_2_
  27.8 0.0 collective-permute-start.4
  27.8 0.0 collective-permute-done.9.refs_10_
  27.8 0.5 collective-permute-start.10
  28.3 1.5 %collective-permute-done.5.refs_6_ = bf16[32,512]{1,0:T(8,128)(2,1)S(1)} collective-permute-done((bf16[32,512]{1,0:T(8,128)(2,1)S(1)}, bf16[32,512]{1,0:T(8,128)(2,1)S(1)}, u32[]{:S(2)}, u32[]{:S(2)}) %collective-permute-start.5) | collective-permute-done | bytes 32800 | tf_op jit(solution)/shard_map/ppermute | solution.py:334
  29.8 0.0 collective-permute-start.6
  29.8 1.7 %collective-permute-done.7.refs_8_ = bf16[32,512]{1,0:T(8,128)(2,1)S(1)} collective-permute-done((bf16[32,512]{1,0:T(8,128)(2,1)S(1)}, bf16[32,512]{1,0:T(8,128)(2,1)S(1)}, u32[]{:S(2)}, u32[]{:S(2)}) %collective-permute-start.7) | collective-permute-done | bytes 32800 | tf_op jit(solution)/shard_map/ppermute | solution.py:334
  31.5 1.7 %outer_grad.1 = (bf16[512,1024]{1,0:T(8,128)(2,1)S(1)}, bf16[4,128,128]{2,1,0:T(8,128)(2,1)S(1)}, f32[8,128]{1,0:T(8,128)S(1)}) custom-call(bf16[16,32,128]{2,1,0:T(8,128)(2,1)S(1)} %copy-done.4, bf16[1024,128]{1,0:T(8,128)(2,1)S(1)} %copy-done.3), custom_call_target="tpu_custom_call" | custom-call | flops 540000000 | bytes 393216 | tf_op jit(solution)/shard_map/outer_grad/pallas_call | solution.py:31
  33.2 0.1 collective-permute-done.2.refs_3_
  33.3 0.7 partials.1
  34.0 0.5 collective-permute-start.14
  34.5 0.7 copy-done.5
  35.2 2.1 %forward.1 = (bf16[16,32,128]{2,1,0:T(8,128)(2,1)}, bf16[4,128,128]{2,1,0:T(8,128)(2,1)S(1)}, bf16[4,128,128]{2,1,0:T(8,128)(2,1)S(1)}) custom-call(f32[128,512]{1,0:T(8,128)S(1)} %get-tuple-element.42.refs_0_, f32[2,128,512]{2,1,0:T(8,128)S(1)} %get-tuple-element.43.refs_1_, bf16[4,128,128]{2,1,0:T(8,128)(2,1)S(1)} %get-tuple-element.44.refs_2_, ...), custom_call_target="tpu_custom_call" | custom-call | flops 800000000 | bytes 1180160 | tf_op jit(solution)/shard_map/forward/pallas_call | solution.py:31
  37.3 0.1 collective-permute-start.19
  37.3 1.4 %collective-permute-start.12 = (bf16[32,512]{1,0:T(8,128)(2,1)S(1)}, bf16[32,512]{1,0:T(8,128)(2,1)S(1)}, u32[]{:S(2)}, u32[]{:S(2)}) collective-permute-start(bf16[32,512]{1,0:T(8,128)(2,1)S(1)} %get-tuple-element.48), channel_id=1, source_target_pairs={{0,2},{1,3},{2,0},{3,1},{4,6},{5,7},{6,4},{7,5},{8,10},{9,11},{10,... | collective-permute-start | bytes 98312 | tf_op jit(solution)/shard_map/ppermute | solution.py:331
  38.8 3.0 %collective-permute-start.13 = (bf16[32,512]{1,0:T(8,128)(2,1)S(1)}, bf16[32,512]{1,0:T(8,128)(2,1)S(1)}, u32[]{:S(2)}, u32[]{:S(2)}) collective-permute-start(bf16[32,512]{1,0:T(8,128)(2,1)S(1)} %get-tuple-element.49), channel_id=1, source_target_pairs={{0,3},{1,2},{2,1},{3,0},{4,7},{5,6},{6,5},{7,4},{8,11},{9,10},{10,... | collective-permute-start | bytes 98312 | tf_op jit(solution)/shard_map/ppermute | solution.py:331
  41.7 0.1 core_sum.1
  41.8 0.7 collective-permute-start.15
  42.5 1.5 %collective-permute-start.16 = (bf16[32,512]{1,0:T(8,128)(2,1)S(1)}, bf16[32,512]{1,0:T(8,128)(2,1)S(1)}, u32[]{:S(2)}, u32[]{:S(2)}) collective-permute-start(bf16[32,512]{1,0:T(8,128)(2,1)S(1)} %get-tuple-element.54), channel_id=1, source_target_pairs={{0,16},{4,20},{8,24},{12,28},{16,0},{20,4},{24,8},{28,12},{1,17},{... | collective-permute-start | bytes 98312 | tf_op jit(solution)/shard_map/ppermute | solution.py:334
  44.0 1.4 %collective-permute-start.17 = (bf16[32,512]{1,0:T(8,128)(2,1)S(1)}, bf16[32,512]{1,0:T(8,128)(2,1)S(1)}, u32[]{:S(2)}, u32[]{:S(2)}) collective-permute-start(bf16[32,512]{1,0:T(8,128)(2,1)S(1)} %get-tuple-element.55), channel_id=1, source_target_pairs={{0,24},{4,28},{8,16},{12,20},{16,8},{20,12},{24,0},{28,4},{1,25},{... | collective-permute-start | bytes 98312 | tf_op jit(solution)/shard_map/ppermute | solution.py:334
  45.4 0.7 collective-permute-done.15.refs_5_
  46.1 0.3 collective-permute-done.16.refs_6_
  46.4 2.4 %collective-permute-done.17.refs_7_ = bf16[32,512]{1,0:T(8,128)(2,1)S(1)} collective-permute-done((bf16[32,512]{1,0:T(8,128)(2,1)S(1)}, bf16[32,512]{1,0:T(8,128)(2,1)S(1)}, u32[]{:S(2)}, u32[]{:S(2)}) %collective-permute-start.17) | collective-permute-done | bytes 32800 | tf_op jit(solution)/shard_map/ppermute | solution.py:334
  48.8 1.1 %moments.1 = (bf16[32,512]{1,0:T(8,128)(2,1)S(1)}, bf16[32,512]{1,0:T(8,128)(2,1)S(1)}, bf16[144,128]{1,0:T(8,128)(2,1)S(1)}) custom-call(bf16[32,512]{1,0:T(8,128)(2,1)S(1)} %get-tuple-element.46.refs_0_, bf16[32,512]{1,0:T(8,128)(2,1)S(1)} %collective-permute-done.11.refs_1_, bf16[32,512]{1,0:T(8,128)(2,1)S(1)} %collective-permute-done.12.refs_2_, ...), custom_call_target="tpu_custom_call" | custom-call | flops 1 | bytes 790528 | tf_op jit(solution)/shard_map/moments/pallas_call | solution.py:31
  49.9 0.1 collective-permute-start.20
  49.9 1.2 %collective-permute-done.20.refs_3_ = bf16[144,128]{1,0:T(8,128)(2,1)S(1)} collective-permute-done((bf16[144,128]{1,0:T(8,128)(2,1)S(1)}, bf16[144,128]{1,0:T(8,128)(2,1)S(1)}, u32[]{:S(2)}, u32[]{:S(2)}) %collective-permute-start.20) | collective-permute-done | bytes 36896 | tf_op jit(solution)/shard_map/ppermute | solution.py:337
  51.1 0.1 first_stat.1
  51.2 2.0 %collective-permute-start.21 = (bf16[272,128]{1,0:T(8,128)(2,1)S(1)}, bf16[272,128]{1,0:T(8,128)(2,1)S(1)}, u32[]{:S(2)}, u32[]{:S(2)}) collective-permute-start(bf16[272,128]{1,0:T(8,128)(2,1)S(1)} %get-tuple-element.63), channel_id=1, source_target_pairs={{0,8},{4,12},{8,0},{12,4},{16,24},{20,28},{24,16},{28,20},{1,9},{5... | collective-permute-start | bytes 208904 | tf_op jit(solution)/shard_map/ppermute | solution.py:334
  53.2 0.1 collective-permute-start.22
  53.3 1.5 %collective-permute-start.23 = (bf16[272,128]{1,0:T(8,128)(2,1)S(1)}, bf16[272,128]{1,0:T(8,128)(2,1)S(1)}, u32[]{:S(2)}, u32[]{:S(2)}) collective-permute-start(bf16[272,128]{1,0:T(8,128)(2,1)S(1)} %get-tuple-element.65), channel_id=1, source_target_pairs={{0,24},{4,28},{8,16},{12,20},{16,8},{20,12},{24,0},{28,4},{1,25},{... | collective-permute-start | bytes 208904 | tf_op jit(solution)/shard_map/ppermute | solution.py:334
  54.8 1.0 %collective-permute-done.21.refs_1_ = bf16[272,128]{1,0:T(8,128)(2,1)S(1)} collective-permute-done((bf16[272,128]{1,0:T(8,128)(2,1)S(1)}, bf16[272,128]{1,0:T(8,128)(2,1)S(1)}, u32[]{:S(2)}, u32[]{:S(2)}) %collective-permute-start.21) | collective-permute-done | bytes 69664 | tf_op jit(solution)/shard_map/ppermute | solution.py:334
  55.7 3.1 %collective-permute-done.22.refs_2_ = bf16[272,128]{1,0:T(8,128)(2,1)S(1)} collective-permute-done((bf16[272,128]{1,0:T(8,128)(2,1)S(1)}, bf16[272,128]{1,0:T(8,128)(2,1)S(1)}, u32[]{:S(2)}, u32[]{:S(2)}) %collective-permute-start.22) | collective-permute-done | bytes 69664 | tf_op jit(solution)/shard_map/ppermute | solution.py:334
  58.8 0.1 second_stat.1
  58.9 0.1 collective-permute-start.24
  59.0 1.4 %collective-permute-start.25 = (bf16[176,128]{1,0:T(8,128)(2,1)S(1)}, bf16[176,128]{1,0:T(8,128)(2,1)S(1)}, u32[]{:S(2)}, u32[]{:S(2)}) collective-permute-start(bf16[176,128]{1,0:T(8,128)(2,1)S(1)} %get-tuple-element.68), channel_id=1, source_target_pairs={{0,2},{1,3},{2,0},{3,1},{4,6},{5,7},{6,4},{7,5},{8,10},{9,11},{10,... | collective-permute-start | bytes 135176 | tf_op jit(solution)/shard_map/ppermute | solution.py:331
  60.4 3.0 %collective-permute-start.26 = (bf16[176,128]{1,0:T(8,128)(2,1)S(1)}, bf16[176,128]{1,0:T(8,128)(2,1)S(1)}, u32[]{:S(2)}, u32[]{:S(2)}) collective-permute-start(bf16[176,128]{1,0:T(8,128)(2,1)S(1)} %get-tuple-element.69), channel_id=1, source_target_pairs={{0,3},{1,2},{2,1},{3,0},{4,7},{5,6},{6,5},{7,4},{8,11},{9,10},{10,... | collective-permute-start | bytes 135176 | tf_op jit(solution)/shard_map/ppermute | solution.py:331
  63.3 3.3 %collective-permute-start.18 = (bf16[32,512]{1,0:T(8,128)(2,1)S(1)}, bf16[32,512]{1,0:T(8,128)(2,1)S(1)}, u32[]{:S(2)}, u32[]{:S(2)}) collective-permute-start(bf16[32,512]{1,0:T(8,128)(2,1)S(1)} %get-tuple-element.58), channel_id=1, source_target_pairs={{0,0},{1,8},{2,16},{3,24},{4,4},{5,12},{6,20},{7,28},{8,1},{9,9},{... | collective-permute-start | bytes 98312 | tf_op jit(solution)/shard_map/ppermute | solution.py:346
  66.7 0.1 copy.24.lw_ref.refs_5_
  66.8 0.1 copy.25.rw_ref.refs_6_
  66.9 0.1 copy.26.refs_4_
  67.1 5.7 %collective-permute-done.18.right_ref = bf16[32,512]{1,0:T(8,128)(2,1)S(1)} collective-permute-done((bf16[32,512]{1,0:T(8,128)(2,1)S(1)}, bf16[32,512]{1,0:T(8,128)(2,1)S(1)}, u32[]{:S(2)}, u32[]{:S(2)}) %collective-permute-start.18) | collective-permute-done | bytes 32800 | tf_op jit(solution)/shard_map/ppermute | solution.py:346
  72.7 1.7 %input_grad.1 = bf16[32,16,256]{2,1,0:T(8,128)(2,1)} custom-call(bf16[32,16,256]{2,1,0:T(8,128)(2,1)S(1)} %copy-done.1, f32[1,256]{1,0:T(1,128)S(1)} %bitcast.9, bf16[256,32]{1,0:T(8,128)(2,1)S(1)} %copy.24.lw_ref.refs_5_, bf16[256,32]{1,0:T(8,128)(2,1)S(1)} %copy.25.rw_ref.refs_6_, bf16[32,512]{1,0:T(8,128)(2,1)S(1)} %get-tuple-element.57.left_ref, ...), custom_call_target="tpu_custom_call" | custom-call | flops 1 | bytes 361472 | tf_op jit(solution)/shard_map/input_grad/pallas_call | solution.py:31
  74.4 1.0 %last_stat.1 = (f32[256,32]{1,0:T(8,128)S(1)}, f32[256,32]{1,0:T(8,128)S(1)}, f32[32,128]{1,0:T(8,128)}, f32[256,1]{1,0:T(8,128)S(1)}, f32[1,128]{1,0:T(1,128)}) custom-call(bf16[176,128]{1,0:T(8,128)(2,1)S(1)} %get-tuple-element.66.refs_0_, bf16[176,128]{1,0:T(8,128)(2,1)S(1)} %collective-permute-done.24.refs_1_, ...), custom_call_target="tpu_custom_call" | custom-call | flops 1 | bytes 214016 | tf_op jit(solution)/shard_map/last_stat/pallas_call | solution.py:31
  75.4 0.7 copy.29
  76.1 0.7 copy.30
  76.7 0.7 reduce
  (27 shorter events, 0.1 us)
Async XLA Ops:
  0.6 14.5 %collective-permute-start.3 = (bf16[32,16,256]{2,1,0:T(8,128)(2,1)}, bf16[32,16,256]{2,1,0:T(8,128)(2,1)S(1)}, u32[]{:S(2)}, u32[]{:S(2)}) collective-permute-start(bf16[32,16,256]{2,1,0:T(8,128)(2,1)} %x_ref.3), channel_id=1, source_target_pairs={{0,0},{1,8},{2,16},{3,24},{4,4},{5,12},{6,20},{7,28},{8,1},{9,9},{... | collective-permute-start | bytes 786440 | tf_op jit(solution)/shard_map/ppermute | solution.py:346
  5.5 0.7 copy-start.2
  6.2 0.9 %copy-start = (bf16[32,16,256]{2,1,0:T(8,128)(2,1)S(1)}, bf16[32,16,256]{2,1,0:T(8,128)(2,1)}, u32[]{:S(2)}) copy-start(bf16[32,16,256]{2,1,0:T(8,128)(2,1)} %x_ref.3) | copy-start | bytes 786436
  7.1 0.8 copy-start.7
  7.8 19.8 %collective-permute-start = (bf16[32,512]{1,0:T(8,128)(2,1)S(1)}, bf16[32,512]{1,0:T(8,128)(2,1)S(1)}, u32[]{:S(2)}, u32[]{:S(2)}) collective-permute-start(bf16[32,512]{1,0:T(8,128)(2,1)S(1)} %left.1.refs_0_), channel_id=1, source_target_pairs={{0,1},{1,0},{2,3},{3,2},{4,5},{5,4},{6,7},{7,6},{8,9},{9,8},{10,11... | collective-permute-start | bytes 98312 | tf_op jit(solution)/shard_map/ppermute | solution.py:331
  7.8 20.0 %collective-permute-start.1 = (bf16[32,512]{1,0:T(8,128)(2,1)S(1)}, bf16[32,512]{1,0:T(8,128)(2,1)S(1)}, u32[]{:S(2)}, u32[]{:S(2)}) collective-permute-start(bf16[32,512]{1,0:T(8,128)(2,1)S(1)} %left.1.refs_0_), channel_id=1, source_target_pairs={{0,2},{1,3},{2,0},{3,1},{4,6},{5,7},{6,4},{7,5},{8,10},{9,11},{10,... | collective-permute-start | bytes 98312 | tf_op jit(solution)/shard_map/ppermute | solution.py:331
  7.9 23.6 %copy-start.3 = (bf16[1024,128]{1,0:T(8,128)(2,1)S(1)}, bf16[1024,128]{1,0:T(8,128)(2,1)}, u32[]{:S(2)}) copy-start(bf16[1024,128]{1,0:T(8,128)(2,1)} %refs_3_.1) | copy-start | bytes 786436
  8.0 23.4 %copy-start.4 = (bf16[16,32,128]{2,1,0:T(8,128)(2,1)S(1)}, bf16[16,32,128]{2,1,0:T(8,128)(2,1)}, u32[]{:S(2)}) copy-start(bf16[16,32,128]{2,1,0:T(8,128)(2,1)} %cot_ref.1) | copy-start | bytes 393220
  15.7 12.1 %collective-permute-start.9 = (bf16[32,512]{1,0:T(8,128)(2,1)S(1)}, bf16[32,512]{1,0:T(8,128)(2,1)S(1)}, u32[]{:S(2)}, u32[]{:S(2)}) collective-permute-start(bf16[32,512]{1,0:T(8,128)(2,1)S(1)} %right.1.refs_4_), channel_id=1, source_target_pairs={{0,24},{4,28},{8,16},{12,20},{16,8},{20,12},{24,0},{28,4},{1,25},{... | collective-permute-start | bytes 98312 | tf_op jit(solution)/shard_map/ppermute | solution.py:334
  15.8 14.0 %collective-permute-start.5 = (bf16[32,512]{1,0:T(8,128)(2,1)S(1)}, bf16[32,512]{1,0:T(8,128)(2,1)S(1)}, u32[]{:S(2)}, u32[]{:S(2)}) collective-permute-start(bf16[32,512]{1,0:T(8,128)(2,1)S(1)} %right.1.refs_4_), channel_id=1, source_target_pairs={{0,8},{4,12},{8,0},{12,4},{16,24},{20,28},{24,16},{28,20},{1,9},{5... | collective-permute-start | bytes 98312 | tf_op jit(solution)/shard_map/ppermute | solution.py:334
  27.6 3.9 %collective-permute-start.7 = (bf16[32,512]{1,0:T(8,128)(2,1)S(1)}, bf16[32,512]{1,0:T(8,128)(2,1)S(1)}, u32[]{:S(2)}, u32[]{:S(2)}) collective-permute-start(bf16[32,512]{1,0:T(8,128)(2,1)S(1)} %right.1.refs_4_), channel_id=1, source_target_pairs={{0,16},{4,20},{8,24},{12,28},{16,0},{20,4},{24,8},{28,12},{1,17},{... | collective-permute-start | bytes 98312 | tf_op jit(solution)/shard_map/ppermute | solution.py:334
  27.6 5.7 %collective-permute-start.2 = (bf16[32,512]{1,0:T(8,128)(2,1)S(1)}, bf16[32,512]{1,0:T(8,128)(2,1)S(1)}, u32[]{:S(2)}, u32[]{:S(2)}) collective-permute-start(bf16[32,512]{1,0:T(8,128)(2,1)S(1)} %left.1.refs_0_), channel_id=1, source_target_pairs={{0,3},{1,2},{2,1},{3,0},{4,7},{5,6},{6,5},{7,4},{8,11},{9,10},{10,... | collective-permute-start | bytes 98312 | tf_op jit(solution)/shard_map/ppermute | solution.py:331
  27.8 5.5 %collective-permute-start.4 = (bf16[32,512]{1,0:T(8,128)(2,1)S(1)}, bf16[32,512]{1,0:T(8,128)(2,1)S(1)}, u32[]{:S(2)}, u32[]{:S(2)}) collective-permute-start(bf16[32,512]{1,0:T(8,128)(2,1)S(1)} %right.1.refs_4_), channel_id=1, source_target_pairs={{0,4},{4,0},{8,12},{12,8},{16,20},{20,16},{24,28},{28,24},{1,5},{5... | collective-permute-start | bytes 98312 | tf_op jit(solution)/shard_map/ppermute | solution.py:337
  27.8 5.5 %collective-permute-start.10 = (bf16[32,512]{1,0:T(8,128)(2,1)S(1)}, bf16[32,512]{1,0:T(8,128)(2,1)S(1)}, u32[]{:S(2)}, u32[]{:S(2)}) collective-permute-start(bf16[32,512]{1,0:T(8,128)(2,1)S(1)} %collective-permute-done.9.refs_10_), channel_id=1, source_target_pairs={{0,4},{4,0},{8,12},{12,8},{16,20},{20,16},{24,28},{28,24},{1,5},{5... | collective-permute-start | bytes 98312 | tf_op jit(solution)/shard_map/ppermute | solution.py:337
  29.8 3.5 %collective-permute-start.6 = (bf16[32,512]{1,0:T(8,128)(2,1)S(1)}, bf16[32,512]{1,0:T(8,128)(2,1)S(1)}, u32[]{:S(2)}, u32[]{:S(2)}) collective-permute-start(bf16[32,512]{1,0:T(8,128)(2,1)S(1)} %collective-permute-done.5.refs_6_), channel_id=1, source_target_pairs={{0,4},{4,0},{8,12},{12,8},{16,20},{20,16},{24,28},{28,24},{1,5},{5... | collective-permute-start | bytes 98312 | tf_op jit(solution)/shard_map/ppermute | solution.py:337
  31.5 1.8 %collective-permute-start.8 = (bf16[32,512]{1,0:T(8,128)(2,1)S(1)}, bf16[32,512]{1,0:T(8,128)(2,1)S(1)}, u32[]{:S(2)}, u32[]{:S(2)}) collective-permute-start(bf16[32,512]{1,0:T(8,128)(2,1)S(1)} %collective-permute-done.7.refs_8_), channel_id=1, source_target_pairs={{0,4},{4,0},{8,12},{12,8},{16,20},{20,16},{24,28},{28,24},{1,5},{5... | collective-permute-start | bytes 98312 | tf_op jit(solution)/shard_map/ppermute | solution.py:337
  34.0 7.7 %collective-permute-start.14 = (bf16[128,512]{1,0:T(8,128)(2,1)S(1)}, bf16[128,512]{1,0:T(8,128)(2,1)S(1)}, u32[]{:S(2)}, u32[]{:S(2)}) collective-permute-start(bf16[128,512]{1,0:T(8,128)(2,1)S(1)} %get-tuple-element.51), channel_id=1, source_target_pairs={{0,4},{4,0},{8,12},{12,8},{16,20},{20,16},{24,28},{28,24},{1,5},{5... | collective-permute-start | bytes 393224 | tf_op jit(solution)/shard_map/ppermute | solution.py:337
  34.5 0.7 copy-start.5
  37.3 11.5 %copy-start.1 = (bf16[32,16,256]{2,1,0:T(8,128)(2,1)S(1)}, bf16[32,16,256]{2,1,0:T(8,128)(2,1)}, u32[]{:S(2)}) copy-start(bf16[32,16,256]{2,1,0:T(8,128)(2,1)} %x_ref.3) | copy-start | bytes 786436
  37.3 12.7 %collective-permute-start.19 = (bf16[4,128,128]{2,1,0:T(8,128)(2,1)S(1)}, bf16[4,128,128]{2,1,0:T(8,128)(2,1)S(1)}, u32[]{:S(2)}, u32[]{:S(2)}) collective-permute-start(bf16[4,128,128]{2,1,0:T(8,128)(2,1)S(1)} %get-tuple-element.60), channel_id=1, source_target_pairs={{0,4},{4,0},{8,12},{12,8},{16,20},{20,16},{24,28},{28,24},{1,5},{5... | collective-permute-start | bytes 393224 | tf_op jit(solution)/shard_map/ppermute | solution.py:337
  37.3 5.2 %collective-permute-start.11 = (bf16[32,512]{1,0:T(8,128)(2,1)S(1)}, bf16[32,512]{1,0:T(8,128)(2,1)S(1)}, u32[]{:S(2)}, u32[]{:S(2)}) collective-permute-start(bf16[32,512]{1,0:T(8,128)(2,1)S(1)} %get-tuple-element.47), channel_id=1, source_target_pairs={{0,1},{1,0},{2,3},{3,2},{4,5},{5,4},{6,7},{7,6},{8,9},{9,8},{10,11... | collective-permute-start | bytes 98312 | tf_op jit(solution)/shard_map/ppermute | solution.py:331
  37.3 6.6 %collective-permute-start.12 = (bf16[32,512]{1,0:T(8,128)(2,1)S(1)}, bf16[32,512]{1,0:T(8,128)(2,1)S(1)}, u32[]{:S(2)}, u32[]{:S(2)}) collective-permute-start(bf16[32,512]{1,0:T(8,128)(2,1)S(1)} %get-tuple-element.48), channel_id=1, source_target_pairs={{0,2},{1,3},{2,0},{3,1},{4,6},{5,7},{6,4},{7,5},{8,10},{9,11},{10,... | collective-permute-start | bytes 98312 | tf_op jit(solution)/shard_map/ppermute | solution.py:331
  38.8 6.6 %collective-permute-start.13 = (bf16[32,512]{1,0:T(8,128)(2,1)S(1)}, bf16[32,512]{1,0:T(8,128)(2,1)S(1)}, u32[]{:S(2)}, u32[]{:S(2)}) collective-permute-start(bf16[32,512]{1,0:T(8,128)(2,1)S(1)} %get-tuple-element.49), channel_id=1, source_target_pairs={{0,3},{1,2},{2,1},{3,0},{4,7},{5,6},{6,5},{7,4},{8,11},{9,10},{10,... | collective-permute-start | bytes 98312 | tf_op jit(solution)/shard_map/ppermute | solution.py:331
  41.8 4.3 %collective-permute-start.15 = (bf16[32,512]{1,0:T(8,128)(2,1)S(1)}, bf16[32,512]{1,0:T(8,128)(2,1)S(1)}, u32[]{:S(2)}, u32[]{:S(2)}) collective-permute-start(bf16[32,512]{1,0:T(8,128)(2,1)S(1)} %get-tuple-element.53), channel_id=1, source_target_pairs={{0,8},{4,12},{8,0},{12,4},{16,24},{20,28},{24,16},{28,20},{1,9},{5... | collective-permute-start | bytes 98312 | tf_op jit(solution)/shard_map/ppermute | solution.py:334
  42.5 3.9 %collective-permute-start.16 = (bf16[32,512]{1,0:T(8,128)(2,1)S(1)}, bf16[32,512]{1,0:T(8,128)(2,1)S(1)}, u32[]{:S(2)}, u32[]{:S(2)}) collective-permute-start(bf16[32,512]{1,0:T(8,128)(2,1)S(1)} %get-tuple-element.54), channel_id=1, source_target_pairs={{0,16},{4,20},{8,24},{12,28},{16,0},{20,4},{24,8},{28,12},{1,17},{... | collective-permute-start | bytes 98312 | tf_op jit(solution)/shard_map/ppermute | solution.py:334
  44.0 4.8 %collective-permute-start.17 = (bf16[32,512]{1,0:T(8,128)(2,1)S(1)}, bf16[32,512]{1,0:T(8,128)(2,1)S(1)}, u32[]{:S(2)}, u32[]{:S(2)}) collective-permute-start(bf16[32,512]{1,0:T(8,128)(2,1)S(1)} %get-tuple-element.55), channel_id=1, source_target_pairs={{0,24},{4,28},{8,16},{12,20},{16,8},{20,12},{24,0},{28,4},{1,25},{... | collective-permute-start | bytes 98312 | tf_op jit(solution)/shard_map/ppermute | solution.py:334
  49.9 1.3 %collective-permute-start.20 = (bf16[144,128]{1,0:T(8,128)(2,1)S(1)}, bf16[144,128]{1,0:T(8,128)(2,1)S(1)}, u32[]{:S(2)}, u32[]{:S(2)}) collective-permute-start(bf16[144,128]{1,0:T(8,128)(2,1)S(1)} %get-tuple-element.61.refs_2_), channel_id=1, source_target_pairs={{0,4},{4,0},{8,12},{12,8},{16,20},{20,16},{24,28},{28,24},{1,5},{5... | collective-permute-start | bytes 110600 | tf_op jit(solution)/shard_map/ppermute | solution.py:337
  51.2 4.5 %collective-permute-start.21 = (bf16[272,128]{1,0:T(8,128)(2,1)S(1)}, bf16[272,128]{1,0:T(8,128)(2,1)S(1)}, u32[]{:S(2)}, u32[]{:S(2)}) collective-permute-start(bf16[272,128]{1,0:T(8,128)(2,1)S(1)} %get-tuple-element.63), channel_id=1, source_target_pairs={{0,8},{4,12},{8,0},{12,4},{16,24},{20,28},{24,16},{28,20},{1,9},{5... | collective-permute-start | bytes 208904 | tf_op jit(solution)/shard_map/ppermute | solution.py:334
  53.2 5.6 %collective-permute-start.22 = (bf16[272,128]{1,0:T(8,128)(2,1)S(1)}, bf16[272,128]{1,0:T(8,128)(2,1)S(1)}, u32[]{:S(2)}, u32[]{:S(2)}) collective-permute-start(bf16[272,128]{1,0:T(8,128)(2,1)S(1)} %get-tuple-element.64), channel_id=1, source_target_pairs={{0,16},{4,20},{8,24},{12,28},{16,0},{20,4},{24,8},{28,12},{1,17},{... | collective-permute-start | bytes 208904 | tf_op jit(solution)/shard_map/ppermute | solution.py:334
  53.3 5.5 %collective-permute-start.23 = (bf16[272,128]{1,0:T(8,128)(2,1)S(1)}, bf16[272,128]{1,0:T(8,128)(2,1)S(1)}, u32[]{:S(2)}, u32[]{:S(2)}) collective-permute-start(bf16[272,128]{1,0:T(8,128)(2,1)S(1)} %get-tuple-element.65), channel_id=1, source_target_pairs={{0,24},{4,28},{8,16},{12,20},{16,8},{20,12},{24,0},{28,4},{1,25},{... | collective-permute-start | bytes 208904 | tf_op jit(solution)/shard_map/ppermute | solution.py:334
  58.8 7.9 %copy-start.6 = (bf16[256,32]{0,1:T(8,128)(2,1)S(1)}, bf16[256,32]{0,1:T(8,128)(2,1)}, u32[]{:S(2)}) copy-start(bf16[256,32]{0,1:T(8,128)(2,1)} %param.9) | copy-start | bytes 49156
  58.9 15.5 %collective-permute-start.24 = (bf16[176,128]{1,0:T(8,128)(2,1)S(1)}, bf16[176,128]{1,0:T(8,128)(2,1)S(1)}, u32[]{:S(2)}, u32[]{:S(2)}) collective-permute-start(bf16[176,128]{1,0:T(8,128)(2,1)S(1)} %get-tuple-element.67), channel_id=1, source_target_pairs={{0,1},{1,0},{2,3},{3,2},{4,5},{5,4},{6,7},{7,6},{8,9},{9,8},{10,11... | collective-permute-start | bytes 135176 | tf_op jit(solution)/shard_map/ppermute | solution.py:331
  59.0 15.4 %collective-permute-start.25 = (bf16[176,128]{1,0:T(8,128)(2,1)S(1)}, bf16[176,128]{1,0:T(8,128)(2,1)S(1)}, u32[]{:S(2)}, u32[]{:S(2)}) collective-permute-start(bf16[176,128]{1,0:T(8,128)(2,1)S(1)} %get-tuple-element.68), channel_id=1, source_target_pairs={{0,2},{1,3},{2,0},{3,1},{4,6},{5,7},{6,4},{7,5},{8,10},{9,11},{10,... | collective-permute-start | bytes 135176 | tf_op jit(solution)/shard_map/ppermute | solution.py:331
  60.4 14.0 %collective-permute-start.26 = (bf16[176,128]{1,0:T(8,128)(2,1)S(1)}, bf16[176,128]{1,0:T(8,128)(2,1)S(1)}, u32[]{:S(2)}, u32[]{:S(2)}) collective-permute-start(bf16[176,128]{1,0:T(8,128)(2,1)S(1)} %get-tuple-element.69), channel_id=1, source_target_pairs={{0,3},{1,2},{2,1},{3,0},{4,7},{5,6},{6,5},{7,4},{8,11},{9,10},{10,... | collective-permute-start | bytes 135176 | tf_op jit(solution)/shard_map/ppermute | solution.py:331
  63.3 9.4 %collective-permute-start.18 = (bf16[32,512]{1,0:T(8,128)(2,1)S(1)}, bf16[32,512]{1,0:T(8,128)(2,1)S(1)}, u32[]{:S(2)}, u32[]{:S(2)}) collective-permute-start(bf16[32,512]{1,0:T(8,128)(2,1)S(1)} %get-tuple-element.58), channel_id=1, source_target_pairs={{0,0},{1,8},{2,16},{3,24},{4,4},{5,12},{6,20},{7,28},{8,1},{9,9},{... | collective-permute-start | bytes 98312 | tf_op jit(solution)/shard_map/ppermute | solution.py:346

commit v2 on v1

v2 whole, which is shorter than its diff:
```python
import functools

import jax
import jax.numpy as jnp
from jax import lax
from jax.experimental import pallas as pl
from jax.experimental.pallas import tpu as pltpu
from jax.sharding import PartitionSpec as P


F32, BF16 = jnp.float32, jnp.bfloat16
LANES = 128


def product(a, b, over=((1,), (0,))):
    return lax.dot_general(a, b, (over, ((), ())), preferred_element_type=F32)


def tree(terms):
    while len(terms) > 1:
        terms = [a + b for a, b in zip(terms[::2], terms[1::2])]
    return terms[0]


def wide(ref):
    return ref[...].astype(F32)


def call(body, args, outs, scratch=(), flops=1, limit=24, far=0):
    spec = pl.BlockSpec(memory_space=pltpu.VMEM)
    args = [
        pltpu.with_memory_space_constraint(a, pltpu.HBM) if n < far else a
        for n, a in enumerate(args)
    ]
    moved = sum(a.size * a.dtype.itemsize for a in args)
    return pl.pallas_call(
        body,
        out_shape=[jax.ShapeDtypeStruct(d, t) for d, t in outs],
        in_specs=[pl.BlockSpec(memory_space=pltpu.HBM)] * far + [spec] * (len(args) - far),
        out_specs=[spec] * len(outs),
        scratch_shapes=list(scratch),
        cost_estimate=pl.CostEstimate(flops=flops, bytes_accessed=moved, transcendentals=0),
        compiler_params=pltpu.CompilerParams(vmem_limit_bytes=limit << 20),
    )(*args)


def normalize(rows):
    center = rows - jnp.mean(rows, axis=-1, keepdims=True)
    inverse = lax.rsqrt(jnp.mean(center * center, axis=-1, keepdims=True) + 1e-05)
    return center * inverse, inverse


def by_residue(x_ref, flat):
    seqs, residues, width = x_ref.shape
    values = wide(x_ref).reshape(seqs * residues, width)
    halves = range(width // LANES)
    for k in halves:
        flat[k] = values[:, k * LANES : (k + 1) * LANES]
    return [
        jnp.concatenate([flat[k, pl.ds(i, seqs, stride=residues), :] for k in halves], axis=1)
        for i in range(residues)
    ]


def channel_first(residues, chans):
    size = residues * chans
    source = lax.broadcasted_iota(jnp.int32, (size, size), 0)
    target = lax.broadcasted_iota(jnp.int32, (size, size), 1)
    place = (source % chans) * residues + source // chans
    return jnp.where(place == target, 1.0, 0.0).astype(BF16)


def fetch(pairs, sems):
    copies = [
        pltpu.make_async_copy(source, target, sems.at[n])
        for n, (source, target) in enumerate(pairs)
    ]
    for copy in copies:
        copy.start()
    return copies


def project_kernel(chans, *refs):
    count = (len(refs) - 4) // 2
    sources, targets = refs[:count], refs[count : 2 * count]
    left_ref, right_ref, flat, sems = refs[2 * count :]
    copies = fetch(zip(sources, targets), sems)
    for copy in copies[:4]:
        copy.wait()
    x_in, gain_in = targets[:2]
    seqs, residues, _ = x_in.shape
    normed, _ = normalize(jnp.concatenate(by_residue(x_in, flat), axis=0))
    ln_out = normed * gain_in[...]
    pack = LANES // chans
    places = []
    for weight_in in targets[2:4]:
        weight = weight_in[...]
        zero = jnp.zeros_like(weight)
        places += [
            jnp.concatenate([weight if k == m else zero for m in range(pack)], axis=1)
            for k in range(pack)
        ]
    weights = jnp.concatenate(places, axis=0)
    left, right = [], []
    for g in range(residues // pack):
        piece = jnp.concatenate(
            [ln_out[(g * pack + k) * seqs : (g * pack + k + 1) * seqs] for k in range(pack)], axis=1
        )
        both = product(piece.astype(BF16), weights, ((1,), (1,)))
        left.append(both[:, :LANES])
        right.append(both[:, LANES:])
    right_ref[...] = jnp.concatenate(right, axis=1).astype(BF16)
    left = jnp.concatenate(left, axis=1).astype(BF16)
    left_ref[...] = product(left, channel_first(residues, chans)).astype(BF16)
    for copy in copies[4:]:
        copy.wait()


def spread_weight(w_ref, spread, chans):
    pack = LANES // chans
    pair_w = w_ref.shape[1]
    spread[...] = jnp.zeros_like(spread)
    for c in range(chans):
        block = w_ref[c * chans : (c + 1) * chans, :]
        for k in range(pack):
            row = c * LANES + k * chans
            spread[row : row + chans, k * pair_w : (k + 1) * pair_w] = block


def grad_kernel(chans, cot_ref, w_ref, og_ref, cotk_ref, bias_ref, flat, spread):
    residues, seconds, pair_w = cot_ref.shape
    pack = LANES // chans
    groups = seconds // pack
    cot = wide(cot_ref).reshape(residues * seconds, pair_w)
    flat[...] = cot
    bias_ref[...] = jnp.broadcast_to(jnp.sum(cot, axis=0, keepdims=True), bias_ref.shape)
    spread_weight(w_ref, spread, chans)
    for k in range(pack):
        rows = [flat[pl.ds(g * pack + k, residues, stride=seconds), :] for g in range(groups)]
        cotk_ref[k] = jnp.concatenate(rows, axis=0).astype(BF16)
    cot_wide = jnp.concatenate([cotk_ref[k] for k in range(pack)], axis=1)
    chunk = 8
    for first in range(0, chans, chunk):
        part = spread[first * LANES : (first + chunk) * LANES, :]
        out = product(cot_wide, part, ((1,), (1,))).astype(BF16)
        for c in range(chunk):
            for g in range(groups):
                row = (first + c) * residues
                og_ref[row : row + residues, g * LANES : (g + 1) * LANES] = out[
                    g * residues : (g + 1) * residues, c * LANES : (c + 1) * LANES
                ]


def places(ratio):
    row, col = lax.axis_index("row"), lax.axis_index("col")
    return row // ratio, row % ratio, col


def right_grad_kernel(cols, ratio, *refs):
    left_in, og_ref = refs[:cols], refs[cols]
    outs, (all_ref, gathered, sums) = refs[cols + 1 : cols + 1 + ratio], refs[cols + 1 + ratio :]
    seqs, width = left_in[0].shape
    _, h, z = places(ratio)
    for k in range(cols):
        gathered[pl.ds(pl.multiple_of((z ^ k) * seqs, seqs), seqs), :] = wide(left_in[k])
    left = gathered[...].astype(BF16)
    all_ref[...] = left
    for e in range(ratio):
        sums[e] = product(left, og_ref[:, e * width : (e + 1) * width]) * (1.0 / (seqs * cols))
    for e in range(ratio):
        outs[e][...] = sums[h ^ e].astype(BF16)


def left_grad_kernel(cols, ratio, *refs):
    right_in, og_ref = refs[: cols * ratio], refs[cols * ratio]
    outs, (all_ref, gathered, sums) = refs[cols * ratio + 1 : -3], refs[-3:]
    seqs, width = right_in[0].shape
    q, h, z = places(ratio)
    for k in range(cols):
        place = pl.ds(pl.multiple_of((q ^ k ^ (cols - 1)) * seqs, seqs), seqs)
        for e in range(ratio):
            gathered[h ^ e, place, :] = wide(right_in[k * ratio + e])
    parts = []
    for e in range(ratio):
        right = gathered[e].astype(BF16)
        all_ref[e] = right
        parts.append(product(right, og_ref[:, e * width : (e + 1) * width], ((1,), (1,))))
    sums[...] = sum(parts) * (1.0 / (seqs * cols))
    for k in range(cols):
        place = pl.ds(pl.multiple_of((z ^ k) * seqs, seqs), seqs)
        outs[k][...] = sums[place, :].astype(BF16)


def forward_kernel(chans, ratio, *refs):
    left_ref, right_ref, cotk_ref, w_ref, bias_ref, pair_ref = refs[:6]
    proj_out, (flat, spread, facing, turned, proj) = refs[6 : 6 + ratio], refs[6 + ratio :]
    residues, seconds, pair_w = pair_ref.shape
    pack = LANES // chans
    groups = seconds // pack
    total = left_ref.shape[0]
    _, h, _ = places(ratio)
    spread_weight(w_ref, spread, chans)
    left = left_ref[...]
    part = groups // ratio
    for e in range(ratio):
        outer = product(left, right_ref[e], ((0,), (0,)))
        outer = (outer * (1.0 / total)).astype(BF16)
        for c in range(chans):
            for g in range(part):
                row = (e * part + g) * residues
                facing[row : row + residues, c * LANES : (c + 1) * LANES] = outer[
                    c * residues : (c + 1) * residues, g * LANES : (g + 1) * LANES
                ]
    pair = product(facing[...], spread[...])
    for g in range(groups):
        for k in range(pack):
            block = pair[g * residues : (g + 1) * residues, k * pair_w : (k + 1) * pair_w]
            flat[pl.ds(g * pack + k, residues, stride=seconds), :] = block + bias_ref[...]
    pair_ref[...] = flat[...].astype(BF16).reshape(residues, seconds, pair_w)
    size = groups * residues
    for c in range(chans):
        block = facing[:, c * LANES : (c + 1) * LANES].T
        for k in range(pack):
            turned[c * chans : (c + 1) * chans, k * size : (k + 1) * size] = block[
                k * chans : (k + 1) * chans
            ]
    cot = jnp.concatenate([cotk_ref[k] for k in range(pack)], axis=0)
    out = product(turned[...], cot)
    count, height = proj_out[0].shape[:2]
    proj[...] = out.reshape(count, ratio, height, pair_w)
    for e in range(ratio):
        for q in range(count):
            proj_out[e][q] = proj[q, h ^ e].astype(BF16)


def stacked(value, residues, chans):
    return jnp.concatenate(
        [value[:, i * chans : (i + 1) * chans] for i in range(residues)], axis=0
    )


def moment_kernel(cols, chans, *refs):
    left_in, (right_ref, x_ref, bias_ref, left_ref, stat_ref, flat) = refs[:cols], refs[cols:]
    residues, width = x_ref.shape[1:]
    normed, _ = normalize(jnp.concatenate(by_residue(x_ref, flat), axis=0))
    left = tree([wide(r) for r in left_in]).astype(BF16)
    left = product(left, channel_first(residues, chans), ((1,), (1,)))
    left_ref[...] = left.astype(BF16)
    both = [stacked(value, residues, chans) for value in (left, wide(right_ref))]
    both = jnp.concatenate(both, axis=1).astype(BF16)
    moment = product(both, normed.astype(BF16), ((0,), (0,)))
    halves = [moment[:, k * LANES : (k + 1) * LANES] for k in range(width // LANES)]
    bias = jnp.concatenate([bias_ref[...]] * 2, axis=0)
    stat_ref[...] = jnp.concatenate(halves + [bias], axis=0).astype(BF16)


def sum_kernel(*refs):
    refs[-1][...] = tree([wide(r) for r in refs[:-1]]).astype(BF16)


def input_grad_kernel(chans, x_ref, gain_ref, lw_ref, rw_ref, left_ref, right_ref, out_ref, flat):
    seqs, residues, width = x_ref.shape
    normed, inverse = normalize(jnp.concatenate(by_residue(x_ref, flat), axis=0))
    left = stacked(wide(left_ref), residues, chans).astype(BF16)
    right = stacked(wide(right_ref), residues, chans).astype(BF16)
    ln_d = product(left, lw_ref[...]) + product(right, rw_ref[...])
    scaled = ln_d * gain_ref[...]
    mean = jnp.mean(scaled, axis=-1, keepdims=True)
    tilt = jnp.mean(scaled * normed, axis=-1, keepdims=True)
    grad = (scaled - mean - normed * tilt) * inverse
    halves = range(width // LANES)
    for i in range(residues):
        for k in halves:
            piece = grad[i * seqs : (i + 1) * seqs, k * LANES : (k + 1) * LANES]
            flat[k, pl.ds(i, seqs, stride=residues), :] = piece
    values = jnp.concatenate([flat[k] for k in halves], axis=1)
    out_ref[...] = values.astype(BF16).reshape(seqs, residues, width)


def core_sum_kernel(ratio, *refs):
    right_in, refs = refs[:ratio], refs[ratio:]
    outs, flat = refs[:-1], refs[-1]
    seqs = outs[0].shape[0]
    q, _, _ = places(ratio)
    flat[...] = tree([wide(r) for r in right_in])
    for k, out in enumerate(outs):
        place = pl.ds(pl.multiple_of((q ^ k ^ (len(outs) - 1)) * seqs, seqs), seqs)
        out[...] = flat[place, :].astype(BF16)


def first_stat_kernel(ratio, *refs):
    proj_in, stat_in = refs[:ratio], refs[ratio : 2 * ratio]
    outs, scratch = refs[2 * ratio : -1], refs[-1]
    height = scratch.shape[1]
    q, _, _ = places(ratio)
    scratch[...] = tree([wide(r) for r in proj_in])
    stat = tree([wide(r) for r in stat_in]).astype(BF16)
    for k, out in enumerate(outs):
        out[:height] = scratch[q ^ k].astype(BF16)
        out[height:] = stat


def second_stat_kernel(ratio, height, *refs):
    count = (len(refs) - 1) // 2
    ins, outs, scratch = refs[:count], refs[count : 2 * count], refs[-1]
    _, _, z = places(ratio)
    total = tree([wide(r) for r in ins])
    size = height * count
    scratch[...] = total[:size].reshape(scratch.shape)
    stat = total[size:].astype(BF16)
    for k, out in enumerate(outs):
        out[:height] = scratch[z ^ k].astype(BF16)
        out[height:] = stat


def last_stat_kernel(chans, height, scale, *refs):
    ins, (gain_ref, lw_ref, rw_ref) = refs[:-8], refs[-8:-5]
    left_ref, right_ref, proj_ref, norm_ref, bias_ref = refs[-5:]
    total = tree([wide(r) for r in ins]) * scale
    proj_ref[...] = total[:height]
    stat = total[height:]
    width = lw_ref.shape[1]
    size = 2 * chans
    halves = width // LANES
    moment = jnp.concatenate([stat[k * size : (k + 1) * size] for k in range(halves)], axis=1)
    left, right = moment[:chans], moment[chans:]
    norm_ref[...] = jnp.sum(left * wide(lw_ref) + right * wide(rw_ref), axis=0, keepdims=True)
    left_ref[...] = left * gain_ref[...]
    right_ref[...] = right * gain_ref[...]
    bias_ref[...] = stat[halves * size : halves * size + 1]


def whole_step(x, gain, left_w, right_w, out_w, bias, cot):
    seqs, residues, width = x.shape
    chans = left_w.shape[1]
    pair_w = out_w.shape[1]
    rows, cols = lax.axis_size("row"), lax.axis_size("col")
    ratio = rows // cols
    seconds = residues * ratio
    total_seqs, total_res = seqs * cols, residues * rows
    wide_proj, wide_pair = residues * chans, seconds * chans
    pack = LANES // chans
    groups = seconds // pack
    gain_row = gain.reshape(1, width)
    left_t, right_t = left_w.T, right_w.T

    def cols_of(parts):
        pairs = [[(i, i ^ k) for i in range(cols)] for k in range(cols)]
        return [parts[0]] + [lax.ppermute(parts[k], "col", pairs[k]) for k in range(1, cols)]

    def chips_of(parts):
        pairs = [[(i, i ^ (k * ratio)) for i in range(rows)] for k in range(cols)]
        return [parts[0]] + [lax.ppermute(parts[k], "row", pairs[k]) for k in range(1, cols)]

    def cores_of(parts):
        pairs = [[(i, i ^ e) for i in range(rows)] for e in range(ratio)]
        return [parts[0]] + [lax.ppermute(parts[e], "row", pairs[e]) for e in range(1, ratio)]

    pairs = [
        ((q * ratio + h) * cols + z, ((z ^ (cols - 1)) * ratio + h) * cols + q)
        for q in range(cols)
        for h in range(ratio)
        for z in range(cols)
    ]

    sources = (x, gain_row, left_t, right_t, cot, out_w, bias.reshape(1, pair_w))
    outs = call(
        functools.partial(project_kernel, chans),
        sources,
        [(a.shape, a.dtype) for a in sources] + [((seqs, wide_proj), BF16)] * 2,
        [
            pltpu.VMEM((width // LANES, seqs * residues, LANES), F32),
            pltpu.SemaphoreType.DMA((len(sources),)),
        ],
        flops=40_000_000,
        far=len(sources),
    )
    x, gain_row, left_t, right_t, cot, out_w, bias_row = outs[:-2]
    left_own, right_own = outs[-2:]
    right_own = lax.ppermute(right_own, ("row", "col"), pairs)
    left_in = cols_of([left_own] * cols)
    og, cotk, bias_part = call(
        functools.partial(grad_kernel, chans),
        (cot, out_w),
        [
            ((chans * residues, wide_pair), BF16),
            ((pack, groups * residues, pair_w), BF16),
            ((8, pair_w), F32),
        ],
        [
            pltpu.VMEM((residues * seconds, pair_w), F32),
            pltpu.VMEM((chans * LANES, pack * pair_w), BF16),
        ],
        flops=540_000_000,
    )
    right_in = []
    for chip in chips_of([right_own] * cols):
        right_in += cores_of([chip] * ratio)

    outs = call(
        functools.partial(right_grad_kernel, cols, ratio),
        (*left_in, og),
        [((total_seqs, wide_proj), BF16)] * (ratio + 1),
        [
            pltpu.VMEM((total_seqs, wide_proj), F32),
            pltpu.VMEM((ratio, total_seqs, wide_proj), F32),
        ],
        flops=134_000_000,
    )
    right_parts, left_all = outs[:ratio], outs[ratio]
    right_parts = call(
        functools.partial(core_sum_kernel, ratio),
        cores_of(right_parts),
        [((seqs, wide_proj), BF16)] * cols,
        [pltpu.VMEM((total_seqs, wide_proj), F32)],
    )
    right_parts = chips_of(right_parts)
    right_sent = call(sum_kernel, right_parts, [((seqs, wide_proj), BF16)])[0]
    right_d = lax.ppermute(right_sent, ("row", "col"), [(b, a) for a, b in pairs])

    outs = call(
        functools.partial(left_grad_kernel, cols, ratio),
        (*right_in, og),
        [((seqs, wide_proj), BF16)] * cols + [((ratio, total_seqs, wide_proj), BF16)],
        [
            pltpu.VMEM((ratio, total_seqs, wide_proj), F32),
            pltpu.VMEM((total_seqs, wide_proj), F32),
        ],
        flops=134_000_000,
    )
    left_parts, right_all = outs[:cols], outs[cols]
    left_parts = cols_of(left_parts)

    block = chans * chans // rows
    outs = call(
        functools.partial(forward_kernel, chans, ratio),
        (left_all, right_all, cotk, out_w, bias_row),
        [((residues, seconds, pair_w), BF16)] + [((cols, block, pair_w), BF16)] * ratio,
        [
            pltpu.VMEM((residues * seconds, pair_w), F32),
            pltpu.VMEM((chans * LANES, pack * pair_w), BF16),
            pltpu.VMEM((groups * residues, chans * LANES), BF16),
            pltpu.VMEM((chans * chans, pack * groups * residues), BF16),
            pltpu.VMEM((cols, ratio, block, pair_w), F32),
        ],
        flops=800_000_000,
        limit=32,
    )
    pair_update, proj_parts = outs[0], outs[1:]
    proj_core = cores_of(proj_parts)

    stat_rows = 2 * chans * (width // LANES) + 16
    left_d, stat = call(
        functools.partial(moment_kernel, cols, chans),
        (*left_parts, right_d, x, bias_part),
        [((seqs, wide_proj), BF16), ((stat_rows, LANES), BF16)],
        [pltpu.VMEM((width // LANES, seqs * residues, LANES), F32)],
    )
    stat_core = cores_of([stat] * ratio)
    firsts = call(
        functools.partial(first_stat_kernel, ratio),
        (*proj_core, *stat_core),
        [((block + stat_rows, pair_w), BF16)] * cols,
        [pltpu.VMEM((cols, block, pair_w), F32)],
    )
    firsts = chips_of(firsts)
    height = block // cols
    seconds_out = call(
        functools.partial(second_stat_kernel, ratio, height),
        firsts,
        [((height + stat_rows, pair_w), BF16)] * cols,
        [pltpu.VMEM((cols, height, pair_w), F32)],
    )
    seconds_out = cols_of(seconds_out)
    grad = call(
        functools.partial(input_grad_kernel, chans),
        (x, gain_row, left_t, right_t, left_d, right_d),
        [((seqs, residues, width), BF16)],
        [pltpu.VMEM((width // LANES, seqs * residues, LANES), F32)],
    )[0]
    left_g, right_g, proj_g, norm_g, bias_g = call(
        functools.partial(last_stat_kernel, chans, height, 1.0 / total_res),
        (*seconds_out, gain_row, left_t, right_t),
        [
            ((chans, width), F32),
            ((chans, width), F32),
            ((height, pair_w), F32),
            ((1, width), F32),
            ((1, pair_w), F32),
        ],
    )
    return (
        pair_update,
        grad,
        left_g.T,
        right_g.T,
        proj_g,
        norm_g.reshape(width),
        bias_g.reshape(pair_w),
    )


def solution(mesh):
    return jax.shard_map(
        whole_step,
        mesh=mesh,
        in_specs=(P("col", "row", None), P(), P(), P(), P(), P(), P("row", "col", None)),
        out_specs=(
            P("row", "col", None),
            P("col", "row", None),
            P(),
            P(),
            P(("row", "col"), None),
            P(),
            P(),
        ),
        check_vma=False,
    )
```

time: 77.7 us -> 57.1 us (0.73)
  the two profiles are of different devices: /device:TPU:24 before, /device:TPU:0 now
where the time goes in v2:
time: 57.1 us; the launch traced here: 57 us
  starting transfers between devices  34.5 us (60%)
  waiting for transfers between devices  11.7 us (20%)
  Pallas kernels  10 us (18%)
  between operations  0.75 us (1%)
    ppermute x9, starting transfers between devices, cols_of(): lax.ppermute(parts[k], 'col', pairs[k])  13.9 us
    ppermute x9, starting transfers between devices, chips_of(): lax.ppermute(parts[k], 'row', pairs[k])  12 us
    pallas_call x12, Pallas kernels, call(): pl.pallas_call(body, out_shape=[jax.ShapeDtypeStruct(d, t) for d, t in ou...  10 us
    ppermute x9, waiting for transfers between devices, chips_of(): lax.ppermute(parts[k], 'row', pairs[k])  5.35 us
    ppermute x1, starting transfers between devices, whole_step(): right_own = lax.ppermute(right_own, ('row', 'col'), pairs)  3.97 us
    ppermute x9, waiting for transfers between devices, cols_of(): lax.ppermute(parts[k], 'col', pairs[k])  3.66 us
    ppermute x1, starting transfers between devices, whole_step(): lax.ppermute(right_sent, ('row', 'col'), [(b, a) for a, b in pairs])  2.96 us
    ppermute x7, starting transfers between devices, cores_of(): lax.ppermute(parts[e], 'row', pairs[e])  1.67 us
  transfers between devices with their start and end apart: 27, of which 8 were waited for; matrix products, arithmetic and copies ran while one was open for 0% of the time, Pallas kernels for 13%

profile of v2, /device:TPU:0, one launch (start us, length us, event | category | flops | bytes accessed | tf_op | source)
XLA Modules:
  0.0 57.0 jit_solution(18408798237334466631)
XLA Ops:
  0.6 2.1 %shard_map.126 = (bf16[32,16,256]{2,1,0:T(8,128)(2,1)S(1)}, f32[1,256]{1,0:T(1,128)S(1)}, bf16[32,256]{1,0:T(8,128)(2,1)S(1)}, bf16[32,256]{1,0:T(8,128)(2,1)S(1...) custom-call(bf16[32,16,256]{2,1,0:T(8,128)(2,1)} %refs_0_.1, ...), custom_call_target="tpu_custom_call" | custom-call | flops 40000000 | bytes 689664 | tf_op jit(solution)/shard_map/pallas_call | solution.py:36
  2.7 4.0 %collective-permute-start.3 = (bf16[32,512]{1,0:T(8,128)(2,1)S(1)}, bf16[32,512]{1,0:T(8,128)(2,1)S(1)}, u32[]{:S(2)}, u32[]{:S(2)}) collective-permute-start(bf16[32,512]{1,0:T(8,128)(2,1)S(1)} %get-tuple-element.54), channel_id=1, source_target_pairs={{0,24},{1,16},{2,8},{3,0},{4,28},{5,20},{6,12},{7,4},{8,25},{9,17}... | collective-permute-start | bytes 98312 | tf_op jit(solution)/shard_map/ppermute | solution.py:380
  6.7 0.5 collective-permute-start
  7.2 1.3 %collective-permute-start.1 = (bf16[32,512]{1,0:T(8,128)(2,1)S(1)}, bf16[32,512]{1,0:T(8,128)(2,1)S(1)}, u32[]{:S(2)}, u32[]{:S(2)}) collective-permute-start(bf16[32,512]{1,0:T(8,128)(2,1)S(1)} %get-tuple-element.49.refs_0_), channel_id=1, source_target_pairs={{0,2},{1,3},{2,0},{3,1},{4,6},{5,7},{6,4},{7,5},{8,10},{9,11},{10,... | collective-permute-start | bytes 98312 | tf_op jit(solution)/shard_map/ppermute | solution.py:349
  8.5 1.3 %collective-permute-done.3.refs_0_ = bf16[32,512]{1,0:T(8,128)(2,1)S(1)} collective-permute-done((bf16[32,512]{1,0:T(8,128)(2,1)S(1)}, bf16[32,512]{1,0:T(8,128)(2,1)S(1)}, u32[]{:S(2)}, u32[]{:S(2)}) %collective-permute-start.3) | collective-permute-done | bytes 32800 | tf_op jit(solution)/shard_map/ppermute | solution.py:380
  9.8 2.1 %collective-permute-start.9 = (bf16[32,512]{1,0:T(8,128)(2,1)S(1)}, bf16[32,512]{1,0:T(8,128)(2,1)S(1)}, u32[]{:S(2)}, u32[]{:S(2)}) collective-permute-start(bf16[32,512]{1,0:T(8,128)(2,1)S(1)} %collective-permute-done.3.refs_0_), channel_id=1, source_target_pairs={{0,24},{4,28},{8,16},{12,20},{16,8},{20,12},{24,0},{28,4},{1,25},{... | collective-permute-start | bytes 98312 | tf_op jit(solution)/shard_map/ppermute | solution.py:353
  11.9 2.0 %collective-permute-start.5 = (bf16[32,512]{1,0:T(8,128)(2,1)S(1)}, bf16[32,512]{1,0:T(8,128)(2,1)S(1)}, u32[]{:S(2)}, u32[]{:S(2)}) collective-permute-start(bf16[32,512]{1,0:T(8,128)(2,1)S(1)} %collective-permute-done.3.refs_0_), channel_id=1, source_target_pairs={{0,8},{4,12},{8,0},{12,4},{16,24},{20,28},{24,16},{28,20},{1,9},{5... | collective-permute-start | bytes 98312 | tf_op jit(solution)/shard_map/ppermute | solution.py:353
  13.9 0.0 collective-permute-start.7
  13.9 0.0 collective-permute-done.refs_1_
  13.9 3.7 %collective-permute-start.2 = (bf16[32,512]{1,0:T(8,128)(2,1)S(1)}, bf16[32,512]{1,0:T(8,128)(2,1)S(1)}, u32[]{:S(2)}, u32[]{:S(2)}) collective-permute-start(bf16[32,512]{1,0:T(8,128)(2,1)S(1)} %get-tuple-element.49.refs_0_), channel_id=1, source_target_pairs={{0,3},{1,2},{2,1},{3,0},{4,7},{5,6},{6,5},{7,4},{8,11},{9,10},{10,... | collective-permute-start | bytes 98312 | tf_op jit(solution)/shard_map/ppermute | solution.py:349
  17.6 0.0 collective-permute-done.1.refs_2_
  17.6 0.0 collective-permute-start.4
  17.6 0.0 collective-permute-done.9.refs_6_
  17.6 0.5 collective-permute-start.10
  18.1 0.0 collective-permute-done.5.refs_2_
  18.1 0.1 collective-permute-start.6
  18.2 0.0 collective-permute-done.7.refs_4_
  18.2 0.4 collective-permute-start.8
  18.6 1.7 %shard_map.127 = (bf16[512,1024]{1,0:T(8,128)(2,1)S(1)}, bf16[4,128,128]{2,1,0:T(8,128)(2,1)S(1)}, f32[8,128]{1,0:T(8,128)S(1)}) custom-call(bf16[16,32,128]{2,1,0:T(8,128)(2,1)S(1)} %get-tuple-element.50.cot_ref, bf16[1024,128]{1,0:T(8,128)(2,1)S(1)} %get-tuple-element.51.w_ref.refs_3_), custom_call_target="tpu_custom_call" | custom-call | flops 540000000 | bytes 393216 | tf_op jit(solution)/shard_map/pallas_call | solution.py:36
  20.4 0.0 collective-permute-done.2.refs_3_
  20.4 0.4 shard_map.128
  20.8 0.1 collective-permute-start.14
  20.9 0.0 collective-permute-done.4.refs_1_
  20.9 0.0 collective-permute-done.10.refs_7_
  20.9 0.0 collective-permute-done.6.refs_3_
  20.9 0.0 collective-permute-done.8.refs_5_
  20.9 0.5 shard_map.129
  21.4 2.0 %shard_map.130 = (bf16[16,32,128]{2,1,0:T(8,128)(2,1)}, bf16[4,128,128]{2,1,0:T(8,128)(2,1)S(1)}, bf16[4,128,128]{2,1,0:T(8,128)(2,1)S(1)}) custom-call(bf16[128,512]{1,0:T(8,128)(2,1)S(1)} %get-tuple-element.53.refs_0_, bf16[2,128,512]{2,1,0:T(8,128)(2,1)S(1)} %get-tuple-element.55.refs_1_, bf16[4,128,128]{2,1,0:T(8,128)(2,1)S(1)} %get-tuple-element.56.refs_2_, ...), custom_call_target="tpu_custom_call" | custom-call | flops 800000000 | bytes 786944 | tf_op jit(solution)/shard_map/pallas_call | solution.py:36
  23.5 0.4 collective-permute-start.19
  23.9 0.0 collective-permute-done.14.refs_1_
  23.9 0.1 shard_map.131
  24.0 0.6 %collective-permute-start.15 = (bf16[32,512]{1,0:T(8,128)(2,1)S(1)}, bf16[32,512]{1,0:T(8,128)(2,1)S(1)}, u32[]{:S(2)}, u32[]{:S(2)}) collective-permute-start(bf16[32,512]{1,0:T(8,128)(2,1)S(1)} %get-tuple-element.70), channel_id=1, source_target_pairs={{0,8},{4,12},{8,0},{12,4},{16,24},{20,28},{24,16},{28,20},{1,9},{5... | collective-permute-start | bytes 98312 | tf_op jit(solution)/shard_map/ppermute | solution.py:353
  24.6 1.9 %collective-permute-start.16 = (bf16[32,512]{1,0:T(8,128)(2,1)S(1)}, bf16[32,512]{1,0:T(8,128)(2,1)S(1)}, u32[]{:S(2)}, u32[]{:S(2)}) collective-permute-start(bf16[32,512]{1,0:T(8,128)(2,1)S(1)} %get-tuple-element.71), channel_id=1, source_target_pairs={{0,16},{4,20},{8,24},{12,28},{16,0},{20,4},{24,8},{28,12},{1,17},{... | collective-permute-start | bytes 98312 | tf_op jit(solution)/shard_map/ppermute | solution.py:353
  26.5 1.0 %collective-permute-start.17 = (bf16[32,512]{1,0:T(8,128)(2,1)S(1)}, bf16[32,512]{1,0:T(8,128)(2,1)S(1)}, u32[]{:S(2)}, u32[]{:S(2)}) collective-permute-start(bf16[32,512]{1,0:T(8,128)(2,1)S(1)} %get-tuple-element.72), channel_id=1, source_target_pairs={{0,24},{4,28},{8,16},{12,20},{16,8},{20,12},{24,0},{28,4},{1,25},{... | collective-permute-start | bytes 98312 | tf_op jit(solution)/shard_map/ppermute | solution.py:353
  27.5 0.0 collective-permute-start.11
  27.5 0.4 collective-permute-done.15.refs_1_
  28.0 3.0 %collective-permute-start.12 = (bf16[32,512]{1,0:T(8,128)(2,1)S(1)}, bf16[32,512]{1,0:T(8,128)(2,1)S(1)}, u32[]{:S(2)}, u32[]{:S(2)}) collective-permute-start(bf16[32,512]{1,0:T(8,128)(2,1)S(1)} %get-tuple-element.65), channel_id=1, source_target_pairs={{0,2},{1,3},{2,0},{3,1},{4,6},{5,7},{6,4},{7,5},{8,10},{9,11},{10,... | collective-permute-start | bytes 98312 | tf_op jit(solution)/shard_map/ppermute | solution.py:349
  31.0 0.0 collective-permute-done.16.refs_2_
  31.0 0.9 %collective-permute-start.13 = (bf16[32,512]{1,0:T(8,128)(2,1)S(1)}, bf16[32,512]{1,0:T(8,128)(2,1)S(1)}, u32[]{:S(2)}, u32[]{:S(2)}) collective-permute-start(bf16[32,512]{1,0:T(8,128)(2,1)S(1)} %get-tuple-element.66), channel_id=1, source_target_pairs={{0,3},{1,2},{2,1},{3,0},{4,7},{5,6},{6,5},{7,4},{8,11},{9,10},{10,... | collective-permute-start | bytes 98312 | tf_op jit(solution)/shard_map/ppermute | solution.py:349
  31.9 0.0 collective-permute-done.17.refs_3_
  32.0 3.0 %collective-permute-start.18 = (bf16[32,512]{1,0:T(8,128)(2,1)S(1)}, bf16[32,512]{1,0:T(8,128)(2,1)S(1)}, u32[]{:S(2)}, u32[]{:S(2)}) collective-permute-start(bf16[32,512]{1,0:T(8,128)(2,1)S(1)} %shard_map.132), channel_id=1, source_target_pairs={{24,0},{16,1},{8,2},{0,3},{28,4},{20,5},{12,6},{4,7},{25,8},{17,9}... | collective-permute-start | bytes 98312 | tf_op jit(solution)/shard_map/ppermute | solution.py:419
  34.9 0.0 collective-permute-done.11.refs_1_
  34.9 0.0 collective-permute-done.12.refs_2_
  34.9 1.8 %collective-permute-done.13.refs_3_ = bf16[32,512]{1,0:T(8,128)(2,1)S(1)} collective-permute-done((bf16[32,512]{1,0:T(8,128)(2,1)S(1)}, bf16[32,512]{1,0:T(8,128)(2,1)S(1)}, u32[]{:S(2)}, u32[]{:S(2)}) %collective-permute-start.13) | collective-permute-done | bytes 32800 | tf_op jit(solution)/shard_map/ppermute | solution.py:349
  36.7 0.2 collective-permute-done.18.refs_4_.right_ref
  37.0 0.8 %shard_map.133 = (bf16[32,512]{1,0:T(8,128)(2,1)S(1)}, bf16[144,128]{1,0:T(8,128)(2,1)S(1)}) custom-call(bf16[32,512]{1,0:T(8,128)(2,1)S(1)} %get-tuple-element.63.refs_0_, bf16[32,512]{1,0:T(8,128)(2,1)S(1)} %collective-permute-done.11.refs_1_, bf16[32,512]{1,0:T(8,128)(2,1)S(1)} %collective-permute-done.12.refs_2_, ...), custom_call_target="tpu_custom_call" | custom-call | flops 1 | bytes 430080 | tf_op jit(solution)/shard_map/pallas_call | solution.py:36
  37.7 0.1 collective-permute-start.20
  37.8 0.0 collective-permute-done.19.refs_1_
  37.8 1.2 %collective-permute-done.20.refs_3_ = bf16[144,128]{1,0:T(8,128)(2,1)S(1)} collective-permute-done((bf16[144,128]{1,0:T(8,128)(2,1)S(1)}, bf16[144,128]{1,0:T(8,128)(2,1)S(1)}, u32[]{:S(2)}, u32[]{:S(2)}) %collective-permute-start.20) | collective-permute-done | bytes 36896 | tf_op jit(solution)/shard_map/ppermute | solution.py:357
  39.0 0.1 shard_map.135
  39.1 1.0 %collective-permute-start.21 = (bf16[272,128]{1,0:T(8,128)(2,1)S(1)}, bf16[272,128]{1,0:T(8,128)(2,1)S(1)}, u32[]{:S(2)}, u32[]{:S(2)}) collective-permute-start(bf16[272,128]{1,0:T(8,128)(2,1)S(1)} %get-tuple-element.79), channel_id=1, source_target_pairs={{0,8},{4,12},{8,0},{12,4},{16,24},{20,28},{24,16},{28,20},{1,9},{5... | collective-permute-start | bytes 208904 | tf_op jit(solution)/shard_map/ppermute | solution.py:353
  40.1 3.0 %collective-permute-start.22 = (bf16[272,128]{1,0:T(8,128)(2,1)S(1)}, bf16[272,128]{1,0:T(8,128)(2,1)S(1)}, u32[]{:S(2)}, u32[]{:S(2)}) collective-permute-start(bf16[272,128]{1,0:T(8,128)(2,1)S(1)} %get-tuple-element.80), channel_id=1, source_target_pairs={{0,16},{4,20},{8,24},{12,28},{16,0},{20,4},{24,8},{28,12},{1,17},{... | collective-permute-start | bytes 208904 | tf_op jit(solution)/shard_map/ppermute | solution.py:353
  43.1 0.3 collective-permute-start.23
  43.4 0.0 collective-permute-done.21.refs_1_
  43.4 2.8 %collective-permute-done.22.refs_2_ = bf16[272,128]{1,0:T(8,128)(2,1)S(1)} collective-permute-done((bf16[272,128]{1,0:T(8,128)(2,1)S(1)}, bf16[272,128]{1,0:T(8,128)(2,1)S(1)}, u32[]{:S(2)}, u32[]{:S(2)}) %collective-permute-start.22) | collective-permute-done | bytes 69664 | tf_op jit(solution)/shard_map/ppermute | solution.py:353
  46.3 2.0 %collective-permute-done.23.refs_3_ = bf16[272,128]{1,0:T(8,128)(2,1)S(1)} collective-permute-done((bf16[272,128]{1,0:T(8,128)(2,1)S(1)}, bf16[272,128]{1,0:T(8,128)(2,1)S(1)}, u32[]{:S(2)}, u32[]{:S(2)}) %collective-permute-start.23) | collective-permute-done | bytes 69664 | tf_op jit(solution)/shard_map/ppermute | solution.py:353
  48.3 0.1 shard_map.136
  48.4 0.3 collective-permute-start.24
  48.7 1.8 %collective-permute-start.25 = (bf16[176,128]{1,0:T(8,128)(2,1)S(1)}, bf16[176,128]{1,0:T(8,128)(2,1)S(1)}, u32[]{:S(2)}, u32[]{:S(2)}) collective-permute-start(bf16[176,128]{1,0:T(8,128)(2,1)S(1)} %get-tuple-element.84), channel_id=1, source_target_pairs={{0,2},{1,3},{2,0},{3,1},{4,6},{5,7},{6,4},{7,5},{8,10},{9,11},{10,... | collective-permute-start | bytes 135176 | tf_op jit(solution)/shard_map/ppermute | solution.py:349
  50.5 2.4 %collective-permute-start.26 = (bf16[176,128]{1,0:T(8,128)(2,1)S(1)}, bf16[176,128]{1,0:T(8,128)(2,1)S(1)}, u32[]{:S(2)}, u32[]{:S(2)}) collective-permute-start(bf16[176,128]{1,0:T(8,128)(2,1)S(1)} %get-tuple-element.85), channel_id=1, source_target_pairs={{0,3},{1,2},{2,1},{3,0},{4,7},{5,6},{6,5},{7,4},{8,11},{9,10},{10,... | collective-permute-start | bytes 135176 | tf_op jit(solution)/shard_map/ppermute | solution.py:349
  52.8 1.6 %shard_map.134 = bf16[32,16,256]{2,1,0:T(8,128)(2,1)} custom-call(bf16[32,16,256]{2,1,0:T(8,128)(2,1)S(1)} %get-tuple-element.59.refs_5_.x_ref, f32[1,256]{1,0:T(1,128)S(1)} %get-tuple-element.60.gain_ref.refs_4_, bf16[32,256]{1,0:T(8,128)(2,1)S(1)} %get-tuple-element.61.lw_ref.refs_5_, bf16[32,256]{1,0:T(8,128)(2,1)S(1)} %get-tuple-element.62.rw_ref.refs_6_, ...), custom_call_target="tpu_custom_call" | custom-call | flops 1 | bytes 361472 | tf_op jit(solution)/shard_map/pallas_call | solution.py:36
  54.5 0.0 collective-permute-done.24.refs_1_
  54.5 1.8 %collective-permute-done.26.refs_3_ = bf16[176,128]{1,0:T(8,128)(2,1)S(1)} collective-permute-done((bf16[176,128]{1,0:T(8,128)(2,1)S(1)}, bf16[176,128]{1,0:T(8,128)(2,1)S(1)}, u32[]{:S(2)}, u32[]{:S(2)}) %collective-permute-start.26) | collective-permute-done | bytes 45088 | tf_op jit(solution)/shard_map/ppermute | solution.py:349
  56.3 0.7 %shard_map.137 = (f32[32,256]{1,0:T(8,128)}, f32[32,256]{1,0:T(8,128)}, f32[32,128]{1,0:T(8,128)}, f32[1,256]{1,0:T(1,128)}, f32[1,128]{1,0:T(1,128)}) custom-call(bf16[176,128]{1,0:T(8,128)(2,1)S(1)} %get-tuple-element.82.refs_0_, bf16[176,128]{1,0:T(8,128)(2,1)S(1)} %collective-permute-done.24.refs_1_, ...), custom_call_target="tpu_custom_call" | custom-call | flops 1 | bytes 214016 | tf_op jit(solution)/shard_map/pallas_call | solution.py:36
  (2 shorter events, 0.0 us)
Async XLA Ops:
  2.7 7.1 %collective-permute-start.3 = (bf16[32,512]{1,0:T(8,128)(2,1)S(1)}, bf16[32,512]{1,0:T(8,128)(2,1)S(1)}, u32[]{:S(2)}, u32[]{:S(2)}) collective-permute-start(bf16[32,512]{1,0:T(8,128)(2,1)S(1)} %get-tuple-element.54), channel_id=1, source_target_pairs={{0,24},{1,16},{2,8},{3,0},{4,28},{5,20},{6,12},{7,4},{8,25},{9,17}... | collective-permute-start | bytes 98312 | tf_op jit(solution)/shard_map/ppermute | solution.py:380
  6.7 7.2 %collective-permute-start = (bf16[32,512]{1,0:T(8,128)(2,1)S(1)}, bf16[32,512]{1,0:T(8,128)(2,1)S(1)}, u32[]{:S(2)}, u32[]{:S(2)}) collective-permute-start(bf16[32,512]{1,0:T(8,128)(2,1)S(1)} %get-tuple-element.49.refs_0_), channel_id=1, source_target_pairs={{0,1},{1,0},{2,3},{3,2},{4,5},{5,4},{6,7},{7,6},{8,9},{9,8},{10,11... | collective-permute-start | bytes 98312 | tf_op jit(solution)/shard_map/ppermute | solution.py:349
  7.2 10.4 %collective-permute-start.1 = (bf16[32,512]{1,0:T(8,128)(2,1)S(1)}, bf16[32,512]{1,0:T(8,128)(2,1)S(1)}, u32[]{:S(2)}, u32[]{:S(2)}) collective-permute-start(bf16[32,512]{1,0:T(8,128)(2,1)S(1)} %get-tuple-element.49.refs_0_), channel_id=1, source_target_pairs={{0,2},{1,3},{2,0},{3,1},{4,6},{5,7},{6,4},{7,5},{8,10},{9,11},{10,... | collective-permute-start | bytes 98312 | tf_op jit(solution)/shard_map/ppermute | solution.py:349
  9.8 7.8 %collective-permute-start.9 = (bf16[32,512]{1,0:T(8,128)(2,1)S(1)}, bf16[32,512]{1,0:T(8,128)(2,1)S(1)}, u32[]{:S(2)}, u32[]{:S(2)}) collective-permute-start(bf16[32,512]{1,0:T(8,128)(2,1)S(1)} %collective-permute-done.3.refs_0_), channel_id=1, source_target_pairs={{0,24},{4,28},{8,16},{12,20},{16,8},{20,12},{24,0},{28,4},{1,25},{... | collective-permute-start | bytes 98312 | tf_op jit(solution)/shard_map/ppermute | solution.py:353
  11.9 6.2 %collective-permute-start.5 = (bf16[32,512]{1,0:T(8,128)(2,1)S(1)}, bf16[32,512]{1,0:T(8,128)(2,1)S(1)}, u32[]{:S(2)}, u32[]{:S(2)}) collective-permute-start(bf16[32,512]{1,0:T(8,128)(2,1)S(1)} %collective-permute-done.3.refs_0_), channel_id=1, source_target_pairs={{0,8},{4,12},{8,0},{12,4},{16,24},{20,28},{24,16},{28,20},{1,9},{5... | collective-permute-start | bytes 98312 | tf_op jit(solution)/shard_map/ppermute | solution.py:353
  13.9 4.3 %collective-permute-start.7 = (bf16[32,512]{1,0:T(8,128)(2,1)S(1)}, bf16[32,512]{1,0:T(8,128)(2,1)S(1)}, u32[]{:S(2)}, u32[]{:S(2)}) collective-permute-start(bf16[32,512]{1,0:T(8,128)(2,1)S(1)} %collective-permute-done.3.refs_0_), channel_id=1, source_target_pairs={{0,16},{4,20},{8,24},{12,28},{16,0},{20,4},{24,8},{28,12},{1,17},{... | collective-permute-start | bytes 98312 | tf_op jit(solution)/shard_map/ppermute | solution.py:353
  13.9 6.5 %collective-permute-start.2 = (bf16[32,512]{1,0:T(8,128)(2,1)S(1)}, bf16[32,512]{1,0:T(8,128)(2,1)S(1)}, u32[]{:S(2)}, u32[]{:S(2)}) collective-permute-start(bf16[32,512]{1,0:T(8,128)(2,1)S(1)} %get-tuple-element.49.refs_0_), channel_id=1, source_target_pairs={{0,3},{1,2},{2,1},{3,0},{4,7},{5,6},{6,5},{7,4},{8,11},{9,10},{10,... | collective-permute-start | bytes 98312 | tf_op jit(solution)/shard_map/ppermute | solution.py:349
  17.6 3.3 %collective-permute-start.4 = (bf16[32,512]{1,0:T(8,128)(2,1)S(1)}, bf16[32,512]{1,0:T(8,128)(2,1)S(1)}, u32[]{:S(2)}, u32[]{:S(2)}) collective-permute-start(bf16[32,512]{1,0:T(8,128)(2,1)S(1)} %collective-permute-done.3.refs_0_), channel_id=1, source_target_pairs={{0,4},{4,0},{8,12},{12,8},{16,20},{20,16},{24,28},{28,24},{1,5},{5... | collective-permute-start | bytes 98312 | tf_op jit(solution)/shard_map/ppermute | solution.py:357
  17.6 3.3 %collective-permute-start.10 = (bf16[32,512]{1,0:T(8,128)(2,1)S(1)}, bf16[32,512]{1,0:T(8,128)(2,1)S(1)}, u32[]{:S(2)}, u32[]{:S(2)}) collective-permute-start(bf16[32,512]{1,0:T(8,128)(2,1)S(1)} %collective-permute-done.9.refs_6_), channel_id=1, source_target_pairs={{0,4},{4,0},{8,12},{12,8},{16,20},{20,16},{24,28},{28,24},{1,5},{5... | collective-permute-start | bytes 98312 | tf_op jit(solution)/shard_map/ppermute | solution.py:357
  18.1 2.8 %collective-permute-start.6 = (bf16[32,512]{1,0:T(8,128)(2,1)S(1)}, bf16[32,512]{1,0:T(8,128)(2,1)S(1)}, u32[]{:S(2)}, u32[]{:S(2)}) collective-permute-start(bf16[32,512]{1,0:T(8,128)(2,1)S(1)} %collective-permute-done.5.refs_2_), channel_id=1, source_target_pairs={{0,4},{4,0},{8,12},{12,8},{16,20},{20,16},{24,28},{28,24},{1,5},{5... | collective-permute-start | bytes 98312 | tf_op jit(solution)/shard_map/ppermute | solution.py:357
  18.2 2.7 %collective-permute-start.8 = (bf16[32,512]{1,0:T(8,128)(2,1)S(1)}, bf16[32,512]{1,0:T(8,128)(2,1)S(1)}, u32[]{:S(2)}, u32[]{:S(2)}) collective-permute-start(bf16[32,512]{1,0:T(8,128)(2,1)S(1)} %collective-permute-done.7.refs_4_), channel_id=1, source_target_pairs={{0,4},{4,0},{8,12},{12,8},{16,20},{20,16},{24,28},{28,24},{1,5},{5... | collective-permute-start | bytes 98312 | tf_op jit(solution)/shard_map/ppermute | solution.py:357
  20.8 3.2 %collective-permute-start.14 = (bf16[128,512]{1,0:T(8,128)(2,1)S(1)}, bf16[128,512]{1,0:T(8,128)(2,1)S(1)}, u32[]{:S(2)}, u32[]{:S(2)}) collective-permute-start(bf16[128,512]{1,0:T(8,128)(2,1)S(1)} %get-tuple-element.68), channel_id=1, source_target_pairs={{0,4},{4,0},{8,12},{12,8},{16,20},{20,16},{24,28},{28,24},{1,5},{5... | collective-permute-start | bytes 393224 | tf_op jit(solution)/shard_map/ppermute | solution.py:357
  23.5 14.3 %collective-permute-start.19 = (bf16[4,128,128]{2,1,0:T(8,128)(2,1)S(1)}, bf16[4,128,128]{2,1,0:T(8,128)(2,1)S(1)}, u32[]{:S(2)}, u32[]{:S(2)}) collective-permute-start(bf16[4,128,128]{2,1,0:T(8,128)(2,1)S(1)} %get-tuple-element.76), channel_id=1, source_target_pairs={{0,4},{4,0},{8,12},{12,8},{16,20},{20,16},{24,28},{28,24},{1,5},{5... | collective-permute-start | bytes 393224 | tf_op jit(solution)/shard_map/ppermute | solution.py:357
  24.0 4.0 %collective-permute-start.15 = (bf16[32,512]{1,0:T(8,128)(2,1)S(1)}, bf16[32,512]{1,0:T(8,128)(2,1)S(1)}, u32[]{:S(2)}, u32[]{:S(2)}) collective-permute-start(bf16[32,512]{1,0:T(8,128)(2,1)S(1)} %get-tuple-element.70), channel_id=1, source_target_pairs={{0,8},{4,12},{8,0},{12,4},{16,24},{20,28},{24,16},{28,20},{1,9},{5... | collective-permute-start | bytes 98312 | tf_op jit(solution)/shard_map/ppermute | solution.py:353
  24.6 6.4 %collective-permute-start.16 = (bf16[32,512]{1,0:T(8,128)(2,1)S(1)}, bf16[32,512]{1,0:T(8,128)(2,1)S(1)}, u32[]{:S(2)}, u32[]{:S(2)}) collective-permute-start(bf16[32,512]{1,0:T(8,128)(2,1)S(1)} %get-tuple-element.71), channel_id=1, source_target_pairs={{0,16},{4,20},{8,24},{12,28},{16,0},{20,4},{24,8},{28,12},{1,17},{... | collective-permute-start | bytes 98312 | tf_op jit(solution)/shard_map/ppermute | solution.py:353
  26.5 5.4 %collective-permute-start.17 = (bf16[32,512]{1,0:T(8,128)(2,1)S(1)}, bf16[32,512]{1,0:T(8,128)(2,1)S(1)}, u32[]{:S(2)}, u32[]{:S(2)}) collective-permute-start(bf16[32,512]{1,0:T(8,128)(2,1)S(1)} %get-tuple-element.72), channel_id=1, source_target_pairs={{0,24},{4,28},{8,16},{12,20},{16,8},{20,12},{24,0},{28,4},{1,25},{... | collective-permute-start | bytes 98312 | tf_op jit(solution)/shard_map/ppermute | solution.py:353
  27.5 7.4 %collective-permute-start.11 = (bf16[32,512]{1,0:T(8,128)(2,1)S(1)}, bf16[32,512]{1,0:T(8,128)(2,1)S(1)}, u32[]{:S(2)}, u32[]{:S(2)}) collective-permute-start(bf16[32,512]{1,0:T(8,128)(2,1)S(1)} %get-tuple-element.64), channel_id=1, source_target_pairs={{0,1},{1,0},{2,3},{3,2},{4,5},{5,4},{6,7},{7,6},{8,9},{9,8},{10,11... | collective-permute-start | bytes 98312 | tf_op jit(solution)/shard_map/ppermute | solution.py:349
  28.0 7.0 %collective-permute-start.12 = (bf16[32,512]{1,0:T(8,128)(2,1)S(1)}, bf16[32,512]{1,0:T(8,128)(2,1)S(1)}, u32[]{:S(2)}, u32[]{:S(2)}) collective-permute-start(bf16[32,512]{1,0:T(8,128)(2,1)S(1)} %get-tuple-element.65), channel_id=1, source_target_pairs={{0,2},{1,3},{2,0},{3,1},{4,6},{5,7},{6,4},{7,5},{8,10},{9,11},{10,... | collective-permute-start | bytes 98312 | tf_op jit(solution)/shard_map/ppermute | solution.py:349
  31.0 5.7 %collective-permute-start.13 = (bf16[32,512]{1,0:T(8,128)(2,1)S(1)}, bf16[32,512]{1,0:T(8,128)(2,1)S(1)}, u32[]{:S(2)}, u32[]{:S(2)}) collective-permute-start(bf16[32,512]{1,0:T(8,128)(2,1)S(1)} %get-tuple-element.66), channel_id=1, source_target_pairs={{0,3},{1,2},{2,1},{3,0},{4,7},{5,6},{6,5},{7,4},{8,11},{9,10},{10,... | collective-permute-start | bytes 98312 | tf_op jit(solution)/shard_map/ppermute | solution.py:349
  32.0 5.0 %collective-permute-start.18 = (bf16[32,512]{1,0:T(8,128)(2,1)S(1)}, bf16[32,512]{1,0:T(8,128)(2,1)S(1)}, u32[]{:S(2)}, u32[]{:S(2)}) collective-permute-start(bf16[32,512]{1,0:T(8,128)(2,1)S(1)} %shard_map.132), channel_id=1, source_target_pairs={{24,0},{16,1},{8,2},{0,3},{28,4},{20,5},{12,6},{4,7},{25,8},{17,9}... | collective-permute-start | bytes 98312 | tf_op jit(solution)/shard_map/ppermute | solution.py:419
  37.7 1.3 %collective-permute-start.20 = (bf16[144,128]{1,0:T(8,128)(2,1)S(1)}, bf16[144,128]{1,0:T(8,128)(2,1)S(1)}, u32[]{:S(2)}, u32[]{:S(2)}) collective-permute-start(bf16[144,128]{1,0:T(8,128)(2,1)S(1)} %get-tuple-element.77.refs_2_), channel_id=1, source_target_pairs={{0,4},{4,0},{8,12},{12,8},{16,20},{20,16},{24,28},{28,24},{1,5},{5... | collective-permute-start | bytes 110600 | tf_op jit(solution)/shard_map/ppermute | solution.py:357
  39.1 4.4 %collective-permute-start.21 = (bf16[272,128]{1,0:T(8,128)(2,1)S(1)}, bf16[272,128]{1,0:T(8,128)(2,1)S(1)}, u32[]{:S(2)}, u32[]{:S(2)}) collective-permute-start(bf16[272,128]{1,0:T(8,128)(2,1)S(1)} %get-tuple-element.79), channel_id=1, source_target_pairs={{0,8},{4,12},{8,0},{12,4},{16,24},{20,28},{24,16},{28,20},{1,9},{5... | collective-permute-start | bytes 208904 | tf_op jit(solution)/shard_map/ppermute | solution.py:353
  40.1 6.2 %collective-permute-start.22 = (bf16[272,128]{1,0:T(8,128)(2,1)S(1)}, bf16[272,128]{1,0:T(8,128)(2,1)S(1)}, u32[]{:S(2)}, u32[]{:S(2)}) collective-permute-start(bf16[272,128]{1,0:T(8,128)(2,1)S(1)} %get-tuple-element.80), channel_id=1, source_target_pairs={{0,16},{4,20},{8,24},{12,28},{16,0},{20,4},{24,8},{28,12},{1,17},{... | collective-permute-start | bytes 208904 | tf_op jit(solution)/shard_map/ppermute | solution.py:353
  43.1 5.2 %collective-permute-start.23 = (bf16[272,128]{1,0:T(8,128)(2,1)S(1)}, bf16[272,128]{1,0:T(8,128)(2,1)S(1)}, u32[]{:S(2)}, u32[]{:S(2)}) collective-permute-start(bf16[272,128]{1,0:T(8,128)(2,1)S(1)} %get-tuple-element.81), channel_id=1, source_target_pairs={{0,24},{4,28},{8,16},{12,20},{16,8},{20,12},{24,0},{28,4},{1,25},{... | collective-permute-start | bytes 208904 | tf_op jit(solution)/shard_map/ppermute | solution.py:353
  48.4 6.1 %collective-permute-start.24 = (bf16[176,128]{1,0:T(8,128)(2,1)S(1)}, bf16[176,128]{1,0:T(8,128)(2,1)S(1)}, u32[]{:S(2)}, u32[]{:S(2)}) collective-permute-start(bf16[176,128]{1,0:T(8,128)(2,1)S(1)} %get-tuple-element.83), channel_id=1, source_target_pairs={{0,1},{1,0},{2,3},{3,2},{4,5},{5,4},{6,7},{7,6},{8,9},{9,8},{10,11... | collective-permute-start | bytes 135176 | tf_op jit(solution)/shard_map/ppermute | solution.py:349
  48.7 5.8 %collective-permute-start.25 = (bf16[176,128]{1,0:T(8,128)(2,1)S(1)}, bf16[176,128]{1,0:T(8,128)(2,1)S(1)}, u32[]{:S(2)}, u32[]{:S(2)}) collective-permute-start(bf16[176,128]{1,0:T(8,128)(2,1)S(1)} %get-tuple-element.84), channel_id=1, source_target_pairs={{0,2},{1,3},{2,0},{3,1},{4,6},{5,7},{6,4},{7,5},{8,10},{9,11},{10,... | collective-permute-start | bytes 135176 | tf_op jit(solution)/shard_map/ppermute | solution.py:349
  50.5 5.8 %collective-permute-start.26 = (bf16[176,128]{1,0:T(8,128)(2,1)S(1)}, bf16[176,128]{1,0:T(8,128)(2,1)S(1)}, u32[]{:S(2)}, u32[]{:S(2)}) collective-permute-start(bf16[176,128]{1,0:T(8,128)(2,1)S(1)} %get-tuple-element.85), channel_id=1, source_target_pairs={{0,3},{1,2},{2,1},{3,0},{4,7},{5,6},{6,5},{7,4},{8,11},{9,10},{10,... | collective-permute-start | bytes 135176 | tf_op jit(solution)/shard_map/ppermute | solution.py:349

commit v3 on v2

--- a/solution.py
+++ b/solution.py
@@ -66,7 +66,7 @@
     size = residues * chans
     source = lax.broadcasted_iota(jnp.int32, (size, size), 0)
     target = lax.broadcasted_iota(jnp.int32, (size, size), 1)
-    place = (source % chans) * residues + source // chans
+    place = (source & (chans - 1)) * residues + (source >> (chans.bit_length() - 1))
     return jnp.where(place == target, 1.0, 0.0).astype(BF16)
 
 
@@ -80,75 +80,63 @@
     return copies
 
 
+def stacked(value, residues, chans):
+    return jnp.concatenate(
+        [value[:, i * chans : (i + 1) * chans] for i in range(residues)], axis=0
+    )
+
+
+def unstacked(value, residues, seqs):
+    return jnp.concatenate(
+        [value[i * seqs : (i + 1) * seqs] for i in range(residues)], axis=1
+    )
+
+
 def project_kernel(chans, *refs):
-    count = (len(refs) - 4) // 2
+    count = (len(refs) - 6) // 2
     sources, targets = refs[:count], refs[count : 2 * count]
-    left_ref, right_ref, flat, sems = refs[2 * count :]
+    left_ref, right_ref, normed_ref, order_ref, flat, sems = refs[2 * count :]
     copies = fetch(zip(sources, targets), sems)
+    order_ref[...] = channel_first(sources[0].shape[1], chans)
     for copy in copies[:4]:
         copy.wait()
     x_in, gain_in = targets[:2]
     seqs, residues, _ = x_in.shape
     normed, _ = normalize(jnp.concatenate(by_residue(x_in, flat), axis=0))
     ln_out = normed * gain_in[...]
-    pack = LANES // chans
-    places = []
-    for weight_in in targets[2:4]:
-        weight = weight_in[...]
-        zero = jnp.zeros_like(weight)
-        places += [
-            jnp.concatenate([weight if k == m else zero for m in range(pack)], axis=1)
-            for k in range(pack)
-        ]
-    weights = jnp.concatenate(places, axis=0)
-    left, right = [], []
-    for g in range(residues // pack):
-        piece = jnp.concatenate(
-            [ln_out[(g * pack + k) * seqs : (g * pack + k + 1) * seqs] for k in range(pack)], axis=1
-        )
-        both = product(piece.astype(BF16), weights, ((1,), (1,)))
-        left.append(both[:, :LANES])
-        right.append(both[:, LANES:])
-    right_ref[...] = jnp.concatenate(right, axis=1).astype(BF16)
-    left = jnp.concatenate(left, axis=1).astype(BF16)
-    left_ref[...] = product(left, channel_first(residues, chans)).astype(BF16)
+    normed_ref[...] = normed.astype(BF16)
+    weights = jnp.concatenate([weight[...] for weight in targets[2:4]], axis=0)
+    both = product(ln_out.astype(BF16), weights, ((1,), (1,)))
+    right_ref[...] = unstacked(both[:, chans:], residues, seqs).astype(BF16)
+    left = unstacked(both[:, :chans], residues, seqs).astype(BF16)
+    left_ref[...] = product(left, order_ref[...]).astype(BF16)
     for copy in copies[4:]:
         copy.wait()
 
 
-def spread_weight(w_ref, spread, chans):
-    pack = LANES // chans
-    pair_w = w_ref.shape[1]
-    spread[...] = jnp.zeros_like(spread)
-    for c in range(chans):
-        block = w_ref[c * chans : (c + 1) * chans, :]
-        for k in range(pack):
-            row = c * LANES + k * chans
-            spread[row : row + chans, k * pair_w : (k + 1) * pair_w] = block
-
-
-def grad_kernel(chans, cot_ref, w_ref, og_ref, cotk_ref, bias_ref, flat, spread):
+def pieces(block, chans):
+    return [block[:, k * chans : (k + 1) * chans] for k in range(block.shape[1] // chans)]
+
+
+def grad_kernel(chans, cot_ref, w_ref, og_ref, cotk_ref, bias_ref, flat):
     residues, seconds, pair_w = cot_ref.shape
     pack = LANES // chans
     groups = seconds // pack
+    size = groups * residues
     cot = wide(cot_ref).reshape(residues * seconds, pair_w)
     flat[...] = cot
     bias_ref[...] = jnp.broadcast_to(jnp.sum(cot, axis=0, keepdims=True), bias_ref.shape)
-    spread_weight(w_ref, spread, chans)
     for k in range(pack):
         rows = [flat[pl.ds(g * pack + k, residues, stride=seconds), :] for g in range(groups)]
-        cotk_ref[k] = jnp.concatenate(rows, axis=0).astype(BF16)
-    cot_wide = jnp.concatenate([cotk_ref[k] for k in range(pack)], axis=1)
-    chunk = 8
-    for first in range(0, chans, chunk):
-        part = spread[first * LANES : (first + chunk) * LANES, :]
-        out = product(cot_wide, part, ((1,), (1,))).astype(BF16)
-        for c in range(chunk):
-            for g in range(groups):
-                row = (first + c) * residues
-                og_ref[row : row + residues, g * LANES : (g + 1) * LANES] = out[
-                    g * residues : (g + 1) * residues, c * LANES : (c + 1) * LANES
-                ]
+        cotk_ref[k * size : (k + 1) * size] = jnp.concatenate(rows, axis=0).astype(BF16)
+    out = product(cotk_ref[...], w_ref[...], ((1,), (1,))).astype(BF16)
+    parts = [pieces(out[k * size : (k + 1) * size], chans) for k in range(pack)]
+    for c in range(chans):
+        block = jnp.concatenate([parts[k][c] for k in range(pack)], axis=1)
+        for g in range(groups):
+            og_ref[c * residues : (c + 1) * residues, g * LANES : (g + 1) * LANES] = block[
+                g * residues : (g + 1) * residues
+            ]
 
 
 def places(ratio):
@@ -189,6 +177,17 @@
     for k in range(cols):
         place = pl.ds(pl.multiple_of((z ^ k) * seqs, seqs), seqs)
         outs[k][...] = sums[place, :].astype(BF16)
+
+
+def spread_weight(w_ref, spread, chans):
+    pack = LANES // chans
+    pair_w = w_ref.shape[1]
+    spread[...] = jnp.zeros_like(spread)
+    for c in range(chans):
+        block = w_ref[c * chans : (c + 1) * chans, :]
+        for k in range(pack):
+            row = c * LANES + k * chans
+            spread[row : row + chans, k * pair_w : (k + 1) * pair_w] = block
 
 
 def forward_kernel(chans, ratio, *refs):
@@ -224,8 +223,7 @@
             turned[c * chans : (c + 1) * chans, k * size : (k + 1) * size] = block[
                 k * chans : (k + 1) * chans
             ]
-    cot = jnp.concatenate([cotk_ref[k] for k in range(pack)], axis=0)
-    out = product(turned[...], cot)
+    out = product(turned[...], cotk_ref[...])
     count, height = proj_out[0].shape[:2]
     proj[...] = out.reshape(count, ratio, height, pair_w)
     for e in range(ratio):
@@ -233,25 +231,20 @@
             proj_out[e][q] = proj[q, h ^ e].astype(BF16)
 
 
-def stacked(value, residues, chans):
-    return jnp.concatenate(
-        [value[:, i * chans : (i + 1) * chans] for i in range(residues)], axis=0
-    )
-
-
 def moment_kernel(cols, chans, *refs):
-    left_in, (right_ref, x_ref, bias_ref, left_ref, stat_ref, flat) = refs[:cols], refs[cols:]
-    residues, width = x_ref.shape[1:]
-    normed, _ = normalize(jnp.concatenate(by_residue(x_ref, flat), axis=0))
+    left_in, (right_ref, normed_ref, order_ref, bias_ref, left_ref, stat_ref) = (
+        refs[:cols],
+        refs[cols:],
+    )
+    residues, width = right_ref.shape[1] // chans, normed_ref.shape[1]
     left = tree([wide(r) for r in left_in]).astype(BF16)
-    left = product(left, channel_first(residues, chans), ((1,), (1,)))
+    left = product(left, order_ref[...], ((1,), (1,)))
     left_ref[...] = left.astype(BF16)
     both = [stacked(value, residues, chans) for value in (left, wide(right_ref))]
     both = jnp.concatenate(both, axis=1).astype(BF16)
-    moment = product(both, normed.astype(BF16), ((0,), (0,)))
+    moment = product(both, normed_ref[...], ((0,), (0,)))
     halves = [moment[:, k * LANES : (k + 1) * LANES] for k in range(width // LANES)]
-    bias = jnp.concatenate([bias_ref[...]] * 2, axis=0)
-    stat_ref[...] = jnp.concatenate(halves + [bias], axis=0).astype(BF16)
+    stat_ref[...] = jnp.concatenate(halves + [bias_ref[...]], axis=0).astype(BF16)
 
 
 def sum_kernel(*refs):
@@ -367,7 +360,9 @@
     outs = call(
         functools.partial(project_kernel, chans),
         sources,
-        [(a.shape, a.dtype) for a in sources] + [((seqs, wide_proj), BF16)] * 2,
+        [(a.shape, a.dtype) for a in sources]
+        + [((seqs, wide_proj), BF16)] * 2
+        + [((residues * seqs, width), BF16), ((wide_proj, wide_proj), BF16)],
         [
             pltpu.VMEM((width // LANES, seqs * residues, LANES), F32),
             pltpu.SemaphoreType.DMA((len(sources),)),
@@ -375,8 +370,8 @@
         flops=40_000_000,
         far=len(sources),
     )
-    x, gain_row, left_t, right_t, cot, out_w, bias_row = outs[:-2]
-    left_own, right_own = outs[-2:]
+    x, gain_row, left_t, right_t, cot, out_w, bias_row = outs[: len(sources)]
+    left_own, right_own, normed, order = outs[len(sources) :]
     right_own = lax.ppermute(right_own, ("row", "col"), pairs)
     left_in = cols_of([left_own] * cols)
     og, cotk, bias_part = call(
@@ -384,13 +379,10 @@
         (cot, out_w),
         [
             ((chans * residues, wide_pair), BF16),
-            ((pack, groups * residues, pair_w), BF16),
+            ((pack * groups * residues, pair_w), BF16),
             ((8, pair_w), F32),
         ],
-        [
-            pltpu.VMEM((residues * seconds, pair_w), F32),
-            pltpu.VMEM((chans * LANES, pack * pair_w), BF16),
-        ],
+        [pltpu.VMEM((residues * seconds, pair_w), F32)],
         flops=540_000_000,
     )
     right_in = []
@@ -449,12 +441,11 @@
     pair_update, proj_parts = outs[0], outs[1:]
     proj_core = cores_of(proj_parts)
 
-    stat_rows = 2 * chans * (width // LANES) + 16
+    stat_rows = 2 * chans * (width // LANES) + 8
     left_d, stat = call(
         functools.partial(moment_kernel, cols, chans),
-        (*left_parts, right_d, x, bias_part),
+        (*left_parts, right_d, normed, order, bias_part),
         [((seqs, wide_proj), BF16), ((stat_rows, LANES), BF16)],
-        [pltpu.VMEM((width // LANES, seqs * residues, LANES), F32)],
     )
     stat_core = cores_of([stat] * ratio)
     firsts = call(

time: 57.1 us -> 56.6 us (level)
  Pallas kernels: 10 us -> 8.94 us
    pallas_call x12, Pallas kernels: 10 us -> 8.94 us  [call(): pl.pallas_call(body, out_shape=[jax.ShapeDtypeStruct(d, t) for d, t in ou...]
  transfers between devices with their start and end apart: 27 -> 27, of which waited for: 8 -> 8; matrix products, arithmetic and copies ran while one was open for 0% -> 0% of each run, Pallas kernels for 13% -> 11%
where the time goes in v3:
time: 56.6 us; the launch traced here: 56.5 us
  starting transfers between devices  34.9 us (62%)
  waiting for transfers between devices  11.9 us (21%)
  Pallas kernels  8.94 us (16%)
  between operations  0.74 us (1%)
    ppermute x9, starting transfers between devices, cols_of(): lax.ppermute(parts[k], 'col', pairs[k])  14.1 us
    ppermute x9, starting transfers between devices, chips_of(): lax.ppermute(parts[k], 'row', pairs[k])  11.7 us
    pallas_call x12, Pallas kernels, call(): pl.pallas_call(body, out_shape=[jax.ShapeDtypeStruct(d, t) for d, t in ou...  8.94 us
    ppermute x9, waiting for transfers between devices, chips_of(): lax.ppermute(parts[k], 'row', pairs[k])  5.62 us
    ppermute x1, starting transfers between devices, whole_step(): right_own = lax.ppermute(right_own, ('row', 'col'), pairs)  3.97 us
    ppermute x9, waiting for transfers between devices, cols_of(): lax.ppermute(parts[k], 'col', pairs[k])  3.81 us
    ppermute x1, starting transfers between devices, whole_step(): lax.ppermute(right_sent, ('row', 'col'), [(b, a) for a, b in pairs])  3.46 us
    ppermute x7, starting transfers between devices, cores_of(): lax.ppermute(parts[e], 'row', pairs[e])  1.67 us
  transfers between devices with their start and end apart: 27, of which 8 were waited for; matrix products, arithmetic and copies ran while one was open for 0% of the time, Pallas kernels for 11%

profile of v3, /device:TPU:0, one launch (start us, length us, event | category | flops | bytes accessed | tf_op | source)
XLA Modules:
  0.0 56.5 jit_solution(6507727343698444352)
XLA Ops:
  0.6 1.8 %shard_map.126 = (bf16[32,16,256]{2,1,0:T(8,128)(2,1)S(1)}, f32[1,256]{1,0:T(1,128)S(1)}, bf16[32,256]{1,0:T(8,128)(2,1)S(1)}, bf16[32,256]{1,0:T(8,128)(2,1)S(1...) custom-call(bf16[32,16,256]{2,1,0:T(8,128)(2,1)} %refs_0_.1, ...), custom_call_target="tpu_custom_call" | custom-call | flops 40000000 | bytes 689664 | tf_op jit(solution)/shard_map/pallas_call | solution.py:36
  2.5 4.0 %collective-permute-start.3 = (bf16[32,512]{1,0:T(8,128)(2,1)S(1)}, bf16[32,512]{1,0:T(8,128)(2,1)S(1)}, u32[]{:S(2)}, u32[]{:S(2)}) collective-permute-start(bf16[32,512]{1,0:T(8,128)(2,1)S(1)} %get-tuple-element.56), channel_id=1, source_target_pairs={{0,24},{1,16},{2,8},{3,0},{4,28},{5,20},{6,12},{7,4},{8,25},{9,17}... | collective-permute-start | bytes 98312 | tf_op jit(solution)/shard_map/ppermute | solution.py:375
  6.5 0.5 collective-permute-start
  7.0 1.3 %collective-permute-start.1 = (bf16[32,512]{1,0:T(8,128)(2,1)S(1)}, bf16[32,512]{1,0:T(8,128)(2,1)S(1)}, u32[]{:S(2)}, u32[]{:S(2)}) collective-permute-start(bf16[32,512]{1,0:T(8,128)(2,1)S(1)} %get-tuple-element.51.refs_0_), channel_id=1, source_target_pairs={{0,2},{1,3},{2,0},{3,1},{4,6},{5,7},{6,4},{7,5},{8,10},{9,11},{10,... | collective-permute-start | bytes 98312 | tf_op jit(solution)/shard_map/ppermute | solution.py:342
  8.3 1.3 %collective-permute-done.3.refs_0_ = bf16[32,512]{1,0:T(8,128)(2,1)S(1)} collective-permute-done((bf16[32,512]{1,0:T(8,128)(2,1)S(1)}, bf16[32,512]{1,0:T(8,128)(2,1)S(1)}, u32[]{:S(2)}, u32[]{:S(2)}) %collective-permute-start.3) | collective-permute-done | bytes 32800 | tf_op jit(solution)/shard_map/ppermute | solution.py:375
  9.6 2.1 %collective-permute-start.9 = (bf16[32,512]{1,0:T(8,128)(2,1)S(1)}, bf16[32,512]{1,0:T(8,128)(2,1)S(1)}, u32[]{:S(2)}, u32[]{:S(2)}) collective-permute-start(bf16[32,512]{1,0:T(8,128)(2,1)S(1)} %collective-permute-done.3.refs_0_), channel_id=1, source_target_pairs={{0,24},{4,28},{8,16},{12,20},{16,8},{20,12},{24,0},{28,4},{1,25},{... | collective-permute-start | bytes 98312 | tf_op jit(solution)/shard_map/ppermute | solution.py:346
  11.7 2.0 %collective-permute-start.5 = (bf16[32,512]{1,0:T(8,128)(2,1)S(1)}, bf16[32,512]{1,0:T(8,128)(2,1)S(1)}, u32[]{:S(2)}, u32[]{:S(2)}) collective-permute-start(bf16[32,512]{1,0:T(8,128)(2,1)S(1)} %collective-permute-done.3.refs_0_), channel_id=1, source_target_pairs={{0,8},{4,12},{8,0},{12,4},{16,24},{20,28},{24,16},{28,20},{1,9},{5... | collective-permute-start | bytes 98312 | tf_op jit(solution)/shard_map/ppermute | solution.py:346
  13.7 0.0 collective-permute-start.7
  13.7 0.0 collective-permute-done.refs_1_
  13.7 3.7 %collective-permute-start.2 = (bf16[32,512]{1,0:T(8,128)(2,1)S(1)}, bf16[32,512]{1,0:T(8,128)(2,1)S(1)}, u32[]{:S(2)}, u32[]{:S(2)}) collective-permute-start(bf16[32,512]{1,0:T(8,128)(2,1)S(1)} %get-tuple-element.51.refs_0_), channel_id=1, source_target_pairs={{0,3},{1,2},{2,1},{3,0},{4,7},{5,6},{6,5},{7,4},{8,11},{9,10},{10,... | collective-permute-start | bytes 98312 | tf_op jit(solution)/shard_map/ppermute | solution.py:342
  17.4 0.0 collective-permute-done.1.refs_2_
  17.4 0.0 collective-permute-start.4
  17.4 0.0 collective-permute-done.9.refs_6_
  17.4 0.5 collective-permute-start.10
  17.9 0.0 collective-permute-done.5.refs_2_
  17.9 0.1 collective-permute-start.6
  17.9 0.0 collective-permute-done.7.refs_4_
  18.0 0.4 collective-permute-start.8
  18.4 1.1 %shard_map.127 = (bf16[512,1024]{1,0:T(8,128)(2,1)S(1)}, bf16[512,128]{1,0:T(8,128)(2,1)S(1)}, f32[8,128]{1,0:T(8,128)S(1)}) custom-call(bf16[16,32,128]{2,1,0:T(8,128)(2,1)S(1)} %get-tuple-element.52.cot_ref, bf16[1024,128]{1,0:T(8,128)(2,1)S(1)} %get-tuple-element.53.w_ref.refs_3_), custom_call_target="tpu_custom_call" | custom-call | flops 540000000 | bytes 393216 | tf_op jit(solution)/shard_map/pallas_call | solution.py:36
  19.5 0.0 collective-permute-done.2.refs_3_
  19.5 0.4 shard_map.128
  19.9 0.1 collective-permute-start.14
  20.0 0.0 collective-permute-done.4.refs_1_
  20.0 0.0 collective-permute-done.10.refs_7_
  20.0 0.0 collective-permute-done.6.refs_3_
  20.1 0.0 collective-permute-done.8.refs_5_
  20.1 0.5 shard_map.129
  20.6 2.0 %shard_map.130 = (bf16[16,32,128]{2,1,0:T(8,128)(2,1)}, bf16[4,128,128]{2,1,0:T(8,128)(2,1)S(1)}, bf16[4,128,128]{2,1,0:T(8,128)(2,1)S(1)}) custom-call(bf16[128,512]{1,0:T(8,128)(2,1)S(1)} %get-tuple-element.55.refs_0_, bf16[2,128,512]{2,1,0:T(8,128)(2,1)S(1)} %get-tuple-element.57.refs_1_, bf16[512,128]{1,0:T(8,128)(2,1)S(1)} %get-tuple-element.58.refs_2_, ...), custom_call_target="tpu_custom_call" | custom-call | flops 800000000 | bytes 786944 | tf_op jit(solution)/shard_map/pallas_call | solution.py:36
  22.6 0.4 collective-permute-start.19
  23.1 0.0 collective-permute-done.14.refs_1_
  23.1 0.1 shard_map.131
  23.1 1.2 %collective-permute-start.15 = (bf16[32,512]{1,0:T(8,128)(2,1)S(1)}, bf16[32,512]{1,0:T(8,128)(2,1)S(1)}, u32[]{:S(2)}, u32[]{:S(2)}) collective-permute-start(bf16[32,512]{1,0:T(8,128)(2,1)S(1)} %get-tuple-element.72), channel_id=1, source_target_pairs={{0,8},{4,12},{8,0},{12,4},{16,24},{20,28},{24,16},{28,20},{1,9},{5... | collective-permute-start | bytes 98312 | tf_op jit(solution)/shard_map/ppermute | solution.py:346
  24.3 1.4 %collective-permute-start.16 = (bf16[32,512]{1,0:T(8,128)(2,1)S(1)}, bf16[32,512]{1,0:T(8,128)(2,1)S(1)}, u32[]{:S(2)}, u32[]{:S(2)}) collective-permute-start(bf16[32,512]{1,0:T(8,128)(2,1)S(1)} %get-tuple-element.73), channel_id=1, source_target_pairs={{0,16},{4,20},{8,24},{12,28},{16,0},{20,4},{24,8},{28,12},{1,17},{... | collective-permute-start | bytes 98312 | tf_op jit(solution)/shard_map/ppermute | solution.py:346
  25.7 1.0 %collective-permute-start.17 = (bf16[32,512]{1,0:T(8,128)(2,1)S(1)}, bf16[32,512]{1,0:T(8,128)(2,1)S(1)}, u32[]{:S(2)}, u32[]{:S(2)}) collective-permute-start(bf16[32,512]{1,0:T(8,128)(2,1)S(1)} %get-tuple-element.74), channel_id=1, source_target_pairs={{0,24},{4,28},{8,16},{12,20},{16,8},{20,12},{24,0},{28,4},{1,25},{... | collective-permute-start | bytes 98312 | tf_op jit(solution)/shard_map/ppermute | solution.py:346
  26.7 0.0 collective-permute-start.11
  26.7 0.4 collective-permute-done.15.refs_1_
  27.1 3.7 %collective-permute-start.12 = (bf16[32,512]{1,0:T(8,128)(2,1)S(1)}, bf16[32,512]{1,0:T(8,128)(2,1)S(1)}, u32[]{:S(2)}, u32[]{:S(2)}) collective-permute-start(bf16[32,512]{1,0:T(8,128)(2,1)S(1)} %get-tuple-element.67), channel_id=1, source_target_pairs={{0,2},{1,3},{2,0},{3,1},{4,6},{5,7},{6,4},{7,5},{8,10},{9,11},{10,... | collective-permute-start | bytes 98312 | tf_op jit(solution)/shard_map/ppermute | solution.py:342
  30.8 0.0 collective-permute-done.16.refs_2_
  30.8 0.4 collective-permute-start.13
  31.2 0.0 collective-permute-done.17.refs_3_
  31.3 3.5 %collective-permute-start.18 = (bf16[32,512]{1,0:T(8,128)(2,1)S(1)}, bf16[32,512]{1,0:T(8,128)(2,1)S(1)}, u32[]{:S(2)}, u32[]{:S(2)}) collective-permute-start(bf16[32,512]{1,0:T(8,128)(2,1)S(1)} %shard_map.132), channel_id=1, source_target_pairs={{24,0},{16,1},{8,2},{0,3},{28,4},{20,5},{12,6},{4,7},{25,8},{17,9}... | collective-permute-start | bytes 98312 | tf_op jit(solution)/shard_map/ppermute | solution.py:411
  34.7 0.0 collective-permute-done.11.refs_1_
  34.7 0.0 collective-permute-done.12.refs_2_
  34.7 1.8 %collective-permute-done.13.refs_3_ = bf16[32,512]{1,0:T(8,128)(2,1)S(1)} collective-permute-done((bf16[32,512]{1,0:T(8,128)(2,1)S(1)}, bf16[32,512]{1,0:T(8,128)(2,1)S(1)}, u32[]{:S(2)}, u32[]{:S(2)}) %collective-permute-start.13) | collective-permute-done | bytes 32800 | tf_op jit(solution)/shard_map/ppermute | solution.py:342
  36.5 0.0 collective-permute-done.18.refs_4_.right_ref
  36.5 0.6 shard_map.133
  37.1 0.1 collective-permute-start.20
  37.2 0.0 collective-permute-done.19.refs_1_
  37.2 1.2 %collective-permute-done.20.refs_3_ = bf16[136,128]{1,0:T(8,128)(2,1)S(1)} collective-permute-done((bf16[136,128]{1,0:T(8,128)(2,1)S(1)}, bf16[136,128]{1,0:T(8,128)(2,1)S(1)}, u32[]{:S(2)}, u32[]{:S(2)}) %collective-permute-start.20) | collective-permute-done | bytes 34848 | tf_op jit(solution)/shard_map/ppermute | solution.py:350
  38.4 0.1 shard_map.135
  38.4 1.2 %collective-permute-start.21 = (bf16[264,128]{1,0:T(8,128)(2,1)S(1)}, bf16[264,128]{1,0:T(8,128)(2,1)S(1)}, u32[]{:S(2)}, u32[]{:S(2)}) collective-permute-start(bf16[264,128]{1,0:T(8,128)(2,1)S(1)} %get-tuple-element.83), channel_id=1, source_target_pairs={{0,8},{4,12},{8,0},{12,4},{16,24},{20,28},{24,16},{28,20},{1,9},{5... | collective-permute-start | bytes 202760 | tf_op jit(solution)/shard_map/ppermute | solution.py:346
  39.6 2.9 %collective-permute-start.22 = (bf16[264,128]{1,0:T(8,128)(2,1)S(1)}, bf16[264,128]{1,0:T(8,128)(2,1)S(1)}, u32[]{:S(2)}, u32[]{:S(2)}) collective-permute-start(bf16[264,128]{1,0:T(8,128)(2,1)S(1)} %get-tuple-element.84), channel_id=1, source_target_pairs={{0,16},{4,20},{8,24},{12,28},{16,0},{20,4},{24,8},{28,12},{1,17},{... | collective-permute-start | bytes 202760 | tf_op jit(solution)/shard_map/ppermute | solution.py:346
  42.5 0.3 collective-permute-done.21.refs_1_
  42.8 2.8 %collective-permute-done.22.refs_2_ = bf16[264,128]{1,0:T(8,128)(2,1)S(1)} collective-permute-done((bf16[264,128]{1,0:T(8,128)(2,1)S(1)}, bf16[264,128]{1,0:T(8,128)(2,1)S(1)}, u32[]{:S(2)}, u32[]{:S(2)}) %collective-permute-start.22) | collective-permute-done | bytes 67616 | tf_op jit(solution)/shard_map/ppermute | solution.py:346
  45.6 2.1 %collective-permute-done.23.refs_3_ = bf16[264,128]{1,0:T(8,128)(2,1)S(1)} collective-permute-done((bf16[264,128]{1,0:T(8,128)(2,1)S(1)}, bf16[264,128]{1,0:T(8,128)(2,1)S(1)}, u32[]{:S(2)}, u32[]{:S(2)}) %collective-permute-start.23) | collective-permute-done | bytes 67616 | tf_op jit(solution)/shard_map/ppermute | solution.py:346
  47.7 0.1 shard_map.136
  47.7 0.4 collective-permute-start.24
  48.2 1.8 %collective-permute-start.25 = (bf16[168,128]{1,0:T(8,128)(2,1)S(1)}, bf16[168,128]{1,0:T(8,128)(2,1)S(1)}, u32[]{:S(2)}, u32[]{:S(2)}) collective-permute-start(bf16[168,128]{1,0:T(8,128)(2,1)S(1)} %get-tuple-element.88), channel_id=1, source_target_pairs={{0,2},{1,3},{2,0},{3,1},{4,6},{5,7},{6,4},{7,5},{8,10},{9,11},{10,... | collective-permute-start | bytes 129032 | tf_op jit(solution)/shard_map/ppermute | solution.py:342
  50.0 2.2 %collective-permute-start.26 = (bf16[168,128]{1,0:T(8,128)(2,1)S(1)}, bf16[168,128]{1,0:T(8,128)(2,1)S(1)}, u32[]{:S(2)}, u32[]{:S(2)}) collective-permute-start(bf16[168,128]{1,0:T(8,128)(2,1)S(1)} %get-tuple-element.89), channel_id=1, source_target_pairs={{0,3},{1,2},{2,1},{3,0},{4,7},{5,6},{6,5},{7,4},{8,11},{9,10},{10,... | collective-permute-start | bytes 129032 | tf_op jit(solution)/shard_map/ppermute | solution.py:342
  52.2 1.6 %shard_map.134 = bf16[32,16,256]{2,1,0:T(8,128)(2,1)} custom-call(bf16[32,16,256]{2,1,0:T(8,128)(2,1)S(1)} %get-tuple-element.61.x_ref, f32[1,256]{1,0:T(1,128)S(1)} %get-tuple-element.62.gain_ref.refs_4_, bf16[32,256]{1,0:T(8,128)(2,1)S(1)} %get-tuple-element.63.lw_ref.refs_5_, bf16[32,256]{1,0:T(8,128)(2,1)S(1)} %get-tuple-element.64.rw_ref.refs_6_, ...), custom_call_target="tpu_custom_call" | custom-call | flops 1 | bytes 361472 | tf_op jit(solution)/shard_map/pallas_call | solution.py:36
  53.8 0.0 collective-permute-done.24.refs_1_
  53.8 0.0 collective-permute-done.25.refs_2_
  53.8 2.0 %collective-permute-done.26.refs_3_ = bf16[168,128]{1,0:T(8,128)(2,1)S(1)} collective-permute-done((bf16[168,128]{1,0:T(8,128)(2,1)S(1)}, bf16[168,128]{1,0:T(8,128)(2,1)S(1)}, u32[]{:S(2)}, u32[]{:S(2)}) %collective-permute-start.26) | collective-permute-done | bytes 43040 | tf_op jit(solution)/shard_map/ppermute | solution.py:342
  55.8 0.7 %shard_map.137 = (f32[32,256]{1,0:T(8,128)}, f32[32,256]{1,0:T(8,128)}, f32[32,128]{1,0:T(8,128)}, f32[1,256]{1,0:T(1,128)}, f32[1,128]{1,0:T(1,128)}) custom-call(bf16[168,128]{1,0:T(8,128)(2,1)S(1)} %get-tuple-element.86.refs_0_, bf16[168,128]{1,0:T(8,128)(2,1)S(1)} %collective-permute-done.24.refs_1_, ...), custom_call_target="tpu_custom_call" | custom-call | flops 1 | bytes 205824 | tf_op jit(solution)/shard_map/pallas_call | solution.py:36
  (2 shorter events, 0.0 us)
Async XLA Ops:
  2.5 7.1 %collective-permute-start.3 = (bf16[32,512]{1,0:T(8,128)(2,1)S(1)}, bf16[32,512]{1,0:T(8,128)(2,1)S(1)}, u32[]{:S(2)}, u32[]{:S(2)}) collective-permute-start(bf16[32,512]{1,0:T(8,128)(2,1)S(1)} %get-tuple-element.56), channel_id=1, source_target_pairs={{0,24},{1,16},{2,8},{3,0},{4,28},{5,20},{6,12},{7,4},{8,25},{9,17}... | collective-permute-start | bytes 98312 | tf_op jit(solution)/shard_map/ppermute | solution.py:375
  6.5 7.2 %collective-permute-start = (bf16[32,512]{1,0:T(8,128)(2,1)S(1)}, bf16[32,512]{1,0:T(8,128)(2,1)S(1)}, u32[]{:S(2)}, u32[]{:S(2)}) collective-permute-start(bf16[32,512]{1,0:T(8,128)(2,1)S(1)} %get-tuple-element.51.refs_0_), channel_id=1, source_target_pairs={{0,1},{1,0},{2,3},{3,2},{4,5},{5,4},{6,7},{7,6},{8,9},{9,8},{10,11... | collective-permute-start | bytes 98312 | tf_op jit(solution)/shard_map/ppermute | solution.py:342
  7.0 10.4 %collective-permute-start.1 = (bf16[32,512]{1,0:T(8,128)(2,1)S(1)}, bf16[32,512]{1,0:T(8,128)(2,1)S(1)}, u32[]{:S(2)}, u32[]{:S(2)}) collective-permute-start(bf16[32,512]{1,0:T(8,128)(2,1)S(1)} %get-tuple-element.51.refs_0_), channel_id=1, source_target_pairs={{0,2},{1,3},{2,0},{3,1},{4,6},{5,7},{6,4},{7,5},{8,10},{9,11},{10,... | collective-permute-start | bytes 98312 | tf_op jit(solution)/shard_map/ppermute | solution.py:342
  9.6 7.8 %collective-permute-start.9 = (bf16[32,512]{1,0:T(8,128)(2,1)S(1)}, bf16[32,512]{1,0:T(8,128)(2,1)S(1)}, u32[]{:S(2)}, u32[]{:S(2)}) collective-permute-start(bf16[32,512]{1,0:T(8,128)(2,1)S(1)} %collective-permute-done.3.refs_0_), channel_id=1, source_target_pairs={{0,24},{4,28},{8,16},{12,20},{16,8},{20,12},{24,0},{28,4},{1,25},{... | collective-permute-start | bytes 98312 | tf_op jit(solution)/shard_map/ppermute | solution.py:346
  11.7 6.2 %collective-permute-start.5 = (bf16[32,512]{1,0:T(8,128)(2,1)S(1)}, bf16[32,512]{1,0:T(8,128)(2,1)S(1)}, u32[]{:S(2)}, u32[]{:S(2)}) collective-permute-start(bf16[32,512]{1,0:T(8,128)(2,1)S(1)} %collective-permute-done.3.refs_0_), channel_id=1, source_target_pairs={{0,8},{4,12},{8,0},{12,4},{16,24},{20,28},{24,16},{28,20},{1,9},{5... | collective-permute-start | bytes 98312 | tf_op jit(solution)/shard_map/ppermute | solution.py:346
  13.7 4.3 %collective-permute-start.7 = (bf16[32,512]{1,0:T(8,128)(2,1)S(1)}, bf16[32,512]{1,0:T(8,128)(2,1)S(1)}, u32[]{:S(2)}, u32[]{:S(2)}) collective-permute-start(bf16[32,512]{1,0:T(8,128)(2,1)S(1)} %collective-permute-done.3.refs_0_), channel_id=1, source_target_pairs={{0,16},{4,20},{8,24},{12,28},{16,0},{20,4},{24,8},{28,12},{1,17},{... | collective-permute-start | bytes 98312 | tf_op jit(solution)/shard_map/ppermute | solution.py:346
  13.7 5.9 %collective-permute-start.2 = (bf16[32,512]{1,0:T(8,128)(2,1)S(1)}, bf16[32,512]{1,0:T(8,128)(2,1)S(1)}, u32[]{:S(2)}, u32[]{:S(2)}) collective-permute-start(bf16[32,512]{1,0:T(8,128)(2,1)S(1)} %get-tuple-element.51.refs_0_), channel_id=1, source_target_pairs={{0,3},{1,2},{2,1},{3,0},{4,7},{5,6},{6,5},{7,4},{8,11},{9,10},{10,... | collective-permute-start | bytes 98312 | tf_op jit(solution)/shard_map/ppermute | solution.py:342
  17.4 2.7 %collective-permute-start.4 = (bf16[32,512]{1,0:T(8,128)(2,1)S(1)}, bf16[32,512]{1,0:T(8,128)(2,1)S(1)}, u32[]{:S(2)}, u32[]{:S(2)}) collective-permute-start(bf16[32,512]{1,0:T(8,128)(2,1)S(1)} %collective-permute-done.3.refs_0_), channel_id=1, source_target_pairs={{0,4},{4,0},{8,12},{12,8},{16,20},{20,16},{24,28},{28,24},{1,5},{5... | collective-permute-start | bytes 98312 | tf_op jit(solution)/shard_map/ppermute | solution.py:350
  17.4 2.7 %collective-permute-start.10 = (bf16[32,512]{1,0:T(8,128)(2,1)S(1)}, bf16[32,512]{1,0:T(8,128)(2,1)S(1)}, u32[]{:S(2)}, u32[]{:S(2)}) collective-permute-start(bf16[32,512]{1,0:T(8,128)(2,1)S(1)} %collective-permute-done.9.refs_6_), channel_id=1, source_target_pairs={{0,4},{4,0},{8,12},{12,8},{16,20},{20,16},{24,28},{28,24},{1,5},{5... | collective-permute-start | bytes 98312 | tf_op jit(solution)/shard_map/ppermute | solution.py:350
  17.9 2.2 %collective-permute-start.6 = (bf16[32,512]{1,0:T(8,128)(2,1)S(1)}, bf16[32,512]{1,0:T(8,128)(2,1)S(1)}, u32[]{:S(2)}, u32[]{:S(2)}) collective-permute-start(bf16[32,512]{1,0:T(8,128)(2,1)S(1)} %collective-permute-done.5.refs_2_), channel_id=1, source_target_pairs={{0,4},{4,0},{8,12},{12,8},{16,20},{20,16},{24,28},{28,24},{1,5},{5... | collective-permute-start | bytes 98312 | tf_op jit(solution)/shard_map/ppermute | solution.py:350
  18.0 2.1 %collective-permute-start.8 = (bf16[32,512]{1,0:T(8,128)(2,1)S(1)}, bf16[32,512]{1,0:T(8,128)(2,1)S(1)}, u32[]{:S(2)}, u32[]{:S(2)}) collective-permute-start(bf16[32,512]{1,0:T(8,128)(2,1)S(1)} %collective-permute-done.7.refs_4_), channel_id=1, source_target_pairs={{0,4},{4,0},{8,12},{12,8},{16,20},{20,16},{24,28},{28,24},{1,5},{5... | collective-permute-start | bytes 98312 | tf_op jit(solution)/shard_map/ppermute | solution.py:350
  19.9 3.2 %collective-permute-start.14 = (bf16[128,512]{1,0:T(8,128)(2,1)S(1)}, bf16[128,512]{1,0:T(8,128)(2,1)S(1)}, u32[]{:S(2)}, u32[]{:S(2)}) collective-permute-start(bf16[128,512]{1,0:T(8,128)(2,1)S(1)} %get-tuple-element.70), channel_id=1, source_target_pairs={{0,4},{4,0},{8,12},{12,8},{16,20},{20,16},{24,28},{28,24},{1,5},{5... | collective-permute-start | bytes 393224 | tf_op jit(solution)/shard_map/ppermute | solution.py:350
  22.6 14.5 %collective-permute-start.19 = (bf16[4,128,128]{2,1,0:T(8,128)(2,1)S(1)}, bf16[4,128,128]{2,1,0:T(8,128)(2,1)S(1)}, u32[]{:S(2)}, u32[]{:S(2)}) collective-permute-start(bf16[4,128,128]{2,1,0:T(8,128)(2,1)S(1)} %get-tuple-element.80), channel_id=1, source_target_pairs={{0,4},{4,0},{8,12},{12,8},{16,20},{20,16},{24,28},{28,24},{1,5},{5... | collective-permute-start | bytes 393224 | tf_op jit(solution)/shard_map/ppermute | solution.py:350
  23.1 4.0 %collective-permute-start.15 = (bf16[32,512]{1,0:T(8,128)(2,1)S(1)}, bf16[32,512]{1,0:T(8,128)(2,1)S(1)}, u32[]{:S(2)}, u32[]{:S(2)}) collective-permute-start(bf16[32,512]{1,0:T(8,128)(2,1)S(1)} %get-tuple-element.72), channel_id=1, source_target_pairs={{0,8},{4,12},{8,0},{12,4},{16,24},{20,28},{24,16},{28,20},{1,9},{5... | collective-permute-start | bytes 98312 | tf_op jit(solution)/shard_map/ppermute | solution.py:346
  24.3 6.5 %collective-permute-start.16 = (bf16[32,512]{1,0:T(8,128)(2,1)S(1)}, bf16[32,512]{1,0:T(8,128)(2,1)S(1)}, u32[]{:S(2)}, u32[]{:S(2)}) collective-permute-start(bf16[32,512]{1,0:T(8,128)(2,1)S(1)} %get-tuple-element.73), channel_id=1, source_target_pairs={{0,16},{4,20},{8,24},{12,28},{16,0},{20,4},{24,8},{28,12},{1,17},{... | collective-permute-start | bytes 98312 | tf_op jit(solution)/shard_map/ppermute | solution.py:346
  25.7 5.5 %collective-permute-start.17 = (bf16[32,512]{1,0:T(8,128)(2,1)S(1)}, bf16[32,512]{1,0:T(8,128)(2,1)S(1)}, u32[]{:S(2)}, u32[]{:S(2)}) collective-permute-start(bf16[32,512]{1,0:T(8,128)(2,1)S(1)} %get-tuple-element.74), channel_id=1, source_target_pairs={{0,24},{4,28},{8,16},{12,20},{16,8},{20,12},{24,0},{28,4},{1,25},{... | collective-permute-start | bytes 98312 | tf_op jit(solution)/shard_map/ppermute | solution.py:346
  26.7 8.0 %collective-permute-start.11 = (bf16[32,512]{1,0:T(8,128)(2,1)S(1)}, bf16[32,512]{1,0:T(8,128)(2,1)S(1)}, u32[]{:S(2)}, u32[]{:S(2)}) collective-permute-start(bf16[32,512]{1,0:T(8,128)(2,1)S(1)} %get-tuple-element.66), channel_id=1, source_target_pairs={{0,1},{1,0},{2,3},{3,2},{4,5},{5,4},{6,7},{7,6},{8,9},{9,8},{10,11... | collective-permute-start | bytes 98312 | tf_op jit(solution)/shard_map/ppermute | solution.py:342
  27.1 7.6 %collective-permute-start.12 = (bf16[32,512]{1,0:T(8,128)(2,1)S(1)}, bf16[32,512]{1,0:T(8,128)(2,1)S(1)}, u32[]{:S(2)}, u32[]{:S(2)}) collective-permute-start(bf16[32,512]{1,0:T(8,128)(2,1)S(1)} %get-tuple-element.67), channel_id=1, source_target_pairs={{0,2},{1,3},{2,0},{3,1},{4,6},{5,7},{6,4},{7,5},{8,10},{9,11},{10,... | collective-permute-start | bytes 98312 | tf_op jit(solution)/shard_map/ppermute | solution.py:342
  30.8 5.7 %collective-permute-start.13 = (bf16[32,512]{1,0:T(8,128)(2,1)S(1)}, bf16[32,512]{1,0:T(8,128)(2,1)S(1)}, u32[]{:S(2)}, u32[]{:S(2)}) collective-permute-start(bf16[32,512]{1,0:T(8,128)(2,1)S(1)} %get-tuple-element.68), channel_id=1, source_target_pairs={{0,3},{1,2},{2,1},{3,0},{4,7},{5,6},{6,5},{7,4},{8,11},{9,10},{10,... | collective-permute-start | bytes 98312 | tf_op jit(solution)/shard_map/ppermute | solution.py:342
  31.3 5.3 %collective-permute-start.18 = (bf16[32,512]{1,0:T(8,128)(2,1)S(1)}, bf16[32,512]{1,0:T(8,128)(2,1)S(1)}, u32[]{:S(2)}, u32[]{:S(2)}) collective-permute-start(bf16[32,512]{1,0:T(8,128)(2,1)S(1)} %shard_map.132), channel_id=1, source_target_pairs={{24,0},{16,1},{8,2},{0,3},{28,4},{20,5},{12,6},{4,7},{25,8},{17,9}... | collective-permute-start | bytes 98312 | tf_op jit(solution)/shard_map/ppermute | solution.py:411
  37.1 1.3 %collective-permute-start.20 = (bf16[136,128]{1,0:T(8,128)(2,1)S(1)}, bf16[136,128]{1,0:T(8,128)(2,1)S(1)}, u32[]{:S(2)}, u32[]{:S(2)}) collective-permute-start(bf16[136,128]{1,0:T(8,128)(2,1)S(1)} %get-tuple-element.81.refs_2_), channel_id=1, source_target_pairs={{0,4},{4,0},{8,12},{12,8},{16,20},{20,16},{24,28},{28,24},{1,5},{5... | collective-permute-start | bytes 104456 | tf_op jit(solution)/shard_map/ppermute | solution.py:350
  38.4 4.4 %collective-permute-start.21 = (bf16[264,128]{1,0:T(8,128)(2,1)S(1)}, bf16[264,128]{1,0:T(8,128)(2,1)S(1)}, u32[]{:S(2)}, u32[]{:S(2)}) collective-permute-start(bf16[264,128]{1,0:T(8,128)(2,1)S(1)} %get-tuple-element.83), channel_id=1, source_target_pairs={{0,8},{4,12},{8,0},{12,4},{16,24},{20,28},{24,16},{28,20},{1,9},{5... | collective-permute-start | bytes 202760 | tf_op jit(solution)/shard_map/ppermute | solution.py:346
  39.6 6.0 %collective-permute-start.22 = (bf16[264,128]{1,0:T(8,128)(2,1)S(1)}, bf16[264,128]{1,0:T(8,128)(2,1)S(1)}, u32[]{:S(2)}, u32[]{:S(2)}) collective-permute-start(bf16[264,128]{1,0:T(8,128)(2,1)S(1)} %get-tuple-element.84), channel_id=1, source_target_pairs={{0,16},{4,20},{8,24},{12,28},{16,0},{20,4},{24,8},{28,12},{1,17},{... | collective-permute-start | bytes 202760 | tf_op jit(solution)/shard_map/ppermute | solution.py:346
  42.5 5.2 %collective-permute-start.23 = (bf16[264,128]{1,0:T(8,128)(2,1)S(1)}, bf16[264,128]{1,0:T(8,128)(2,1)S(1)}, u32[]{:S(2)}, u32[]{:S(2)}) collective-permute-start(bf16[264,128]{1,0:T(8,128)(2,1)S(1)} %get-tuple-element.85), channel_id=1, source_target_pairs={{0,24},{4,28},{8,16},{12,20},{16,8},{20,12},{24,0},{28,4},{1,25},{... | collective-permute-start | bytes 202760 | tf_op jit(solution)/shard_map/ppermute | solution.py:346
  47.7 6.1 %collective-permute-start.24 = (bf16[168,128]{1,0:T(8,128)(2,1)S(1)}, bf16[168,128]{1,0:T(8,128)(2,1)S(1)}, u32[]{:S(2)}, u32[]{:S(2)}) collective-permute-start(bf16[168,128]{1,0:T(8,128)(2,1)S(1)} %get-tuple-element.87), channel_id=1, source_target_pairs={{0,1},{1,0},{2,3},{3,2},{4,5},{5,4},{6,7},{7,6},{8,9},{9,8},{10,11... | collective-permute-start | bytes 129032 | tf_op jit(solution)/shard_map/ppermute | solution.py:342
  48.2 5.7 %collective-permute-start.25 = (bf16[168,128]{1,0:T(8,128)(2,1)S(1)}, bf16[168,128]{1,0:T(8,128)(2,1)S(1)}, u32[]{:S(2)}, u32[]{:S(2)}) collective-permute-start(bf16[168,128]{1,0:T(8,128)(2,1)S(1)} %get-tuple-element.88), channel_id=1, source_target_pairs={{0,2},{1,3},{2,0},{3,1},{4,6},{5,7},{6,4},{7,5},{8,10},{9,11},{10,... | collective-permute-start | bytes 129032 | tf_op jit(solution)/shard_map/ppermute | solution.py:342
  50.0 5.8 %collective-permute-start.26 = (bf16[168,128]{1,0:T(8,128)(2,1)S(1)}, bf16[168,128]{1,0:T(8,128)(2,1)S(1)}, u32[]{:S(2)}, u32[]{:S(2)}) collective-permute-start(bf16[168,128]{1,0:T(8,128)(2,1)S(1)} %get-tuple-element.89), channel_id=1, source_target_pairs={{0,3},{1,2},{2,1},{3,0},{4,7},{5,6},{6,5},{7,4},{8,11},{9,10},{10,... | collective-permute-start | bytes 129032 | tf_op jit(solution)/shard_map/ppermute | solution.py:342

commit v4 on v3

--- a/solution.py
+++ b/solution.py
@@ -142,6 +142,13 @@
 def places(ratio):
     row, col = lax.axis_index("row"), lax.axis_index("col")
     return row // ratio, row % ratio, col
+
+
+def order_of(bits):
+    order = [0]
+    for bit in bits:
+        order = order + [k ^ bit for k in order]
+    return order
 
 
 def right_grad_kernel(cols, ratio, *refs):
@@ -247,8 +254,12 @@
     stat_ref[...] = jnp.concatenate(halves + [bias_ref[...]], axis=0).astype(BF16)
 
 
-def sum_kernel(*refs):
-    refs[-1][...] = tree([wide(r) for r in refs[:-1]]).astype(BF16)
+def split_kernel(*refs):
+    total = tree([wide(r) for r in refs[:2]])
+    outs = refs[2:]
+    size = outs[0].shape[0]
+    for n, out in enumerate(outs):
+        out[...] = total[n * size : (n + 1) * size].astype(BF16)
 
 
 def input_grad_kernel(chans, x_ref, gain_ref, lw_ref, rw_ref, left_ref, right_ref, out_ref, flat):
@@ -270,15 +281,16 @@
     out_ref[...] = values.astype(BF16).reshape(seqs, residues, width)
 
 
-def core_sum_kernel(ratio, *refs):
-    right_in, refs = refs[:ratio], refs[ratio:]
-    outs, flat = refs[:-1], refs[-1]
-    seqs = outs[0].shape[0]
+def core_sum_kernel(order, ratio, *refs):
+    right_in, outs, flat = refs[:ratio], refs[ratio:-1], refs[-1]
+    cols = len(order)
+    seqs = flat.shape[0] // cols
     q, _, _ = places(ratio)
     flat[...] = tree([wide(r) for r in right_in])
-    for k, out in enumerate(outs):
-        place = pl.ds(pl.multiple_of((q ^ k ^ (len(outs) - 1)) * seqs, seqs), seqs)
-        out[...] = flat[place, :].astype(BF16)
+    for n, k in enumerate(order):
+        place = pl.ds(pl.multiple_of((q ^ k ^ (cols - 1)) * seqs, seqs), seqs)
+        row = n * seqs % outs[0].shape[0]
+        outs[n * 2 // cols][row : row + seqs] = flat[place, :].astype(BF16)
 
 
 def first_stat_kernel(ratio, *refs):
@@ -349,6 +361,8 @@
         pairs = [[(i, i ^ e) for i in range(rows)] for e in range(ratio)]
         return [parts[0]] + [lax.ppermute(parts[e], "row", pairs[e]) for e in range(1, ratio)]
 
+    up = [1 << n for n in range(cols.bit_length() - 1)]
+    down = up[::-1]
     pairs = [
         ((q * ratio + h) * cols + z, ((z ^ (cols - 1)) * ratio + h) * cols + q)
         for q in range(cols)
@@ -400,14 +414,19 @@
         flops=134_000_000,
     )
     right_parts, left_all = outs[:ratio], outs[ratio]
-    right_parts = call(
-        functools.partial(core_sum_kernel, ratio),
+    kept, moved = call(
+        functools.partial(core_sum_kernel, order_of(up), ratio),
         cores_of(right_parts),
-        [((seqs, wide_proj), BF16)] * cols,
+        [((total_seqs // 2, wide_proj), BF16)] * 2,
         [pltpu.VMEM((total_seqs, wide_proj), F32)],
     )
-    right_parts = chips_of(right_parts)
-    right_sent = call(sum_kernel, right_parts, [((seqs, wide_proj), BF16)])[0]
+    for bit in down:
+        moved = lax.ppermute(moved, "row", [(i, i ^ (bit * ratio)) for i in range(rows)])
+        shape = ((seqs * max(bit // 2, 1), wide_proj), BF16)
+        outs_of = [shape] * (2 if bit > 1 else 1)
+        parts = call(split_kernel, (kept, moved), outs_of)
+        kept, moved = parts[0], parts[-1]
+    right_sent = kept
     right_d = lax.ppermute(right_sent, ("row", "col"), [(b, a) for a, b in pairs])
 
     outs = call(

time: 56.6 us -> 61.1 us (1.080)
  waiting for transfers between devices: 11.9 us -> 21.7 us
  starting transfers between devices: 34.9 us -> 29.5 us
    ppermute x9 -> x6, starting transfers between devices: 11.7 us -> 7.8 us  [chips_of(): lax.ppermute(parts[k], 'row', pairs[k])]
    ppermute x9, waiting for transfers between devices: 3.81 us -> 7.21 us  [cols_of(): lax.ppermute(parts[k], 'col', pairs[k])]
    ppermute x0 -> x2, starting transfers between devices: none -> 3.27 us  [whole_step(): lax.ppermute(moved, 'row', [(i, i ^ bit * ratio) for i in range(rows)])]
    ppermute x1, starting transfers between devices: 3.46 us -> 1.21 us  [whole_step(): lax.ppermute(right_sent, ('row', 'col'), [(b, a) for a, b in pairs])]
    ppermute x1, waiting for transfers between devices: 1.31 us -> 3.3 us  [whole_step(): right_own = lax.ppermute(right_own, ('row', 'col'), pairs)]
    ppermute x1, waiting for transfers between devices: 0.01 us -> 1.84 us  [whole_step(): lax.ppermute(right_sent, ('row', 'col'), [(b, a) for a, b in pairs])]
    ppermute x1, starting transfers between devices: 3.97 us -> 2.5 us  [whole_step(): right_own = lax.ppermute(right_own, ('row', 'col'), pairs)]
    ppermute x7, starting transfers between devices: 1.67 us -> 0.22 us  [cores_of(): lax.ppermute(parts[e], 'row', pairs[e])]
  transfers between devices with their start and end apart: 27 -> 26, of which waited for: 8 -> 16; matrix products, arithmetic and copies ran while one was open for 0% -> 0% of each run, Pallas kernels for 11% -> 10%
where the time goes in v4:
time: 61.1 us; the launch traced here: 61 us
  starting transfers between devices  29.5 us (48%)
  waiting for transfers between devices  21.7 us (36%)
  Pallas kernels  8.95 us (15%)
  between operations  0.76 us (1%)
    ppermute x9, starting transfers between devices, cols_of(): lax.ppermute(parts[k], 'col', pairs[k])  14.5 us
    pallas_call x13, Pallas kernels, call(): pl.pallas_call(body, out_shape=[jax.ShapeDtypeStruct(d, t) for d, t in ou...  8.95 us
    ppermute x6, starting transfers between devices, chips_of(): lax.ppermute(parts[k], 'row', pairs[k])  7.8 us
    ppermute x9, waiting for transfers between devices, cols_of(): lax.ppermute(parts[k], 'col', pairs[k])  7.21 us
    ppermute x6, waiting for transfers between devices, chips_of(): lax.ppermute(parts[k], 'row', pairs[k])  6.41 us
    ppermute x1, waiting for transfers between devices, whole_step(): right_own = lax.ppermute(right_own, ('row', 'col'), pairs)  3.3 us
    ppermute x2, starting transfers between devices, whole_step(): lax.ppermute(moved, 'row', [(i, i ^ bit * ratio) for i in range(rows)])  3.27 us
    ppermute x1, starting transfers between devices, whole_step(): right_own = lax.ppermute(right_own, ('row', 'col'), pairs)  2.5 us
  transfers between devices with their start and end apart: 26, of which 16 were waited for; matrix products, arithmetic and copies ran while one was open for 0% of the time, Pallas kernels for 10%

profile of v4, /device:TPU:0, one launch (start us, length us, event | category | flops | bytes accessed | tf_op | source)
XLA Modules:
  0.0 61.0 jit_solution(16768199073026387511)
XLA Ops:
  0.6 1.8 %shard_map.126 = (bf16[32,16,256]{2,1,0:T(8,128)(2,1)S(1)}, f32[1,256]{1,0:T(1,128)S(1)}, bf16[32,256]{1,0:T(8,128)(2,1)S(1)}, bf16[32,256]{1,0:T(8,128)(2,1)S(1...) custom-call(bf16[32,16,256]{2,1,0:T(8,128)(2,1)} %refs_0_.1, ...), custom_call_target="tpu_custom_call" | custom-call | flops 40000000 | bytes 689664 | tf_op jit(solution)/shard_map/pallas_call | solution.py:36
  2.5 3.1 %collective-permute-start = (bf16[32,512]{1,0:T(8,128)(2,1)S(1)}, bf16[32,512]{1,0:T(8,128)(2,1)S(1)}, u32[]{:S(2)}, u32[]{:S(2)}) collective-permute-start(bf16[32,512]{1,0:T(8,128)(2,1)S(1)} %get-tuple-element.51.refs_0_), channel_id=1, source_target_pairs={{0,1},{1,0},{2,3},{3,2},{4,5},{5,4},{6,7},{7,6},{8,9},{9,8},{10,11... | collective-permute-start | bytes 98312 | tf_op jit(solution)/shard_map/ppermute | solution.py:354
  5.6 2.6 %collective-permute-start.1 = (bf16[32,512]{1,0:T(8,128)(2,1)S(1)}, bf16[32,512]{1,0:T(8,128)(2,1)S(1)}, u32[]{:S(2)}, u32[]{:S(2)}) collective-permute-start(bf16[32,512]{1,0:T(8,128)(2,1)S(1)} %get-tuple-element.51.refs_0_), channel_id=1, source_target_pairs={{0,2},{1,3},{2,0},{3,1},{4,6},{5,7},{6,4},{7,5},{8,10},{9,11},{10,... | collective-permute-start | bytes 98312 | tf_op jit(solution)/shard_map/ppermute | solution.py:354
  8.2 0.0 collective-permute-start.2
  8.2 1.1 %shard_map.127 = (bf16[512,1024]{1,0:T(8,128)(2,1)S(1)}, bf16[512,128]{1,0:T(8,128)(2,1)S(1)}, f32[8,128]{1,0:T(8,128)S(1)}) custom-call(bf16[16,32,128]{2,1,0:T(8,128)(2,1)S(1)} %get-tuple-element.52.cot_ref, bf16[1024,128]{1,0:T(8,128)(2,1)S(1)} %get-tuple-element.53.w_ref.refs_3_), custom_call_target="tpu_custom_call" | custom-call | flops 540000000 | bytes 393216 | tf_op jit(solution)/shard_map/pallas_call | solution.py:36
  9.3 0.0 collective-permute-done.refs_1_
  9.3 1.7 %collective-permute-done.1.refs_2_ = bf16[32,512]{1,0:T(8,128)(2,1)S(1)} collective-permute-done((bf16[32,512]{1,0:T(8,128)(2,1)S(1)}, bf16[32,512]{1,0:T(8,128)(2,1)S(1)}, u32[]{:S(2)}, u32[]{:S(2)}) %collective-permute-start.1) | collective-permute-done | bytes 32800 | tf_op jit(solution)/shard_map/ppermute | solution.py:354
  11.0 2.9 %collective-permute-done.2.refs_3_ = bf16[32,512]{1,0:T(8,128)(2,1)S(1)} collective-permute-done((bf16[32,512]{1,0:T(8,128)(2,1)S(1)}, bf16[32,512]{1,0:T(8,128)(2,1)S(1)}, u32[]{:S(2)}, u32[]{:S(2)}) %collective-permute-start.2) | collective-permute-done | bytes 32800 | tf_op jit(solution)/shard_map/ppermute | solution.py:354
  13.9 0.4 shard_map.128
  14.3 0.1 collective-permute-start.14
  14.4 2.5 %collective-permute-start.3 = (bf16[32,512]{1,0:T(8,128)(2,1)S(1)}, bf16[32,512]{1,0:T(8,128)(2,1)S(1)}, u32[]{:S(2)}, u32[]{:S(2)}) collective-permute-start(bf16[32,512]{1,0:T(8,128)(2,1)S(1)} %get-tuple-element.56), channel_id=1, source_target_pairs={{0,24},{1,16},{2,8},{3,0},{4,28},{5,20},{6,12},{7,4},{8,25},{9,17}... | collective-permute-start | bytes 98312 | tf_op jit(solution)/shard_map/ppermute | solution.py:389
  16.9 3.3 %collective-permute-done.3.refs_0_ = bf16[32,512]{1,0:T(8,128)(2,1)S(1)} collective-permute-done((bf16[32,512]{1,0:T(8,128)(2,1)S(1)}, bf16[32,512]{1,0:T(8,128)(2,1)S(1)}, u32[]{:S(2)}, u32[]{:S(2)}) %collective-permute-start.3) | collective-permute-done | bytes 32800 | tf_op jit(solution)/shard_map/ppermute | solution.py:389
  20.2 1.5 %collective-permute-start.9 = (bf16[32,512]{1,0:T(8,128)(2,1)S(1)}, bf16[32,512]{1,0:T(8,128)(2,1)S(1)}, u32[]{:S(2)}, u32[]{:S(2)}) collective-permute-start(bf16[32,512]{1,0:T(8,128)(2,1)S(1)} %collective-permute-done.3.refs_0_), channel_id=1, source_target_pairs={{0,24},{4,28},{8,16},{12,20},{16,8},{20,12},{24,0},{28,4},{1,25},{... | collective-permute-start | bytes 98312 | tf_op jit(solution)/shard_map/ppermute | solution.py:358
  21.7 0.5 collective-permute-start.5
  22.2 1.4 %collective-permute-start.7 = (bf16[32,512]{1,0:T(8,128)(2,1)S(1)}, bf16[32,512]{1,0:T(8,128)(2,1)S(1)}, u32[]{:S(2)}, u32[]{:S(2)}) collective-permute-start(bf16[32,512]{1,0:T(8,128)(2,1)S(1)} %collective-permute-done.3.refs_0_), channel_id=1, source_target_pairs={{0,16},{4,20},{8,24},{12,28},{16,0},{20,4},{24,8},{28,12},{1,17},{... | collective-permute-start | bytes 98312 | tf_op jit(solution)/shard_map/ppermute | solution.py:358
  23.7 0.0 collective-permute-start.4
  23.7 1.4 %collective-permute-done.9.refs_6_ = bf16[32,512]{1,0:T(8,128)(2,1)S(1)} collective-permute-done((bf16[32,512]{1,0:T(8,128)(2,1)S(1)}, bf16[32,512]{1,0:T(8,128)(2,1)S(1)}, u32[]{:S(2)}, u32[]{:S(2)}) %collective-permute-start.9) | collective-permute-done | bytes 32800 | tf_op jit(solution)/shard_map/ppermute | solution.py:358
  25.1 0.0 collective-permute-start.10
  25.1 0.5 collective-permute-done.5.refs_2_
  25.6 0.0 collective-permute-start.6
  25.6 0.5 collective-permute-done.7.refs_4_
  26.1 0.0 collective-permute-start.8
  26.2 0.0 collective-permute-done.4.refs_1_
  26.2 0.1 collective-permute-done.10.refs_7_
  26.3 0.5 collective-permute-done.6.refs_3_
  26.8 0.5 collective-permute-done.8.refs_5_
  27.4 0.5 shard_map.129
  27.9 0.0 collective-permute-done.14.refs_1_
  27.9 0.1 shard_map.131
  28.0 1.6 %collective-permute-start.15 = (bf16[64,512]{1,0:T(8,128)(2,1)S(1)}, bf16[64,512]{1,0:T(8,128)(2,1)S(1)}, u32[]{:S(2)}, u32[]{:S(2)}) collective-permute-start(bf16[64,512]{1,0:T(8,128)(2,1)S(1)} %get-tuple-element.72), channel_id=1, source_target_pairs={{0,16},{4,20},{8,24},{12,28},{16,0},{20,4},{24,8},{28,12},{1,17},{... | collective-permute-start | bytes 196616 | tf_op jit(solution)/shard_map/ppermute | solution.py:424
  29.6 2.0 %shard_map.130 = (bf16[16,32,128]{2,1,0:T(8,128)(2,1)}, bf16[4,128,128]{2,1,0:T(8,128)(2,1)S(1)}, bf16[4,128,128]{2,1,0:T(8,128)(2,1)S(1)}) custom-call(bf16[128,512]{1,0:T(8,128)(2,1)S(1)} %get-tuple-element.55.refs_0_, bf16[2,128,512]{2,1,0:T(8,128)(2,1)S(1)} %get-tuple-element.57.refs_1_, bf16[512,128]{1,0:T(8,128)(2,1)S(1)} %get-tuple-element.58.refs_2_, ...), custom_call_target="tpu_custom_call" | custom-call | flops 800000000 | bytes 786944 | tf_op jit(solution)/shard_map/pallas_call | solution.py:36
  31.6 0.1 collective-permute-start.18
  31.7 0.6 collective-permute-done.15.refs_1_
  32.3 1.6 %collective-permute-start.16 = (bf16[32,512]{1,0:T(8,128)(2,1)S(1)}, bf16[32,512]{1,0:T(8,128)(2,1)S(1)}, u32[]{:S(2)}, u32[]{:S(2)}) collective-permute-start(bf16[32,512]{1,0:T(8,128)(2,1)S(1)} %get-tuple-element.74), channel_id=1, source_target_pairs={{0,8},{4,12},{8,0},{12,4},{16,24},{20,28},{24,16},{28,20},{1,9},{5... | collective-permute-start | bytes 98312 | tf_op jit(solution)/shard_map/ppermute | solution.py:424
  33.9 0.0 collective-permute-start.11
  33.9 1.7 %collective-permute-start.12 = (bf16[32,512]{1,0:T(8,128)(2,1)S(1)}, bf16[32,512]{1,0:T(8,128)(2,1)S(1)}, u32[]{:S(2)}, u32[]{:S(2)}) collective-permute-start(bf16[32,512]{1,0:T(8,128)(2,1)S(1)} %get-tuple-element.67), channel_id=1, source_target_pairs={{0,2},{1,3},{2,0},{3,1},{4,6},{5,7},{6,4},{7,5},{8,10},{9,11},{10,... | collective-permute-start | bytes 98312 | tf_op jit(solution)/shard_map/ppermute | solution.py:354
  35.7 2.7 %collective-permute-start.13 = (bf16[32,512]{1,0:T(8,128)(2,1)S(1)}, bf16[32,512]{1,0:T(8,128)(2,1)S(1)}, u32[]{:S(2)}, u32[]{:S(2)}) collective-permute-start(bf16[32,512]{1,0:T(8,128)(2,1)S(1)} %get-tuple-element.68), channel_id=1, source_target_pairs={{0,3},{1,2},{2,1},{3,0},{4,7},{5,6},{6,5},{7,4},{8,11},{9,10},{10,... | collective-permute-start | bytes 98312 | tf_op jit(solution)/shard_map/ppermute | solution.py:354
  38.3 0.0 collective-permute-done.16.refs_1_
  38.4 1.2 %collective-permute-start.17 = (bf16[32,512]{1,0:T(8,128)(2,1)S(1)}, bf16[32,512]{1,0:T(8,128)(2,1)S(1)}, u32[]{:S(2)}, u32[]{:S(2)}) collective-permute-start(bf16[32,512]{1,0:T(8,128)(2,1)S(1)} %shard_map.133), channel_id=1, source_target_pairs={{24,0},{16,1},{8,2},{0,3},{28,4},{20,5},{12,6},{4,7},{25,8},{17,9}... | collective-permute-start | bytes 98312 | tf_op jit(solution)/shard_map/ppermute | solution.py:430
  39.6 0.0 collective-permute-done.11.refs_1_
  39.6 0.0 collective-permute-done.12.refs_2_
  39.6 1.8 %collective-permute-done.13.refs_3_ = bf16[32,512]{1,0:T(8,128)(2,1)S(1)} collective-permute-done((bf16[32,512]{1,0:T(8,128)(2,1)S(1)}, bf16[32,512]{1,0:T(8,128)(2,1)S(1)}, u32[]{:S(2)}, u32[]{:S(2)}) %collective-permute-start.13) | collective-permute-done | bytes 32800 | tf_op jit(solution)/shard_map/ppermute | solution.py:354
  41.4 1.8 %collective-permute-done.17.refs_4_.right_ref = bf16[32,512]{1,0:T(8,128)(2,1)S(1)} collective-permute-done((bf16[32,512]{1,0:T(8,128)(2,1)S(1)}, bf16[32,512]{1,0:T(8,128)(2,1)S(1)}, u32[]{:S(2)}, u32[]{:S(2)}) %collective-permute-start.17) | collective-permute-done | bytes 32800 | tf_op jit(solution)/shard_map/ppermute | solution.py:430
  43.2 0.5 shard_map.134
  43.8 0.1 collective-permute-start.19
  43.8 0.0 collective-permute-done.18.refs_1_
  43.9 1.2 %collective-permute-done.19.refs_3_ = bf16[136,128]{1,0:T(8,128)(2,1)S(1)} collective-permute-done((bf16[136,128]{1,0:T(8,128)(2,1)S(1)}, bf16[136,128]{1,0:T(8,128)(2,1)S(1)}, u32[]{:S(2)}, u32[]{:S(2)}) %collective-permute-start.19) | collective-permute-done | bytes 34848 | tf_op jit(solution)/shard_map/ppermute | solution.py:362
  45.0 0.1 shard_map.136
  45.1 0.5 collective-permute-start.20
  45.6 2.5 %collective-permute-start.21 = (bf16[264,128]{1,0:T(8,128)(2,1)S(1)}, bf16[264,128]{1,0:T(8,128)(2,1)S(1)}, u32[]{:S(2)}, u32[]{:S(2)}) collective-permute-start(bf16[264,128]{1,0:T(8,128)(2,1)S(1)} %get-tuple-element.84), channel_id=1, source_target_pairs={{0,16},{4,20},{8,24},{12,28},{16,0},{20,4},{24,8},{28,12},{1,17},{... | collective-permute-start | bytes 202760 | tf_op jit(solution)/shard_map/ppermute | solution.py:358
  48.2 1.3 %collective-permute-start.22 = (bf16[264,128]{1,0:T(8,128)(2,1)S(1)}, bf16[264,128]{1,0:T(8,128)(2,1)S(1)}, u32[]{:S(2)}, u32[]{:S(2)}) collective-permute-start(bf16[264,128]{1,0:T(8,128)(2,1)S(1)} %get-tuple-element.85), channel_id=1, source_target_pairs={{0,24},{4,28},{8,16},{12,20},{16,8},{20,12},{24,0},{28,4},{1,25},{... | collective-permute-start | bytes 202760 | tf_op jit(solution)/shard_map/ppermute | solution.py:358
  49.4 0.0 collective-permute-done.20.refs_1_
  49.5 2.0 %collective-permute-done.21.refs_2_ = bf16[264,128]{1,0:T(8,128)(2,1)S(1)} collective-permute-done((bf16[264,128]{1,0:T(8,128)(2,1)S(1)}, bf16[264,128]{1,0:T(8,128)(2,1)S(1)}, u32[]{:S(2)}, u32[]{:S(2)}) %collective-permute-start.21) | collective-permute-done | bytes 67616 | tf_op jit(solution)/shard_map/ppermute | solution.py:358
  51.5 1.9 %collective-permute-done.22.refs_3_ = bf16[264,128]{1,0:T(8,128)(2,1)S(1)} collective-permute-done((bf16[264,128]{1,0:T(8,128)(2,1)S(1)}, bf16[264,128]{1,0:T(8,128)(2,1)S(1)}, u32[]{:S(2)}, u32[]{:S(2)}) %collective-permute-start.22) | collective-permute-done | bytes 67616 | tf_op jit(solution)/shard_map/ppermute | solution.py:358
  53.4 0.1 shard_map.137
  53.4 0.1 collective-permute-start.23
  53.5 0.7 %collective-permute-start.24 = (bf16[168,128]{1,0:T(8,128)(2,1)S(1)}, bf16[168,128]{1,0:T(8,128)(2,1)S(1)}, u32[]{:S(2)}, u32[]{:S(2)}) collective-permute-start(bf16[168,128]{1,0:T(8,128)(2,1)S(1)} %get-tuple-element.88), channel_id=1, source_target_pairs={{0,2},{1,3},{2,0},{3,1},{4,6},{5,7},{6,4},{7,5},{8,10},{9,11},{10,... | collective-permute-start | bytes 129032 | tf_op jit(solution)/shard_map/ppermute | solution.py:354
  54.2 3.7 %collective-permute-start.25 = (bf16[168,128]{1,0:T(8,128)(2,1)S(1)}, bf16[168,128]{1,0:T(8,128)(2,1)S(1)}, u32[]{:S(2)}, u32[]{:S(2)}) collective-permute-start(bf16[168,128]{1,0:T(8,128)(2,1)S(1)} %get-tuple-element.89), channel_id=1, source_target_pairs={{0,3},{1,2},{2,1},{3,0},{4,7},{5,6},{6,5},{7,4},{8,11},{9,10},{10,... | collective-permute-start | bytes 129032 | tf_op jit(solution)/shard_map/ppermute | solution.py:354
  57.9 1.7 %shard_map.135 = bf16[32,16,256]{2,1,0:T(8,128)(2,1)} custom-call(bf16[32,16,256]{2,1,0:T(8,128)(2,1)S(1)} %get-tuple-element.61.x_ref, f32[1,256]{1,0:T(1,128)S(1)} %get-tuple-element.62.gain_ref.refs_4_, bf16[32,256]{1,0:T(8,128)(2,1)S(1)} %get-tuple-element.63.lw_ref.refs_5_, bf16[32,256]{1,0:T(8,128)(2,1)S(1)} %get-tuple-element.64.rw_ref.refs_6_, ...), custom_call_target="tpu_custom_call" | custom-call | flops 1 | bytes 361472 | tf_op jit(solution)/shard_map/pallas_call | solution.py:36
  59.5 0.0 collective-permute-done.23.refs_1_
  59.5 0.0 collective-permute-done.24.refs_2_
  59.5 0.8 %collective-permute-done.25.refs_3_ = bf16[168,128]{1,0:T(8,128)(2,1)S(1)} collective-permute-done((bf16[168,128]{1,0:T(8,128)(2,1)S(1)}, bf16[168,128]{1,0:T(8,128)(2,1)S(1)}, u32[]{:S(2)}, u32[]{:S(2)}) %collective-permute-start.25) | collective-permute-done | bytes 43040 | tf_op jit(solution)/shard_map/ppermute | solution.py:354
  60.3 0.7 %shard_map.138 = (f32[32,256]{1,0:T(8,128)}, f32[32,256]{1,0:T(8,128)}, f32[32,128]{1,0:T(8,128)}, f32[1,256]{1,0:T(1,128)}, f32[1,128]{1,0:T(1,128)}) custom-call(bf16[168,128]{1,0:T(8,128)(2,1)S(1)} %get-tuple-element.86.refs_0_, bf16[168,128]{1,0:T(8,128)(2,1)S(1)} %collective-permute-done.23.refs_1_, ...), custom_call_target="tpu_custom_call" | custom-call | flops 1 | bytes 205824 | tf_op jit(solution)/shard_map/pallas_call | solution.py:36
  (2 shorter events, 0.0 us)
Async XLA Ops:
  2.5 6.8 %collective-permute-start = (bf16[32,512]{1,0:T(8,128)(2,1)S(1)}, bf16[32,512]{1,0:T(8,128)(2,1)S(1)}, u32[]{:S(2)}, u32[]{:S(2)}) collective-permute-start(bf16[32,512]{1,0:T(8,128)(2,1)S(1)} %get-tuple-element.51.refs_0_), channel_id=1, source_target_pairs={{0,1},{1,0},{2,3},{3,2},{4,5},{5,4},{6,7},{7,6},{8,9},{9,8},{10,11... | collective-permute-start | bytes 98312 | tf_op jit(solution)/shard_map/ppermute | solution.py:354
  5.6 5.4 %collective-permute-start.1 = (bf16[32,512]{1,0:T(8,128)(2,1)S(1)}, bf16[32,512]{1,0:T(8,128)(2,1)S(1)}, u32[]{:S(2)}, u32[]{:S(2)}) collective-permute-start(bf16[32,512]{1,0:T(8,128)(2,1)S(1)} %get-tuple-element.51.refs_0_), channel_id=1, source_target_pairs={{0,2},{1,3},{2,0},{3,1},{4,6},{5,7},{6,4},{7,5},{8,10},{9,11},{10,... | collective-permute-start | bytes 98312 | tf_op jit(solution)/shard_map/ppermute | solution.py:354
  8.2 5.7 %collective-permute-start.2 = (bf16[32,512]{1,0:T(8,128)(2,1)S(1)}, bf16[32,512]{1,0:T(8,128)(2,1)S(1)}, u32[]{:S(2)}, u32[]{:S(2)}) collective-permute-start(bf16[32,512]{1,0:T(8,128)(2,1)S(1)} %get-tuple-element.51.refs_0_), channel_id=1, source_target_pairs={{0,3},{1,2},{2,1},{3,0},{4,7},{5,6},{6,5},{7,4},{8,11},{9,10},{10,... | collective-permute-start | bytes 98312 | tf_op jit(solution)/shard_map/ppermute | solution.py:354
  14.3 13.6 %collective-permute-start.14 = (bf16[128,512]{1,0:T(8,128)(2,1)S(1)}, bf16[128,512]{1,0:T(8,128)(2,1)S(1)}, u32[]{:S(2)}, u32[]{:S(2)}) collective-permute-start(bf16[128,512]{1,0:T(8,128)(2,1)S(1)} %get-tuple-element.70), channel_id=1, source_target_pairs={{0,4},{4,0},{8,12},{12,8},{16,20},{20,16},{24,28},{28,24},{1,5},{5... | collective-permute-start | bytes 393224 | tf_op jit(solution)/shard_map/ppermute | solution.py:362
  14.4 5.8 %collective-permute-start.3 = (bf16[32,512]{1,0:T(8,128)(2,1)S(1)}, bf16[32,512]{1,0:T(8,128)(2,1)S(1)}, u32[]{:S(2)}, u32[]{:S(2)}) collective-permute-start(bf16[32,512]{1,0:T(8,128)(2,1)S(1)} %get-tuple-element.56), channel_id=1, source_target_pairs={{0,24},{1,16},{2,8},{3,0},{4,28},{5,20},{6,12},{7,4},{8,25},{9,17}... | collective-permute-start | bytes 98312 | tf_op jit(solution)/shard_map/ppermute | solution.py:389
  20.2 4.9 %collective-permute-start.9 = (bf16[32,512]{1,0:T(8,128)(2,1)S(1)}, bf16[32,512]{1,0:T(8,128)(2,1)S(1)}, u32[]{:S(2)}, u32[]{:S(2)}) collective-permute-start(bf16[32,512]{1,0:T(8,128)(2,1)S(1)} %collective-permute-done.3.refs_0_), channel_id=1, source_target_pairs={{0,24},{4,28},{8,16},{12,20},{16,8},{20,12},{24,0},{28,4},{1,25},{... | collective-permute-start | bytes 98312 | tf_op jit(solution)/shard_map/ppermute | solution.py:358
  21.7 3.9 %collective-permute-start.5 = (bf16[32,512]{1,0:T(8,128)(2,1)S(1)}, bf16[32,512]{1,0:T(8,128)(2,1)S(1)}, u32[]{:S(2)}, u32[]{:S(2)}) collective-permute-start(bf16[32,512]{1,0:T(8,128)(2,1)S(1)} %collective-permute-done.3.refs_0_), channel_id=1, source_target_pairs={{0,8},{4,12},{8,0},{12,4},{16,24},{20,28},{24,16},{28,20},{1,9},{5... | collective-permute-start | bytes 98312 | tf_op jit(solution)/shard_map/ppermute | solution.py:358
  22.2 3.9 %collective-permute-start.7 = (bf16[32,512]{1,0:T(8,128)(2,1)S(1)}, bf16[32,512]{1,0:T(8,128)(2,1)S(1)}, u32[]{:S(2)}, u32[]{:S(2)}) collective-permute-start(bf16[32,512]{1,0:T(8,128)(2,1)S(1)} %collective-permute-done.3.refs_0_), channel_id=1, source_target_pairs={{0,16},{4,20},{8,24},{12,28},{16,0},{20,4},{24,8},{28,12},{1,17},{... | collective-permute-start | bytes 98312 | tf_op jit(solution)/shard_map/ppermute | solution.py:358
  23.7 2.5 %collective-permute-start.4 = (bf16[32,512]{1,0:T(8,128)(2,1)S(1)}, bf16[32,512]{1,0:T(8,128)(2,1)S(1)}, u32[]{:S(2)}, u32[]{:S(2)}) collective-permute-start(bf16[32,512]{1,0:T(8,128)(2,1)S(1)} %collective-permute-done.3.refs_0_), channel_id=1, source_target_pairs={{0,4},{4,0},{8,12},{12,8},{16,20},{20,16},{24,28},{28,24},{1,5},{5... | collective-permute-start | bytes 98312 | tf_op jit(solution)/shard_map/ppermute | solution.py:362
  25.1 1.2 %collective-permute-start.10 = (bf16[32,512]{1,0:T(8,128)(2,1)S(1)}, bf16[32,512]{1,0:T(8,128)(2,1)S(1)}, u32[]{:S(2)}, u32[]{:S(2)}) collective-permute-start(bf16[32,512]{1,0:T(8,128)(2,1)S(1)} %collective-permute-done.9.refs_6_), channel_id=1, source_target_pairs={{0,4},{4,0},{8,12},{12,8},{16,20},{20,16},{24,28},{28,24},{1,5},{5... | collective-permute-start | bytes 98312 | tf_op jit(solution)/shard_map/ppermute | solution.py:362
  25.6 1.2 %collective-permute-start.6 = (bf16[32,512]{1,0:T(8,128)(2,1)S(1)}, bf16[32,512]{1,0:T(8,128)(2,1)S(1)}, u32[]{:S(2)}, u32[]{:S(2)}) collective-permute-start(bf16[32,512]{1,0:T(8,128)(2,1)S(1)} %collective-permute-done.5.refs_2_), channel_id=1, source_target_pairs={{0,4},{4,0},{8,12},{12,8},{16,20},{20,16},{24,28},{28,24},{1,5},{5... | collective-permute-start | bytes 98312 | tf_op jit(solution)/shard_map/ppermute | solution.py:362
  26.1 1.2 %collective-permute-start.8 = (bf16[32,512]{1,0:T(8,128)(2,1)S(1)}, bf16[32,512]{1,0:T(8,128)(2,1)S(1)}, u32[]{:S(2)}, u32[]{:S(2)}) collective-permute-start(bf16[32,512]{1,0:T(8,128)(2,1)S(1)} %collective-permute-done.7.refs_4_), channel_id=1, source_target_pairs={{0,4},{4,0},{8,12},{12,8},{16,20},{20,16},{24,28},{28,24},{1,5},{5... | collective-permute-start | bytes 98312 | tf_op jit(solution)/shard_map/ppermute | solution.py:362
  28.0 4.3 %collective-permute-start.15 = (bf16[64,512]{1,0:T(8,128)(2,1)S(1)}, bf16[64,512]{1,0:T(8,128)(2,1)S(1)}, u32[]{:S(2)}, u32[]{:S(2)}) collective-permute-start(bf16[64,512]{1,0:T(8,128)(2,1)S(1)} %get-tuple-element.72), channel_id=1, source_target_pairs={{0,16},{4,20},{8,24},{12,28},{16,0},{20,4},{24,8},{28,12},{1,17},{... | collective-permute-start | bytes 196616 | tf_op jit(solution)/shard_map/ppermute | solution.py:424
  31.6 12.2 %collective-permute-start.18 = (bf16[4,128,128]{2,1,0:T(8,128)(2,1)S(1)}, bf16[4,128,128]{2,1,0:T(8,128)(2,1)S(1)}, u32[]{:S(2)}, u32[]{:S(2)}) collective-permute-start(bf16[4,128,128]{2,1,0:T(8,128)(2,1)S(1)} %get-tuple-element.80), channel_id=1, source_target_pairs={{0,4},{4,0},{8,12},{12,8},{16,20},{20,16},{24,28},{28,24},{1,5},{5... | collective-permute-start | bytes 393224 | tf_op jit(solution)/shard_map/ppermute | solution.py:362
  32.3 6.0 %collective-permute-start.16 = (bf16[32,512]{1,0:T(8,128)(2,1)S(1)}, bf16[32,512]{1,0:T(8,128)(2,1)S(1)}, u32[]{:S(2)}, u32[]{:S(2)}) collective-permute-start(bf16[32,512]{1,0:T(8,128)(2,1)S(1)} %get-tuple-element.74), channel_id=1, source_target_pairs={{0,8},{4,12},{8,0},{12,4},{16,24},{20,28},{24,16},{28,20},{1,9},{5... | collective-permute-start | bytes 98312 | tf_op jit(solution)/shard_map/ppermute | solution.py:424
  33.9 5.6 %collective-permute-start.11 = (bf16[32,512]{1,0:T(8,128)(2,1)S(1)}, bf16[32,512]{1,0:T(8,128)(2,1)S(1)}, u32[]{:S(2)}, u32[]{:S(2)}) collective-permute-start(bf16[32,512]{1,0:T(8,128)(2,1)S(1)} %get-tuple-element.66), channel_id=1, source_target_pairs={{0,1},{1,0},{2,3},{3,2},{4,5},{5,4},{6,7},{7,6},{8,9},{9,8},{10,11... | collective-permute-start | bytes 98312 | tf_op jit(solution)/shard_map/ppermute | solution.py:354
  33.9 5.6 %collective-permute-start.12 = (bf16[32,512]{1,0:T(8,128)(2,1)S(1)}, bf16[32,512]{1,0:T(8,128)(2,1)S(1)}, u32[]{:S(2)}, u32[]{:S(2)}) collective-permute-start(bf16[32,512]{1,0:T(8,128)(2,1)S(1)} %get-tuple-element.67), channel_id=1, source_target_pairs={{0,2},{1,3},{2,0},{3,1},{4,6},{5,7},{6,4},{7,5},{8,10},{9,11},{10,... | collective-permute-start | bytes 98312 | tf_op jit(solution)/shard_map/ppermute | solution.py:354
  35.7 5.7 %collective-permute-start.13 = (bf16[32,512]{1,0:T(8,128)(2,1)S(1)}, bf16[32,512]{1,0:T(8,128)(2,1)S(1)}, u32[]{:S(2)}, u32[]{:S(2)}) collective-permute-start(bf16[32,512]{1,0:T(8,128)(2,1)S(1)} %get-tuple-element.68), channel_id=1, source_target_pairs={{0,3},{1,2},{2,1},{3,0},{4,7},{5,6},{6,5},{7,4},{8,11},{9,10},{10,... | collective-permute-start | bytes 98312 | tf_op jit(solution)/shard_map/ppermute | solution.py:354
  38.4 4.9 %collective-permute-start.17 = (bf16[32,512]{1,0:T(8,128)(2,1)S(1)}, bf16[32,512]{1,0:T(8,128)(2,1)S(1)}, u32[]{:S(2)}, u32[]{:S(2)}) collective-permute-start(bf16[32,512]{1,0:T(8,128)(2,1)S(1)} %shard_map.133), channel_id=1, source_target_pairs={{24,0},{16,1},{8,2},{0,3},{28,4},{20,5},{12,6},{4,7},{25,8},{17,9}... | collective-permute-start | bytes 98312 | tf_op jit(solution)/shard_map/ppermute | solution.py:430
  43.8 1.3 %collective-permute-start.19 = (bf16[136,128]{1,0:T(8,128)(2,1)S(1)}, bf16[136,128]{1,0:T(8,128)(2,1)S(1)}, u32[]{:S(2)}, u32[]{:S(2)}) collective-permute-start(bf16[136,128]{1,0:T(8,128)(2,1)S(1)} %get-tuple-element.81.refs_2_), channel_id=1, source_target_pairs={{0,4},{4,0},{8,12},{12,8},{16,20},{20,16},{24,28},{28,24},{1,5},{5... | collective-permute-start | bytes 104456 | tf_op jit(solution)/shard_map/ppermute | solution.py:362
  45.1 4.4 %collective-permute-start.20 = (bf16[264,128]{1,0:T(8,128)(2,1)S(1)}, bf16[264,128]{1,0:T(8,128)(2,1)S(1)}, u32[]{:S(2)}, u32[]{:S(2)}) collective-permute-start(bf16[264,128]{1,0:T(8,128)(2,1)S(1)} %get-tuple-element.83), channel_id=1, source_target_pairs={{0,8},{4,12},{8,0},{12,4},{16,24},{20,28},{24,16},{28,20},{1,9},{5... | collective-permute-start | bytes 202760 | tf_op jit(solution)/shard_map/ppermute | solution.py:358
  45.6 5.8 %collective-permute-start.21 = (bf16[264,128]{1,0:T(8,128)(2,1)S(1)}, bf16[264,128]{1,0:T(8,128)(2,1)S(1)}, u32[]{:S(2)}, u32[]{:S(2)}) collective-permute-start(bf16[264,128]{1,0:T(8,128)(2,1)S(1)} %get-tuple-element.84), channel_id=1, source_target_pairs={{0,16},{4,20},{8,24},{12,28},{16,0},{20,4},{24,8},{28,12},{1,17},{... | collective-permute-start | bytes 202760 | tf_op jit(solution)/shard_map/ppermute | solution.py:358
  48.2 5.2 %collective-permute-start.22 = (bf16[264,128]{1,0:T(8,128)(2,1)S(1)}, bf16[264,128]{1,0:T(8,128)(2,1)S(1)}, u32[]{:S(2)}, u32[]{:S(2)}) collective-permute-start(bf16[264,128]{1,0:T(8,128)(2,1)S(1)} %get-tuple-element.85), channel_id=1, source_target_pairs={{0,24},{4,28},{8,16},{12,20},{16,8},{20,12},{24,0},{28,4},{1,25},{... | collective-permute-start | bytes 202760 | tf_op jit(solution)/shard_map/ppermute | solution.py:358
  53.4 6.1 %collective-permute-start.23 = (bf16[168,128]{1,0:T(8,128)(2,1)S(1)}, bf16[168,128]{1,0:T(8,128)(2,1)S(1)}, u32[]{:S(2)}, u32[]{:S(2)}) collective-permute-start(bf16[168,128]{1,0:T(8,128)(2,1)S(1)} %get-tuple-element.87), channel_id=1, source_target_pairs={{0,1},{1,0},{2,3},{3,2},{4,5},{5,4},{6,7},{7,6},{8,9},{9,8},{10,11... | collective-permute-start | bytes 129032 | tf_op jit(solution)/shard_map/ppermute | solution.py:354
  53.5 6.0 %collective-permute-start.24 = (bf16[168,128]{1,0:T(8,128)(2,1)S(1)}, bf16[168,128]{1,0:T(8,128)(2,1)S(1)}, u32[]{:S(2)}, u32[]{:S(2)}) collective-permute-start(bf16[168,128]{1,0:T(8,128)(2,1)S(1)} %get-tuple-element.88), channel_id=1, source_target_pairs={{0,2},{1,3},{2,0},{3,1},{4,6},{5,7},{6,4},{7,5},{8,10},{9,11},{10,... | collective-permute-start | bytes 129032 | tf_op jit(solution)/shard_map/ppermute | solution.py:354
  54.2 6.1 %collective-permute-start.25 = (bf16[168,128]{1,0:T(8,128)(2,1)S(1)}, bf16[168,128]{1,0:T(8,128)(2,1)S(1)}, u32[]{:S(2)}, u32[]{:S(2)}) collective-permute-start(bf16[168,128]{1,0:T(8,128)(2,1)S(1)} %get-tuple-element.89), channel_id=1, source_target_pairs={{0,3},{1,2},{2,1},{3,0},{4,7},{5,6},{6,5},{7,4},{8,11},{9,10},{10,... | collective-permute-start | bytes 129032 | tf_op jit(solution)/shard_map/ppermute | solution.py:354
